TPU v7x, 128 devices: a whole 4x4x4 slice. The times are simulated.
128 devices in a mesh: wide: 64 (over y, x, z), narrow: 2 (over core).
Axes of the slice: x: 4, y: 4, z: 4, core: 2. Of those that a mesh axis runs over, the one named last changes fastest.
Arguments:
- pool_tokens: bfloat16 [49152, 2048], P(('wide', 'narrow')), may hold values from -6 to 6
- cotangent: bfloat16 [98304, 2048], P(('wide', 'narrow')), may hold values from -6 to 6
- slot_weights: bfloat16 [128, 3, 2048, 512], P(('wide', 'narrow')), may hold values from -6 to 6
- row_index: int32 [128, 768], P(('wide', 'narrow')), may hold values from 0 to 383
- route_weight: float32 [128, 768], P(('wide', 'narrow')), may hold values from 0.05 to 1
- slot_expert: int32 [128, 1], replicated, may hold values from 0 to 7
- next_expert: int32 [128, 1], replicated, may hold values from 0 to 7
- master: float32 [8, 3, 2048, 512], P(None, None, ('wide', 'narrow')), may hold values from -6 to 6
- moment_m: float32 [8, 3, 2048, 512], P(None, None, ('wide', 'narrow')), may hold values from -4 to 4
- moment_v: float32 [8, 3, 2048, 512], P(None, None, ('wide', 'narrow')), may hold values from 0.05 to 1
Outputs:
- token_grads: bfloat16 [49152, 2048], P(('wide', 'narrow'))
- master_next: float32 [8, 3, 2048, 512], P(None, None, ('wide', 'narrow'))
- moment_m_next: float32 [8, 3, 2048, 512], P(None, None, ('wide', 'narrow'))
- moment_v_next: float32 [8, 3, 2048, 512], P(None, None, ('wide', 'narrow'))
- next_weights: bfloat16 [128, 3, 2048, 512], P(('wide', 'narrow'))
Inputs may be any that keep to these rules, and one draw needn't show every extreme that they name: `slot_expert`: every one of the 8 experts is held by at least one slot; counts are uneven. `next_expert`: every one of the 8 experts is held by at least one slot; counts are uneven. `row_index`: indices into the pool of the slot's own device; a token may appear more than once.
All inputs are finite; a program needn't handle non-finite values.
Results may differ from a plain program's by a relative error of at most 0.0065.
Values may be sent and summed in bfloat16 or wider, within the bound.
No kernel may reach another device: no remote copies, remote signals or barrier semaphores. Data moves between devices by JAX's collectives and lax.ppermute only.
A program may use at most 128 MiB of HBM per device.

v0:
```python
import functools

import jax
import jax.numpy as jnp
from jax import lax
from jax.experimental import pallas as pl
from jax.experimental.pallas import tpu as pltpu
from jax.sharding import PartitionSpec as P

EXPERTS = 8
RING = 4
CORES = 2
STRIDES = (16, 4, 1)
BLOCK = 16
HIDDEN = 512
LANES = 128
VMEM_BYTES = 9 * 2**20
ORDERS = ((0, 1, 2), (1, 2, 0), (2, 0, 1))
BF16 = jnp.bfloat16
F32 = jnp.float32


VMEM = pl.BlockSpec(memory_space=pltpu.VMEM)
SMEM = pl.BlockSpec(memory_space=pltpu.SMEM)
ANY = pl.BlockSpec(memory_space=pl.ANY)
HBM = pl.BlockSpec(memory_space=pltpu.HBM)


def moved(chip, axis, steps):
    stride = STRIDES[axis]
    here = (chip // stride) % RING
    return chip + ((here + steps) % RING - here) * stride


def shift(array, axis, steps, swap=0):
    chips = RING**3
    if swap:
        pairs = [
            (CORES * chip + core, CORES * moved(chip, axis, steps) + (core ^ 1))
            for chip in range(chips)
            for core in range(CORES)
        ]
        return lax.ppermute(array, ("wide", "narrow"), pairs)
    return lax.ppermute(array, "wide", [(chip, moved(chip, axis, steps)) for chip in range(chips)])


def at_axis(ranks, axis, index, *more):
    where = [slice(None)] * ranks
    where[axis] = index
    return tuple(where) + more


def rest(order):
    return sorted(order[1:])


def slot_of(pos, order, back_a, back_b, swap):
    spot = [pos[0], pos[1], pos[2]]
    spot[order[0]] = (spot[order[0]] - back_a) & (RING - 1)
    spot[order[1]] = (spot[order[1]] - back_b) & (RING - 1)
    chip = sum(s * stride for s, stride in zip(spot, STRIDES))
    return chip * CORES + (pos[3] ^ swap)


def cut_first(order, pos, own, other, *outs):
    a = order[0]

    def step(i, carry):
        for steps in range(RING):
            target = (pos[a] + steps) & (RING - 1)
            for k, half in enumerate((own, other)):
                where = (target, i) if a == 0 else (i, *at_axis(2, a - 1, target))
                outs[steps][k, i] = half[where]
        return carry

    lax.fori_loop(0, RING, step, 0)


def cut_second(order, pos, *refs):
    ins, outs = refs[:RING], refs[RING:]
    b = order[1]
    dim = rest(order).index(b)
    for steps in range(RING):
        target = (pos[b] + steps) & (RING - 1)
        for back_a, piece in enumerate(ins):
            for k in range(CORES):
                outs[steps][CORES * back_a + k] = piece[(k,) + at_axis(2, dim, target)]


def sum_slots(order, pos, expert_of, *refs):
    ins, outs, total = refs[:4], refs[4:8], refs[8]
    d = order[2]
    total[...] = jnp.zeros_like(total)
    for back_b in range(RING):
        for k in range(RING * CORES):
            expert = expert_of[slot_of(pos, order, k // CORES, back_b, k % CORES)]

            def add(block, carry, expert=expert, piece=ins[back_b].at[k]):
                total[block, expert] += piece[block].astype(F32)
                return carry

            lax.fori_loop(0, RING, add, 0)
    for steps in range(RING):
        target = (pos[d] + steps) & (RING - 1)
        outs[steps][...] = total[target].astype(outs[steps].dtype)


def adam(own, one, two, three, master, moment_m, moment_v, fresh, first, second, weights):
    grad = own[...] + one[...].astype(F32) + two[...].astype(F32) + three[...].astype(F32)
    m_next = 0.9 * moment_m[...] + 0.1 * grad
    v_next = 0.95 * moment_v[...] + 0.05 * grad * grad
    old = master[...]
    new = old - 0.05 * (m_next / (jnp.sqrt(v_next) + 1e-08) + 0.1 * old)
    fresh[...] = new
    first[...] = m_next
    second[...] = v_next
    weights[...] = new.astype(BF16)


def pick(order, pos, expert_of, *refs):
    ins, outs, sent = refs[:RING], refs[RING:-1], refs[-1]
    b, d = order[1], order[2]
    b_first = rest(order)[0] == b
    for steps in range(RING):
        for swap in range(CORES):
            expert = expert_of[slot_of(pos, order, -steps, 0, swap)]
            for back_b in range(RING):
                for back_d in range(RING):
                    at_b = (pos[b] - back_b) & (RING - 1)
                    at_d = (pos[d] - back_d) & (RING - 1)
                    spot = (at_b, at_d) if b_first else (at_d, at_b)
                    tile = ins[back_b][back_d, expert]
                    if swap:
                        sent[(steps,) + spot] = tile
                    else:
                        outs[steps][spot] = tile


def join(*refs):
    kept, other, outs = refs[:RING], refs[RING], refs[RING + 1 :]
    for steps in range(RING):
        outs[steps][0] = kept[steps][...]
        outs[steps][1] = other[steps]


def lay_out(order, pos, *refs):
    ins, out = refs[:RING], refs[-1]
    a = order[0]
    for back in range(RING):
        source = (pos[a] - back) & (RING - 1)
        for k in range(CORES):
            out[(0,) + at_axis(3, a, source, pos[3] ^ k)] = ins[back][k]


def shaped(shape, dtype=BF16):
    return jax.ShapeDtypeStruct(shape, dtype)


def call(body, outs, in_specs, args, limit=VMEM_BYTES, work=0, **more):
    specs = more.pop("out_specs", [VMEM] * len(outs))
    return pl.pallas_call(
        body,
        out_shape=outs,
        in_specs=in_specs,
        out_specs=specs,
        compiler_params=pltpu.CompilerParams(vmem_limit_bytes=limit),
        cost_estimate=pl.CostEstimate(flops=work, bytes_accessed=0, transcendentals=0),
        **more,
    )(*args)


def around(parts, axis):
    got = [parts[0]]
    for k in (2, 1, 3):
        got.append(shift(parts[k], axis, k))
    return got


def start_grads(own, other, order, pos):
    pair = (CORES, RING, RING, BLOCK, HIDDEN)
    cube = (RING, RING, RING, BLOCK, HIDDEN)
    other = lax.ppermute(other, "narrow", [(0, 1), (1, 0)])
    return call(
        functools.partial(cut_first, order),
        [shaped(pair)] * RING,
        [SMEM, VMEM, VMEM],
        (pos, own.reshape(cube), other.reshape(cube)),
    )


def send_grads(parts, order, pos, slot_expert):
    a, b, d = order
    row = (RING * CORES, RING, BLOCK, HIDDEN)
    tile = (EXPERTS, BLOCK, HIDDEN)
    parts = around(parts, a)
    parts = call(
        functools.partial(cut_second, order),
        [shaped(row)] * RING,
        [SMEM] + [VMEM] * RING,
        (pos, parts[0], parts[2], parts[1], parts[3]),
    )
    parts = around(parts, b)
    parts = call(
        functools.partial(sum_slots, order),
        [shaped(tile, F32)] + [shaped(tile)] * 3,
        [SMEM, SMEM] + [VMEM] * RING,
        (pos, slot_expert, parts[0], parts[2], parts[1], parts[3]),
        scratch_shapes=[pltpu.VMEM((RING, *tile), F32)],
    )
    return around(parts, d)


def update(grads, part, master, moment_m, moment_v):
    tile = (EXPERTS, BLOCK, HIDDEN)
    whole = pl.BlockSpec(tile, lambda i: (0, 0, 0))
    third = pl.BlockSpec((EXPERTS, None, BLOCK, HIDDEN), lambda i: (0, part, 0, 0))
    return call(
        adam,
        [shaped(tile, F32)] * 3 + [shaped(tile)],
        [whole] * 4 + [third] * 3,
        (*grads, master, moment_m, moment_v),
        out_specs=[whole] * 4,
        grid=(1,),
    )


def send_weights(weights, order, pos, next_expert):
    a, b, d = order
    side = (RING, RING, BLOCK, HIDDEN)
    line = around([weights] * RING, d)
    line = jnp.stack([line[0], line[2], line[1], line[3]])
    plane = around([line] * RING, b)
    *kept, sent = call(
        functools.partial(pick, order),
        [shaped(side)] * RING + [shaped((RING, *side))],
        [SMEM, SMEM] + [VMEM] * RING,
        (pos, next_expert, plane[0], plane[2], plane[1], plane[3]),
    )
    other = lax.ppermute(sent, "narrow", [(0, 1), (1, 0)])
    parts = call(
        join, [shaped((CORES, *side))] * RING, [VMEM] * (RING + 1), (*kept, other)
    )
    parts = around(parts, a)
    return parts[0], parts[2], parts[1], parts[3]


def assemble(pieces, order, part, pos, into):
    dims = (3, RING, RING, RING, CORES, BLOCK, HIDDEN)
    specs = [SMEM] + [VMEM] * RING
    args = (pos, *pieces)
    alias = {}
    if into is not None:
        specs, args, alias = specs + [ANY], args + (into,), {RING + 1: 0}
    return call(
        functools.partial(lay_out, order),
        [shaped(dims)],
        specs,
        args,
        out_specs=[pl.BlockSpec((1, *dims[1:]), lambda i: (part,) + (0,) * 6)],
        grid=(1,),
        input_output_aliases=alias,
    )[0]


def mul(left, right, dims):
    return lax.dot_general(left, right, ((dims[:1], dims[1:]), ((), ())), preferred_element_type=F32)


def down_columns(row):
    return jnp.transpose(jnp.broadcast_to(row, (LANES, row.shape[1])))


def forward(pos, index, route, pool, weights_in, cot_in, own, other, gate, upper, scaled, wd,
            wg, wu, cot, spot, factor, high, low, hidden, grad, sems):
    pairs = (
        (weights_in.at[0, 0], wg),
        (weights_in.at[0, 1], wu),
        (cot_in, cot),
        (weights_in.at[0, 2], wd),
    )
    copies = [pltpu.make_async_copy(a, b, sems.at[k]) for k, (a, b) in enumerate(pairs)]
    copies[0].start()
    width, hidden_units = wg.shape
    rows = index.shape[1]
    scale_in, scale_out = width ** (-0.5), hidden_units ** (-0.5)
    spot[...] = down_columns(index[...].astype(F32))
    factor[...] = down_columns(route[...])
    for k, w in enumerate((wg, wu)):
        copies[k].wait()
        copies[k + 1].start()
        values = mul(pool[...], w[...], (1, 0)) * scale_in
        top = values.astype(BF16)
        high[k] = top
        low[k] = (values - top.astype(F32)).astype(BF16)
    lanes = lax.broadcasted_iota(jnp.int32, (256, LANES), 1).astype(F32)

    def expand(step, carry):
        r = pl.ds(pl.multiple_of(step * 256, 256), 256)
        chosen = jnp.concatenate(
            [
                jnp.where(spot[r, :] == lanes + float(k), 1.0, 0.0).astype(BF16)
                for k in range(0, pool.shape[0], LANES)
            ],
            axis=1,
        )
        for k, out in enumerate((gate, upper)):
            out[r, :] = mul(chosen, high[k], (1, 0)) + mul(chosen, low[k], (1, 0))
        return carry

    lax.fori_loop(0, rows // 256, expand, 0)

    def activate(step, carry):
        r = pl.ds(pl.multiple_of(step * 64, 64), 64)
        g = gate[r, :]
        hidden[r, :] = (g * jax.nn.sigmoid(g) * upper[r, :]).astype(BF16)
        return carry

    lax.fori_loop(0, rows // 64, activate, 0)
    copies[2].wait()
    copies[3].start()

    def scale(step, carry):
        r = pl.ds(pl.multiple_of(step * 32, 32), 32)
        by = factor[r, :]
        for k in range(0, width, LANES):
            scaled[r, k : k + LANES] = (by * cot[r, k : k + LANES].astype(F32)).astype(BF16)
        return carry

    lax.fori_loop(0, rows // 32, scale, 0)
    blocks = hidden_units // (BLOCK * CORES)

    def outer(step, carry):
        r = pl.ds(pl.multiple_of(step * hidden_units, hidden_units), hidden_units)
        values = (mul(scaled[:, r], hidden[...], (0, 0)) * scale_out).astype(BF16)
        grad[pl.ds(step * blocks, blocks)] = values.reshape(blocks, CORES, BLOCK, hidden_units)
        return carry

    lax.fori_loop(0, width // hidden_units, outer, 0)
    halve(pos, grad, own, other)
    copies[3].wait()


def halve(pos, grad, own, other):
    count = grad.shape[0] // 16

    def step(k, carry):
        at = pl.ds(k * count, count)
        own[at] = grad[at, pos[3]]
        other[at] = grad[at, 1 - pos[3]]
        return carry

    lax.fori_loop(0, 16, step, 0)


def backward(index, gate, upper, scaled, wd, gate_sum, up_sum, d_gate, d_up):
    spots = lax.broadcasted_iota(jnp.int32, (gate_sum.shape[0], index.shape[1]), 0)
    chosen = jnp.where(index[...] == spots, 1.0, 0.0).astype(BF16)
    scale_out = wd.shape[1] ** (-0.5)

    def step(k, carry):
        r = pl.ds(pl.multiple_of(k * 256, 256), 256)
        back = mul(scaled[r, :], wd[...], (1, 0)) * scale_out
        g = gate[r, :]
        sigma = jax.nn.sigmoid(g)
        d_gate[r, :] = (back * upper[r, :] * sigma * (1.0 + g * (1.0 - sigma))).astype(BF16)
        d_up[r, :] = (back * (g * sigma)).astype(BF16)
        return carry

    lax.fori_loop(0, gate.shape[0] // 256, step, 0)
    gate_sum[...] = mul(chosen, d_gate[...], (1, 0)).astype(BF16)
    up_sum[...] = mul(chosen, d_up[...], (1, 0)).astype(BF16)


def pool_grads(pos, pool, gate_sum, up_sum, gate_own, gate_other, up_own, up_other, grad):
    width, hidden_units = pool.shape[1], gate_sum.shape[1]
    scale_in = width ** (-0.5)
    blocks = hidden_units // (BLOCK * CORES)
    for total, own, other in ((gate_sum, gate_own, gate_other), (up_sum, up_own, up_other)):

        def outer(step, carry, total=total):
            r = pl.ds(pl.multiple_of(step * hidden_units, hidden_units), hidden_units)
            values = (mul(pool[:, r], total[...], (0, 0)) * scale_in).astype(BF16)
            grad[pl.ds(step * blocks, blocks)] = values.reshape(blocks, CORES, BLOCK, hidden_units)
            return carry

        lax.fori_loop(0, width // hidden_units, outer, 0)
        halve(pos, grad, own, other)


def run_forward(pos, index, route, pool, weights, cot):
    rows, width = cot.shape
    tokens, hid = pool.shape[0], weights.shape[3]
    half = (width // (BLOCK * CORES), BLOCK, hid)
    return call(
        forward,
        [shaped(half)] * 2
        + [shaped((rows, hid), F32)] * 2
        + [shaped((rows, width)), shaped((width, hid))],
        [SMEM, VMEM, VMEM, VMEM, HBM, HBM],
        (pos, index, route, pool, weights, cot),
        scratch_shapes=[
            pltpu.VMEM((width, hid), BF16),
            pltpu.VMEM((width, hid), BF16),
            pltpu.VMEM(cot.shape, BF16),
            pltpu.VMEM((rows, LANES), F32),
            pltpu.VMEM((rows, LANES), F32),
            pltpu.VMEM((2, tokens, hid), BF16),
            pltpu.VMEM((2, tokens, hid), BF16),
            pltpu.VMEM((rows, hid), BF16),
            pltpu.VMEM((half[0], CORES, BLOCK, hid), BF16),
            pltpu.SemaphoreType.DMA((4,)),
        ],
        limit=40 * 2**20,
        work=5 * 10**9,
    )


def run_backward(index, gate, upper, scaled, wd, tokens):
    rows, hid = gate.shape
    return call(
        backward,
        [shaped((tokens, hid))] * 2,
        [VMEM] * 5,
        (index, gate, upper, scaled, wd),
        scratch_shapes=[pltpu.VMEM((rows, hid), BF16), pltpu.VMEM((rows, hid), BF16)],
        limit=24 * 2**20,
        work=3 * 10**9,
    )


def run_pool_grads(pos, pool, gate_sum, up_sum):
    width, hid = pool.shape[1], gate_sum.shape[1]
    half = (width // (BLOCK * CORES), BLOCK, hid)
    return call(
        pool_grads,
        [shaped(half)] * 4,
        [SMEM, VMEM, VMEM, VMEM],
        (pos, pool, gate_sum, up_sum),
        scratch_shapes=[pltpu.VMEM((half[0], CORES, BLOCK, hid), BF16)],
        limit=20 * 2**20,
        work=2 * 10**9,
    )


def local(
    pool_tokens,
    cotangent,
    slot_weights,
    row_index,
    route_weight,
    slot_expert,
    next_expert,
    master,
    moment_m,
    moment_v,
):
    chip = lax.axis_index("wide")
    pos = jnp.stack(
        [(chip // s) % RING for s in STRIDES] + [lax.axis_index("narrow")]
    ).astype(jnp.int32)
    slot_expert, next_expert = slot_expert[:, 0], next_expert[:, 0]
    weights_in = slot_weights
    scale_in = pool_tokens.shape[1] ** (-0.5)
    tokens = pool_tokens.shape[0]
    own, other, gate, upper, scaled, wd = run_forward(
        pos, row_index, route_weight, pool_tokens, weights_in, cotangent
    )
    cut = {2: start_grads(own, other, ORDERS[2], pos)}
    gate_sum, up_sum = run_backward(row_index, gate, upper, scaled, wd, tokens)
    cut[2], (gate_sum, up_sum) = lax.optimization_barrier((cut[2], (gate_sum, up_sum)))
    own_0, other_0, own_1, other_1 = run_pool_grads(pos, pool_tokens, gate_sum, up_sum)
    cut[0] = start_grads(own_0, other_0, ORDERS[0], pos)
    cut[1] = start_grads(own_1, other_1, ORDERS[1], pos)
    token_grads = (
        mul(gate_sum, weights_in[0, 0], (1, 1)) + mul(up_sum, weights_in[0, 1], (1, 1))
    ) * scale_in
    token_grads = token_grads.astype(BF16)

    results = {}
    out = None
    for part in (2, 0, 1):
        grads = send_grads(cut[part], ORDERS[part], pos, slot_expert)
        results[part] = update(grads, part, master, moment_m, moment_v)
        pieces = send_weights(results[part][3], ORDERS[part], pos, next_expert)
        out = assemble(pieces, ORDERS[part], part, pos, out)
    fresh, first, second = (
        jnp.stack([results[part][k] for part in range(3)], axis=1) for k in range(3)
    )
    next_weights = out.reshape(slot_weights.shape)
    return (token_grads, fresh, first, second, next_weights)


def solution(mesh):
    rows = P(("wide", "narrow"), None)
    cube = P(None, None, ("wide", "narrow"), None)
    slots = P(("wide", "narrow"), None, None, None)
    in_specs = (rows, rows, slots, rows, rows, P(), P(), cube, cube, cube)
    out_specs = (rows, cube, cube, cube, slots)
    return jax.shard_map(local, mesh=mesh, in_specs=in_specs, out_specs=out_specs, check_vma=False)
```

profile of v0, /device:TPU:1, one launch (start us, length us, event | category | flops | bytes accessed | tf_op | source)
XLA Modules:
  0.0 306.8 jit_solution(8826628147307472185)
XLA Ops:
  3.5 10.9 %shard_map.137 = (bf16[64,16,512]{2,1,0:T(8,128)(2,1)S(1)}, bf16[64,16,512]{2,1,0:T(8,128)(2,1)S(1)}, f32[768,512]{1,0:T(8,128)S(1)}, f32[768,512]{1,0:T(8,128)S...) custom-call(s32[4]{0:T(128)S(1)} %pad_add_fusion.pos, s32[1,768]{1,0:T(1,128)S(1)} %copy-done.7, ...), custom_call_target="tpu_custom_call" | custom-call | flops 5000000000 | tf_op jit(solution)/shard_map/pallas_call | solution.py:161
  14.5 1.4 collective-permute-start
  15.9 3.4 %shard_map.139 = (bf16[384,512]{1,0:T(8,128)(2,1)S(1)}, bf16[384,512]{1,0:T(8,128)(2,1)S(1)}) custom-call(s32[1,768]{1,0:T(1,128)S(1)} %copy-done.7, f32[768,512]{1,0:T(8,128)S(1)} %get-tuple-element.104.gate, f32[768,512]{1,0:T(8,128)S(1)} %get-tuple-element.105.upper, bf16[768,2048]{1,0:T(8,128)(2,1)S(1)} %get-tuple-element.106.scaled, ...), custom_call_target="tpu_custom_call" | custom-call | flops 3000000000 | tf_op jit(solution)/shard_map/pallas_call | solution.py:161
  20.1 1.8 collective-permute-start.21
  21.9 3.3 %collective-permute-start.22 = (bf16[2,4,4,16,512]{4,3,2,1,0:T(8,128)(2,1)S(1)}, bf16[2,4,4,16,512]{4,3,2,1,0:T(8,128)(2,1)S(1)}, u32[]{:S(2)}, u32[]{:S(2)}) collective-permute-start(bf16[2,4,4,16,512]{4,3,2,1,0:T(8,128)(2,1)S(1)} %get-tuple-element.144), channel_id=1, source_target_pairs={{0,4},{2,6},{4,0},{6,2},{8,12},{10,14},{12,8},{14,10},{16,20},{18,... | collective-permute-start | bytes 1572872 | tf_op jit(solution)/shard_map/ppermute | solution.py:44
  25.2 4.8 %shard_map.140 = (bf16[64,16,512]{2,1,0:T(8,128)(2,1)S(1)}, bf16[64,16,512]{2,1,0:T(8,128)(2,1)S(1)}, bf16[64,16,512]{2,1,0:T(8,128)(2,1)S(1)}, bf16[64,16,512]{2,1,0:T(8,128)(2,1)S(1)}) custom-call(s32[4]{0:T(128)S(1)} %pad_add_fusion.pos, bf16[384,2048]{1,0:T(8,128)(2,1)S(1)} %copy-done.5, bf16[384,512]{1,0:T(8,128)(2,1)S(1)} %get-tuple-element.110.gate_sum, ...), custom_call_target="tpu_custom_call" | custom-call | flops 2000000000 | tf_op jit(solution)/shard_map/pallas_call | solution.py:161
  31.7 4.6 %collective-permute-done.21.refs_1_ = bf16[2,4,4,16,512]{4,3,2,1,0:T(8,128)(2,1)S(1)} collective-permute-done((bf16[2,4,4,16,512]{4,3,2,1,0:T(8,128)(2,1)S(1)}, bf16[2,4,4,16,512]{4,3,2,1,0:T(8,128)(2,1)S(1)}, u32[]{:S(2)}, u32[]{:S(2)}) %collective-permute-start.21) | collective-permute-done | bytes 524320 | tf_op jit(solution)/shard_map/ppermute | solution.py:44
  36.3 12.1 %collective-permute-done.22.refs_2_ = bf16[2,4,4,16,512]{4,3,2,1,0:T(8,128)(2,1)S(1)} collective-permute-done((bf16[2,4,4,16,512]{4,3,2,1,0:T(8,128)(2,1)S(1)}, bf16[2,4,4,16,512]{4,3,2,1,0:T(8,128)(2,1)S(1)}, u32[]{:S(2)}, u32[]{:S(2)}) %collective-permute-start.22) | collective-permute-done | bytes 524320 | tf_op jit(solution)/shard_map/ppermute | solution.py:44
  50.5 2.6 collective-permute-start.25
  55.4 7.8 %collective-permute-done.24.refs_1_ = bf16[8,4,16,512]{3,2,1,0:T(8,128)(2,1)S(1)} collective-permute-done((bf16[8,4,16,512]{3,2,1,0:T(8,128)(2,1)S(1)}, bf16[8,4,16,512]{3,2,1,0:T(8,128)(2,1)S(1)}, u32[]{:S(2)}, u32[]{:S(2)}) %collective-permute-start.24) | collective-permute-done | bytes 524320 | tf_op jit(solution)/shard_map/ppermute | solution.py:44
  63.2 12.4 %collective-permute-done.25.refs_2_ = bf16[8,4,16,512]{3,2,1,0:T(8,128)(2,1)S(1)} collective-permute-done((bf16[8,4,16,512]{3,2,1,0:T(8,128)(2,1)S(1)}, bf16[8,4,16,512]{3,2,1,0:T(8,128)(2,1)S(1)}, u32[]{:S(2)}, u32[]{:S(2)}) %collective-permute-start.25) | collective-permute-done | bytes 524320 | tf_op jit(solution)/shard_map/ppermute | solution.py:44
  75.6 1.8 shard_map.150
  77.4 2.8 collective-permute-start.27
  80.2 2.0 collective-permute-start.3
  82.2 1.8 collective-permute-start.4
  85.2 3.9 %collective-permute-done.28.two = bf16[8,16,512]{2,1,0:T(8,128)(2,1)S(1)} collective-permute-done((bf16[8,16,512]{2,1,0:T(8,128)(2,1)S(1)}, bf16[8,16,512]{2,1,0:T(8,128)(2,1)S(1)}, u32[]{:S(2)}, u32[]{:S(2)}) %collective-permute-start.28) | collective-permute-done | bytes 131104 | tf_op jit(solution)/shard_map/ppermute | solution.py:44
  89.1 4.1 %collective-permute-done.29.three = bf16[8,16,512]{2,1,0:T(8,128)(2,1)S(1)} collective-permute-done((bf16[8,16,512]{2,1,0:T(8,128)(2,1)S(1)}, bf16[8,16,512]{2,1,0:T(8,128)(2,1)S(1)}, u32[]{:S(2)}, u32[]{:S(2)}) %collective-permute-start.29) | collective-permute-done | bytes 131104 | tf_op jit(solution)/shard_map/ppermute | solution.py:44
  93.6 8.8 %collective-permute-done.50 = bf16[8,16,512]{2,1,0:T(8,128)(2,1)S(1)} collective-permute-done((bf16[8,16,512]{2,1,0:T(8,128)(2,1)S(1)}, bf16[8,16,512]{2,1,0:T(8,128)(2,1)S(1)}, u32[]{:S(2)}, u32[]{:S(2)}) %collective-permute-start.50) | collective-permute-done | bytes 131104 | tf_op jit(solution)/shard_map/ppermute | solution.py:44
  103.6 1.8 collective-permute-start.52
  108.8 2.0 collective-permute-start.6
  110.8 4.3 %collective-permute-start.7 = (bf16[8,4,16,512]{3,2,1,0:T(8,128)(2,1)S(1)}, bf16[8,4,16,512]{3,2,1,0:T(8,128)(2,1)S(1)}, u32[]{:S(2)}, u32[]{:S(2)}) collective-permute-start(bf16[8,4,16,512]{3,2,1,0:T(8,128)(2,1)S(1)} %get-tuple-element.121), channel_id=1, source_target_pairs={{0,24},{2,26},{4,28},{6,30},{8,0},{10,2},{12,4},{14,6},{16,8},{18,... | collective-permute-start | bytes 1572872 | tf_op jit(solution)/shard_map/ppermute | solution.py:44
  115.3 5.3 %collective-permute-done.13.refs_2_ = bf16[2,4,4,16,512]{4,3,2,1,0:T(8,128)(2,1)S(1)} collective-permute-done((bf16[2,4,4,16,512]{4,3,2,1,0:T(8,128)(2,1)S(1)}, bf16[2,4,4,16,512]{4,3,2,1,0:T(8,128)(2,1)S(1)}, u32[]{:S(2)}, u32[]{:S(2)}) %collective-permute-start.13) | collective-permute-done | bytes 524320 | tf_op jit(solution)/shard_map/ppermute | solution.py:44
  120.6 11.4 %collective-permute-done.14.refs_3_ = bf16[2,4,4,16,512]{4,3,2,1,0:T(8,128)(2,1)S(1)} collective-permute-done((bf16[2,4,4,16,512]{4,3,2,1,0:T(8,128)(2,1)S(1)}, bf16[2,4,4,16,512]{4,3,2,1,0:T(8,128)(2,1)S(1)}, u32[]{:S(2)}, u32[]{:S(2)}) %collective-permute-start.14) | collective-permute-done | bytes 524320 | tf_op jit(solution)/shard_map/ppermute | solution.py:44
  132.7 1.8 collective-permute-start.15
  135.0 2.0 collective-permute-start.16
  136.9 6.1 %collective-permute-done.6.refs_2_ = bf16[8,4,16,512]{3,2,1,0:T(8,128)(2,1)S(1)} collective-permute-done((bf16[8,4,16,512]{3,2,1,0:T(8,128)(2,1)S(1)}, bf16[8,4,16,512]{3,2,1,0:T(8,128)(2,1)S(1)}, u32[]{:S(2)}, u32[]{:S(2)}) %collective-permute-start.6) | collective-permute-done | bytes 524320 | tf_op jit(solution)/shard_map/ppermute | solution.py:44
  143.0 11.1 %collective-permute-done.7.refs_3_ = bf16[8,4,16,512]{3,2,1,0:T(8,128)(2,1)S(1)} collective-permute-done((bf16[8,4,16,512]{3,2,1,0:T(8,128)(2,1)S(1)}, bf16[8,4,16,512]{3,2,1,0:T(8,128)(2,1)S(1)}, u32[]{:S(2)}, u32[]{:S(2)}) %collective-permute-start.7) | collective-permute-done | bytes 524320 | tf_op jit(solution)/shard_map/ppermute | solution.py:44
  154.1 1.8 shard_map.143
  156.0 2.4 collective-permute-start.10
  158.4 2.0 collective-permute-done.10.three
  160.4 1.8 collective-permute-start.8
  162.2 3.6 %collective-permute-done.8.one = bf16[8,16,512]{2,1,0:T(8,128)(2,1)S(1)} collective-permute-done((bf16[8,16,512]{2,1,0:T(8,128)(2,1)S(1)}, bf16[8,16,512]{2,1,0:T(8,128)(2,1)S(1)}, u32[]{:S(2)}, u32[]{:S(2)}) %collective-permute-start.8) | collective-permute-done | bytes 131104 | tf_op jit(solution)/shard_map/ppermute | solution.py:44
  165.7 8.2 %collective-permute-start.9 = (bf16[8,16,512]{2,1,0:T(8,128)(2,1)S(1)}, bf16[8,16,512]{2,1,0:T(8,128)(2,1)S(1)}, u32[]{:S(2)}, u32[]{:S(2)}) collective-permute-start(bf16[8,16,512]{2,1,0:T(8,128)(2,1)S(1)} %get-tuple-element.124), channel_id=1, source_target_pairs={{0,2},{2,4},{4,6},{6,0},{8,10},{10,12},{12,14},{14,8},{16,18},{18,... | collective-permute-start | bytes 393224 | tf_op jit(solution)/shard_map/ppermute | solution.py:44
  173.9 4.7 %collective-permute-done.9.two = bf16[8,16,512]{2,1,0:T(8,128)(2,1)S(1)} collective-permute-done((bf16[8,16,512]{2,1,0:T(8,128)(2,1)S(1)}, bf16[8,16,512]{2,1,0:T(8,128)(2,1)S(1)}, u32[]{:S(2)}, u32[]{:S(2)}) %collective-permute-start.9) | collective-permute-done | bytes 131104 | tf_op jit(solution)/shard_map/ppermute | solution.py:44
  178.6 3.3 %collective-permute-start.54 = (bf16[4,8,16,512]{3,2,1,0:T(8,128)(2,1)S(1)}, bf16[4,8,16,512]{3,2,1,0:T(8,128)(2,1)S(1)}, u32[]{:S(2)}, u32[]{:S(2)}) collective-permute-start(bf16[4,8,16,512]{3,2,1,0:T(8,128)(2,1)S(1)} %pad_maximum_fusion.5.refs_0_), channel_id=1, source_target_pairs={{0,64},{2,66},{4,68},{6,70},{8,72},{10,74},{12,76},{14,78},{16,80}... | collective-permute-start | bytes 1572872 | tf_op jit(solution)/shard_map/ppermute | solution.py:44
  182.3 2.6 collective-permute-start.41
  185.2 1.8 shard_map.147
  189.7 2.0 collective-permute-start.20
  191.8 2.9 collective-permute-done.18.one
  197.5 2.0 collective-permute-start.44
  199.4 6.8 %collective-permute-done.20.three = bf16[8,16,512]{2,1,0:T(8,128)(2,1)S(1)} collective-permute-done((bf16[8,16,512]{2,1,0:T(8,128)(2,1)S(1)}, bf16[8,16,512]{2,1,0:T(8,128)(2,1)S(1)}, u32[]{:S(2)}, u32[]{:S(2)}) %collective-permute-start.20) | collective-permute-done | bytes 131104 | tf_op jit(solution)/shard_map/ppermute | solution.py:44
  206.2 7.0 %collective-permute-start.45 = (bf16[4,8,16,512]{3,2,1,0:T(8,128)(2,1)S(1)}, bf16[4,8,16,512]{3,2,1,0:T(8,128)(2,1)S(1)}, u32[]{:S(2)}, u32[]{:S(2)}) collective-permute-start(bf16[4,8,16,512]{3,2,1,0:T(8,128)(2,1)S(1)} %pad_maximum_fusion.4.refs_0_), channel_id=1, source_target_pairs={{0,24},{2,26},{4,28},{6,30},{8,0},{10,2},{12,4},{14,6},{16,8},{18,... | collective-permute-start | bytes 1572872 | tf_op jit(solution)/shard_map/ppermute | solution.py:44
  213.5 2.2 collective-permute-start.30
  215.7 2.6 collective-permute-start.31
  218.3 1.5 collective-permute-done.30
  219.8 1.5 collective-permute-start.32
  224.0 2.6 collective-permute-start.34
  226.7 5.3 %collective-permute-start.56 = (bf16[4,4,4,16,512]{4,3,2,1,0:T(8,128)(2,1)S(1)}, bf16[4,4,4,16,512]{4,3,2,1,0:T(8,128)(2,1)S(1)}, u32[]{:S(2)}, u32[]{:S(2)}) collective-permute-start(bf16[4,4,4,16,512]{4,3,2,1,0:T(8,128)(2,1)S(1)} %get-tuple-element.186), channel_id=1, source_target_pairs={{0,1},{1,0},{2,3},{3,2},{4,5},{5,4},{6,7},{7,6},{8,9},{9,8},{10,11... | collective-permute-start | bytes 3145736 | tf_op jit(solution)/shard_map/ppermute | solution.py:239
  232.9 2.2 collective-permute-done.33.refs_1_
  235.1 11.2 %collective-permute-done.34.refs_2_ = bf16[4,8,16,512]{3,2,1,0:T(8,128)(2,1)S(1)} collective-permute-done((bf16[4,8,16,512]{3,2,1,0:T(8,128)(2,1)S(1)}, bf16[4,8,16,512]{3,2,1,0:T(8,128)(2,1)S(1)}, u32[]{:S(2)}, u32[]{:S(2)}) %collective-permute-start.34) | collective-permute-done | bytes 524320 | tf_op jit(solution)/shard_map/ppermute | solution.py:44
  246.3 3.0 collective-permute-done.35.refs_3_
  250.1 2.2 collective-permute-start.36
  252.5 3.2 %collective-permute-start.58 = (bf16[2,4,4,16,512]{4,3,2,1,0:T(8,128)(2,1)S(1)}, bf16[2,4,4,16,512]{4,3,2,1,0:T(8,128)(2,1)S(1)}, u32[]{:S(2)}, u32[]{:S(2)}) collective-permute-start(bf16[2,4,4,16,512]{4,3,2,1,0:T(8,128)(2,1)S(1)} %get-tuple-element.189), channel_id=1, source_target_pairs={{0,4},{2,6},{4,0},{6,2},{8,12},{10,14},{12,8},{14,10},{16,20},{18,... | collective-permute-start | bytes 1572872 | tf_op jit(solution)/shard_map/ppermute | solution.py:44
  257.9 3.0 collective-permute-start.48
  261.1 6.1 %collective-permute-done.57.refs_1_ = bf16[2,4,4,16,512]{4,3,2,1,0:T(8,128)(2,1)S(1)} collective-permute-done((bf16[2,4,4,16,512]{4,3,2,1,0:T(8,128)(2,1)S(1)}, bf16[2,4,4,16,512]{4,3,2,1,0:T(8,128)(2,1)S(1)}, u32[]{:S(2)}, u32[]{:S(2)}) %collective-permute-start.57) | collective-permute-done | bytes 524320 | tf_op jit(solution)/shard_map/ppermute | solution.py:44
  267.2 2.7 collective-permute-start.49
  269.9 9.1 %collective-permute-done.58.refs_2_ = bf16[2,4,4,16,512]{4,3,2,1,0:T(8,128)(2,1)S(1)} collective-permute-done((bf16[2,4,4,16,512]{4,3,2,1,0:T(8,128)(2,1)S(1)}, bf16[2,4,4,16,512]{4,3,2,1,0:T(8,128)(2,1)S(1)}, u32[]{:S(2)}, u32[]{:S(2)}) %collective-permute-start.58) | collective-permute-done | bytes 524320 | tf_op jit(solution)/shard_map/ppermute | solution.py:44
  279.0 2.1 collective-permute-start.38
  281.9 2.2 multiply_convert_fusion
  287.2 2.0 shard_map.158.refs_4_
  289.2 2.0 shard_map.159.refs_4_
  291.2 2.2 collective-permute-done.37.refs_1_
  293.4 10.1 %collective-permute-done.38.refs_2_ = bf16[2,4,4,16,512]{4,3,2,1,0:T(8,128)(2,1)S(1)} collective-permute-done((bf16[2,4,4,16,512]{4,3,2,1,0:T(8,128)(2,1)S(1)}, bf16[2,4,4,16,512]{4,3,2,1,0:T(8,128)(2,1)S(1)}, u32[]{:S(2)}, u32[]{:S(2)}) %collective-permute-start.38) | collective-permute-done | bytes 524320 | tf_op jit(solution)/shard_map/ppermute | solution.py:44
  304.8 2.0 shard_map.160
  (113 shorter events, 35.6 us)
Async XLA Ops:
  14.5 4.9 %collective-permute-start = (bf16[64,16,512]{2,1,0:T(8,128)(2,1)S(1)}, bf16[64,16,512]{2,1,0:T(8,128)(2,1)S(1)}, u32[]{:S(2)}, u32[]{:S(2)}) collective-permute-start(bf16[64,16,512]{2,1,0:T(8,128)(2,1)S(1)} %get-tuple-element.99), channel_id=1, source_target_pairs={{0,1},{1,0},{2,3},{3,2},{4,5},{5,4},{6,7},{7,6},{8,9},{9,8},{10,11... | collective-permute-start | bytes 3145736 | tf_op jit(solution)/shard_map/ppermute | solution.py:182
  20.1 16.2 %collective-permute-start.21 = (bf16[2,4,4,16,512]{4,3,2,1,0:T(8,128)(2,1)S(1)}, bf16[2,4,4,16,512]{4,3,2,1,0:T(8,128)(2,1)S(1)}, u32[]{:S(2)}, u32[]{:S(2)}) collective-permute-start(bf16[2,4,4,16,512]{4,3,2,1,0:T(8,128)(2,1)S(1)} %get-tuple-element.143), channel_id=1, source_target_pairs={{0,2},{2,4},{4,6},{6,0},{8,10},{10,12},{12,14},{14,8},{16,18},{18,... | collective-permute-start | bytes 1572872 | tf_op jit(solution)/shard_map/ppermute | solution.py:44
  21.9 26.5 %collective-permute-start.22 = (bf16[2,4,4,16,512]{4,3,2,1,0:T(8,128)(2,1)S(1)}, bf16[2,4,4,16,512]{4,3,2,1,0:T(8,128)(2,1)S(1)}, u32[]{:S(2)}, u32[]{:S(2)}) collective-permute-start(bf16[2,4,4,16,512]{4,3,2,1,0:T(8,128)(2,1)S(1)} %get-tuple-element.144), channel_id=1, source_target_pairs={{0,4},{2,6},{4,0},{6,2},{8,12},{10,14},{12,8},{14,10},{16,20},{18,... | collective-permute-start | bytes 1572872 | tf_op jit(solution)/shard_map/ppermute | solution.py:44
  30.0 45.6 %copy-start.3 = (s32[128,1]{0,1:T(1,128)S(1)}, s32[128,1]{0,1:T(1,128)}, u32[]{:S(2)}) copy-start(s32[128,1]{0,1:T(1,128)} %param.15) | copy-start | bytes 1540
  30.0 24.2 %collective-permute-start.1 = (bf16[64,16,512]{2,1,0:T(8,128)(2,1)S(1)}, bf16[64,16,512]{2,1,0:T(8,128)(2,1)S(1)}, u32[]{:S(2)}, u32[]{:S(2)}) collective-permute-start(bf16[64,16,512]{2,1,0:T(8,128)(2,1)S(1)} %get-tuple-element.113), channel_id=1, source_target_pairs={{0,1},{1,0},{2,3},{3,2},{4,5},{5,4},{6,7},{7,6},{8,9},{9,8},{10,11... | collective-permute-start | bytes 3145736 | tf_op jit(solution)/shard_map/ppermute | solution.py:182
  30.6 17.8 %collective-permute-start.23 = (bf16[2,4,4,16,512]{4,3,2,1,0:T(8,128)(2,1)S(1)}, bf16[2,4,4,16,512]{4,3,2,1,0:T(8,128)(2,1)S(1)}, u32[]{:S(2)}, u32[]{:S(2)}) collective-permute-start(bf16[2,4,4,16,512]{4,3,2,1,0:T(8,128)(2,1)S(1)} %get-tuple-element.145), channel_id=1, source_target_pairs={{0,6},{2,0},{4,2},{6,4},{8,14},{10,8},{12,10},{14,12},{16,22},{18,... | collective-permute-start | bytes 1572872 | tf_op jit(solution)/shard_map/ppermute | solution.py:44
  31.4 52.7 %collective-permute-start.11 = (bf16[64,16,512]{2,1,0:T(8,128)(2,1)S(1)}, bf16[64,16,512]{2,1,0:T(8,128)(2,1)S(1)}, u32[]{:S(2)}, u32[]{:S(2)}) collective-permute-start(bf16[64,16,512]{2,1,0:T(8,128)(2,1)S(1)} %get-tuple-element.128), channel_id=1, source_target_pairs={{0,1},{1,0},{2,3},{3,2},{4,5},{5,4},{6,7},{7,6},{8,9},{9,8},{10,11... | collective-permute-start | bytes 3145736 | tf_op jit(solution)/shard_map/ppermute | solution.py:182
  49.1 14.1 %collective-permute-start.24 = (bf16[8,4,16,512]{3,2,1,0:T(8,128)(2,1)S(1)}, bf16[8,4,16,512]{3,2,1,0:T(8,128)(2,1)S(1)}, u32[]{:S(2)}, u32[]{:S(2)}) collective-permute-start(bf16[8,4,16,512]{3,2,1,0:T(8,128)(2,1)S(1)} %get-tuple-element.147), channel_id=1, source_target_pairs={{0,32},{2,34},{4,36},{6,38},{8,40},{10,42},{12,44},{14,46},{16,48}... | collective-permute-start | bytes 1572872 | tf_op jit(solution)/shard_map/ppermute | solution.py:44
  50.5 25.0 %collective-permute-start.25 = (bf16[8,4,16,512]{3,2,1,0:T(8,128)(2,1)S(1)}, bf16[8,4,16,512]{3,2,1,0:T(8,128)(2,1)S(1)}, u32[]{:S(2)}, u32[]{:S(2)}) collective-permute-start(bf16[8,4,16,512]{3,2,1,0:T(8,128)(2,1)S(1)} %get-tuple-element.148), channel_id=1, source_target_pairs={{0,64},{2,66},{4,68},{6,70},{8,72},{10,74},{12,76},{14,78},{16,80}... | collective-permute-start | bytes 1572872 | tf_op jit(solution)/shard_map/ppermute | solution.py:44
  53.1 22.4 %collective-permute-start.26 = (bf16[8,4,16,512]{3,2,1,0:T(8,128)(2,1)S(1)}, bf16[8,4,16,512]{3,2,1,0:T(8,128)(2,1)S(1)}, u32[]{:S(2)}, u32[]{:S(2)}) collective-permute-start(bf16[8,4,16,512]{3,2,1,0:T(8,128)(2,1)S(1)} %get-tuple-element.149), channel_id=1, source_target_pairs={{0,96},{2,98},{4,100},{6,102},{8,104},{10,106},{12,108},{14,110},{... | collective-permute-start | bytes 1572872 | tf_op jit(solution)/shard_map/ppermute | solution.py:44
  54.2 39.0 %copy-start.2 = (f32[8,3,16,512]{3,2,1,0:T(8,128)S(1)}, f32[8,3,16,512]{3,2,1,0:T(8,128)}, u32[]{:S(2)}) copy-start(f32[8,3,16,512]{3,2,1,0:T(8,128)} %moment_v.5) | copy-start | bytes 2359300
  54.9 48.7 %collective-permute-start.2 = (bf16[2,4,4,16,512]{4,3,2,1,0:T(8,128)(2,1)S(1)}, bf16[2,4,4,16,512]{4,3,2,1,0:T(8,128)(2,1)S(1)}, u32[]{:S(2)}, u32[]{:S(2)}) collective-permute-start(bf16[2,4,4,16,512]{4,3,2,1,0:T(8,128)(2,1)S(1)} %get-tuple-element.115), channel_id=1, source_target_pairs={{0,32},{2,34},{4,36},{6,38},{8,40},{10,42},{12,44},{14,46},{16,48}... | collective-permute-start | bytes 1572872 | tf_op jit(solution)/shard_map/ppermute | solution.py:44
  77.4 7.7 %collective-permute-start.27 = (bf16[8,16,512]{2,1,0:T(8,128)(2,1)S(1)}, bf16[8,16,512]{2,1,0:T(8,128)(2,1)S(1)}, u32[]{:S(2)}, u32[]{:S(2)}) collective-permute-start(bf16[8,16,512]{2,1,0:T(8,128)(2,1)S(1)} %get-tuple-element.151), channel_id=1, source_target_pairs={{0,16},{2,18},{4,20},{6,22},{8,24},{10,26},{12,28},{14,30},{16,0},... | collective-permute-start | bytes 393224 | tf_op jit(solution)/shard_map/ppermute | solution.py:44
  80.2 25.2 %collective-permute-start.3 = (bf16[2,4,4,16,512]{4,3,2,1,0:T(8,128)(2,1)S(1)}, bf16[2,4,4,16,512]{4,3,2,1,0:T(8,128)(2,1)S(1)}, u32[]{:S(2)}, u32[]{:S(2)}) collective-permute-start(bf16[2,4,4,16,512]{4,3,2,1,0:T(8,128)(2,1)S(1)} %get-tuple-element.116), channel_id=1, source_target_pairs={{0,64},{2,66},{4,68},{6,70},{8,72},{10,74},{12,76},{14,78},{16,80}... | collective-permute-start | bytes 1572872 | tf_op jit(solution)/shard_map/ppermute | solution.py:44
  82.2 24.2 %collective-permute-start.4 = (bf16[2,4,4,16,512]{4,3,2,1,0:T(8,128)(2,1)S(1)}, bf16[2,4,4,16,512]{4,3,2,1,0:T(8,128)(2,1)S(1)}, u32[]{:S(2)}, u32[]{:S(2)}) collective-permute-start(bf16[2,4,4,16,512]{4,3,2,1,0:T(8,128)(2,1)S(1)} %get-tuple-element.117), channel_id=1, source_target_pairs={{0,96},{2,98},{4,100},{6,102},{8,104},{10,106},{12,108},{14,110},{... | collective-permute-start | bytes 1572872 | tf_op jit(solution)/shard_map/ppermute | solution.py:44
  84.1 5.0 %collective-permute-start.28 = (bf16[8,16,512]{2,1,0:T(8,128)(2,1)S(1)}, bf16[8,16,512]{2,1,0:T(8,128)(2,1)S(1)}, u32[]{:S(2)}, u32[]{:S(2)}) collective-permute-start(bf16[8,16,512]{2,1,0:T(8,128)(2,1)S(1)} %get-tuple-element.152), channel_id=1, source_target_pairs={{0,8},{2,10},{4,12},{6,14},{8,16},{10,18},{12,20},{14,22},{16,24},... | collective-permute-start | bytes 393224 | tf_op jit(solution)/shard_map/ppermute | solution.py:44
  85.1 25.8 %collective-permute-start.12 = (bf16[2,4,4,16,512]{4,3,2,1,0:T(8,128)(2,1)S(1)}, bf16[2,4,4,16,512]{4,3,2,1,0:T(8,128)(2,1)S(1)}, u32[]{:S(2)}, u32[]{:S(2)}) collective-permute-start(bf16[2,4,4,16,512]{4,3,2,1,0:T(8,128)(2,1)S(1)} %get-tuple-element.130), channel_id=1, source_target_pairs={{0,8},{2,10},{4,12},{6,14},{8,16},{10,18},{12,20},{14,22},{16,24},... | collective-permute-start | bytes 1572872 | tf_op jit(solution)/shard_map/ppermute | solution.py:44
  89.1 4.1 %collective-permute-start.29 = (bf16[8,16,512]{2,1,0:T(8,128)(2,1)S(1)}, bf16[8,16,512]{2,1,0:T(8,128)(2,1)S(1)}, u32[]{:S(2)}, u32[]{:S(2)}) collective-permute-start(bf16[8,16,512]{2,1,0:T(8,128)(2,1)S(1)} %get-tuple-element.153), channel_id=1, source_target_pairs={{0,24},{2,26},{4,28},{6,30},{8,0},{10,2},{12,4},{14,6},{16,8},{18,... | collective-permute-start | bytes 393224 | tf_op jit(solution)/shard_map/ppermute | solution.py:44
  93.5 8.9 %collective-permute-start.50 = (bf16[8,16,512]{2,1,0:T(8,128)(2,1)S(1)}, bf16[8,16,512]{2,1,0:T(8,128)(2,1)S(1)}, u32[]{:S(2)}, u32[]{:S(2)}) collective-permute-start(bf16[8,16,512]{2,1,0:T(8,128)(2,1)S(1)} %get-tuple-element.181), channel_id=1, source_target_pairs={{0,8},{2,10},{4,12},{6,14},{8,16},{10,18},{12,20},{14,22},{16,24},... | collective-permute-start | bytes 393224 | tf_op jit(solution)/shard_map/ppermute | solution.py:44
  102.3 5.8 %collective-permute-start.51 = (bf16[8,16,512]{2,1,0:T(8,128)(2,1)S(1)}, bf16[8,16,512]{2,1,0:T(8,128)(2,1)S(1)}, u32[]{:S(2)}, u32[]{:S(2)}) collective-permute-start(bf16[8,16,512]{2,1,0:T(8,128)(2,1)S(1)} %get-tuple-element.181), channel_id=1, source_target_pairs={{0,16},{2,18},{4,20},{6,22},{8,24},{10,26},{12,28},{14,30},{16,0},... | collective-permute-start | bytes 393224 | tf_op jit(solution)/shard_map/ppermute | solution.py:44
  103.6 5.3 %collective-permute-start.52 = (bf16[8,16,512]{2,1,0:T(8,128)(2,1)S(1)}, bf16[8,16,512]{2,1,0:T(8,128)(2,1)S(1)}, u32[]{:S(2)}, u32[]{:S(2)}) collective-permute-start(bf16[8,16,512]{2,1,0:T(8,128)(2,1)S(1)} %get-tuple-element.181), channel_id=1, source_target_pairs={{0,24},{2,26},{4,28},{6,30},{8,0},{10,2},{12,4},{14,6},{16,8},{18,... | collective-permute-start | bytes 393224 | tf_op jit(solution)/shard_map/ppermute | solution.py:44
  105.4 15.2 %collective-permute-start.13 = (bf16[2,4,4,16,512]{4,3,2,1,0:T(8,128)(2,1)S(1)}, bf16[2,4,4,16,512]{4,3,2,1,0:T(8,128)(2,1)S(1)}, u32[]{:S(2)}, u32[]{:S(2)}) collective-permute-start(bf16[2,4,4,16,512]{4,3,2,1,0:T(8,128)(2,1)S(1)} %get-tuple-element.131), channel_id=1, source_target_pairs={{0,16},{2,18},{4,20},{6,22},{8,24},{10,26},{12,28},{14,30},{16,0},... | collective-permute-start | bytes 1572872 | tf_op jit(solution)/shard_map/ppermute | solution.py:44
  106.5 25.5 %collective-permute-start.14 = (bf16[2,4,4,16,512]{4,3,2,1,0:T(8,128)(2,1)S(1)}, bf16[2,4,4,16,512]{4,3,2,1,0:T(8,128)(2,1)S(1)}, u32[]{:S(2)}, u32[]{:S(2)}) collective-permute-start(bf16[2,4,4,16,512]{4,3,2,1,0:T(8,128)(2,1)S(1)} %get-tuple-element.132), channel_id=1, source_target_pairs={{0,24},{2,26},{4,28},{6,30},{8,0},{10,2},{12,4},{14,6},{16,8},{18,... | collective-permute-start | bytes 1572872 | tf_op jit(solution)/shard_map/ppermute | solution.py:44
  108.2 26.8 %collective-permute-start.5 = (bf16[8,4,16,512]{3,2,1,0:T(8,128)(2,1)S(1)}, bf16[8,4,16,512]{3,2,1,0:T(8,128)(2,1)S(1)}, u32[]{:S(2)}, u32[]{:S(2)}) collective-permute-start(bf16[8,4,16,512]{3,2,1,0:T(8,128)(2,1)S(1)} %get-tuple-element.119), channel_id=1, source_target_pairs={{0,8},{2,10},{4,12},{6,14},{8,16},{10,18},{12,20},{14,22},{16,24},... | collective-permute-start | bytes 1572872 | tf_op jit(solution)/shard_map/ppermute | solution.py:44
  108.8 34.2 %collective-permute-start.6 = (bf16[8,4,16,512]{3,2,1,0:T(8,128)(2,1)S(1)}, bf16[8,4,16,512]{3,2,1,0:T(8,128)(2,1)S(1)}, u32[]{:S(2)}, u32[]{:S(2)}) collective-permute-start(bf16[8,4,16,512]{3,2,1,0:T(8,128)(2,1)S(1)} %get-tuple-element.120), channel_id=1, source_target_pairs={{0,16},{2,18},{4,20},{6,22},{8,24},{10,26},{12,28},{14,30},{16,0},... | collective-permute-start | bytes 1572872 | tf_op jit(solution)/shard_map/ppermute | solution.py:44
  110.8 43.3 %collective-permute-start.7 = (bf16[8,4,16,512]{3,2,1,0:T(8,128)(2,1)S(1)}, bf16[8,4,16,512]{3,2,1,0:T(8,128)(2,1)S(1)}, u32[]{:S(2)}, u32[]{:S(2)}) collective-permute-start(bf16[8,4,16,512]{3,2,1,0:T(8,128)(2,1)S(1)} %get-tuple-element.121), channel_id=1, source_target_pairs={{0,24},{2,26},{4,28},{6,30},{8,0},{10,2},{12,4},{14,6},{16,8},{18,... | collective-permute-start | bytes 1572872 | tf_op jit(solution)/shard_map/ppermute | solution.py:44
  120.5 61.7 %collective-permute-start.53 = (bf16[4,8,16,512]{3,2,1,0:T(8,128)(2,1)S(1)}, bf16[4,8,16,512]{3,2,1,0:T(8,128)(2,1)S(1)}, u32[]{:S(2)}, u32[]{:S(2)}) collective-permute-start(bf16[4,8,16,512]{3,2,1,0:T(8,128)(2,1)S(1)} %pad_maximum_fusion.5.refs_0_), channel_id=1, source_target_pairs={{0,32},{2,34},{4,36},{6,38},{8,40},{10,42},{12,44},{14,46},{16,48}... | collective-permute-start | bytes 1572872 | tf_op jit(solution)/shard_map/ppermute | solution.py:44
  132.7 49.7 %collective-permute-start.15 = (bf16[8,4,16,512]{3,2,1,0:T(8,128)(2,1)S(1)}, bf16[8,4,16,512]{3,2,1,0:T(8,128)(2,1)S(1)}, u32[]{:S(2)}, u32[]{:S(2)}) collective-permute-start(bf16[8,4,16,512]{3,2,1,0:T(8,128)(2,1)S(1)} %get-tuple-element.134), channel_id=1, source_target_pairs={{0,2},{2,4},{4,6},{6,0},{8,10},{10,12},{12,14},{14,8},{16,18},{18,... | collective-permute-start | bytes 1572872 | tf_op jit(solution)/shard_map/ppermute | solution.py:44
  135.0 50.0 %collective-permute-start.16 = (bf16[8,4,16,512]{3,2,1,0:T(8,128)(2,1)S(1)}, bf16[8,4,16,512]{3,2,1,0:T(8,128)(2,1)S(1)}, u32[]{:S(2)}, u32[]{:S(2)}) collective-permute-start(bf16[8,4,16,512]{3,2,1,0:T(8,128)(2,1)S(1)} %get-tuple-element.135), channel_id=1, source_target_pairs={{0,4},{2,6},{4,0},{6,2},{8,12},{10,14},{12,8},{14,10},{16,20},{18,... | collective-permute-start | bytes 1572872 | tf_op jit(solution)/shard_map/ppermute | solution.py:44
  156.0 4.4 %collective-permute-start.10 = (bf16[8,16,512]{2,1,0:T(8,128)(2,1)S(1)}, bf16[8,16,512]{2,1,0:T(8,128)(2,1)S(1)}, u32[]{:S(2)}, u32[]{:S(2)}) collective-permute-start(bf16[8,16,512]{2,1,0:T(8,128)(2,1)S(1)} %get-tuple-element.125), channel_id=1, source_target_pairs={{0,6},{2,0},{4,2},{6,4},{8,14},{10,8},{12,10},{14,12},{16,22},{18,... | collective-permute-start | bytes 393224 | tf_op jit(solution)/shard_map/ppermute | solution.py:44
  158.3 26.8 %collective-permute-start.17 = (bf16[8,4,16,512]{3,2,1,0:T(8,128)(2,1)S(1)}, bf16[8,4,16,512]{3,2,1,0:T(8,128)(2,1)S(1)}, u32[]{:S(2)}, u32[]{:S(2)}) collective-permute-start(bf16[8,4,16,512]{3,2,1,0:T(8,128)(2,1)S(1)} %get-tuple-element.136), channel_id=1, source_target_pairs={{0,6},{2,0},{4,2},{6,4},{8,14},{10,8},{12,10},{14,12},{16,22},{18,... | collective-permute-start | bytes 1572872 | tf_op jit(solution)/shard_map/ppermute | solution.py:44
  160.4 5.3 %collective-permute-start.8 = (bf16[8,16,512]{2,1,0:T(8,128)(2,1)S(1)}, bf16[8,16,512]{2,1,0:T(8,128)(2,1)S(1)}, u32[]{:S(2)}, u32[]{:S(2)}) collective-permute-start(bf16[8,16,512]{2,1,0:T(8,128)(2,1)S(1)} %get-tuple-element.123), channel_id=1, source_target_pairs={{0,4},{2,6},{4,0},{6,2},{8,12},{10,14},{12,8},{14,10},{16,20},{18,... | collective-permute-start | bytes 393224 | tf_op jit(solution)/shard_map/ppermute | solution.py:44
  165.7 12.9 %collective-permute-start.9 = (bf16[8,16,512]{2,1,0:T(8,128)(2,1)S(1)}, bf16[8,16,512]{2,1,0:T(8,128)(2,1)S(1)}, u32[]{:S(2)}, u32[]{:S(2)}) collective-permute-start(bf16[8,16,512]{2,1,0:T(8,128)(2,1)S(1)} %get-tuple-element.124), channel_id=1, source_target_pairs={{0,2},{2,4},{4,6},{6,0},{8,10},{10,12},{12,14},{14,8},{16,18},{18,... | collective-permute-start | bytes 393224 | tf_op jit(solution)/shard_map/ppermute | solution.py:44
  178.6 34.8 %collective-permute-start.54 = (bf16[4,8,16,512]{3,2,1,0:T(8,128)(2,1)S(1)}, bf16[4,8,16,512]{3,2,1,0:T(8,128)(2,1)S(1)}, u32[]{:S(2)}, u32[]{:S(2)}) collective-permute-start(bf16[4,8,16,512]{3,2,1,0:T(8,128)(2,1)S(1)} %pad_maximum_fusion.5.refs_0_), channel_id=1, source_target_pairs={{0,64},{2,66},{4,68},{6,70},{8,72},{10,74},{12,76},{14,78},{16,80}... | collective-permute-start | bytes 1572872 | tf_op jit(solution)/shard_map/ppermute | solution.py:44
  182.2 39.0 %copy-start.4 = (s32[128,1]{0,1:T(1,128)S(1)}, s32[128,1]{0,1:T(1,128)}, u32[]{:S(2)}) copy-start(s32[128,1]{0,1:T(1,128)} %param.16) | copy-start | bytes 1540
  182.2 5.4 %collective-permute-start.40 = (bf16[8,16,512]{2,1,0:T(8,128)(2,1)S(1)}, bf16[8,16,512]{2,1,0:T(8,128)(2,1)S(1)}, u32[]{:S(2)}, u32[]{:S(2)}) collective-permute-start(bf16[8,16,512]{2,1,0:T(8,128)(2,1)S(1)} %get-tuple-element.171), channel_id=1, source_target_pairs={{0,2},{2,4},{4,6},{6,0},{8,10},{10,12},{12,14},{14,8},{16,18},{18,... | collective-permute-start | bytes 393224 | tf_op jit(solution)/shard_map/ppermute | solution.py:44
  182.3 6.7 %collective-permute-start.41 = (bf16[8,16,512]{2,1,0:T(8,128)(2,1)S(1)}, bf16[8,16,512]{2,1,0:T(8,128)(2,1)S(1)}, u32[]{:S(2)}, u32[]{:S(2)}) collective-permute-start(bf16[8,16,512]{2,1,0:T(8,128)(2,1)S(1)} %get-tuple-element.171), channel_id=1, source_target_pairs={{0,4},{2,6},{4,0},{6,2},{8,12},{10,14},{12,8},{14,10},{16,20},{18,... | collective-permute-start | bytes 393224 | tf_op jit(solution)/shard_map/ppermute | solution.py:44
  185.0 4.7 %collective-permute-start.42 = (bf16[8,16,512]{2,1,0:T(8,128)(2,1)S(1)}, bf16[8,16,512]{2,1,0:T(8,128)(2,1)S(1)}, u32[]{:S(2)}, u32[]{:S(2)}) collective-permute-start(bf16[8,16,512]{2,1,0:T(8,128)(2,1)S(1)} %get-tuple-element.171), channel_id=1, source_target_pairs={{0,6},{2,0},{4,2},{6,4},{8,14},{10,8},{12,10},{14,12},{16,22},{18,... | collective-permute-start | bytes 393224 | tf_op jit(solution)/shard_map/ppermute | solution.py:44
  185.2 30.6 %collective-permute-start.55 = (bf16[4,8,16,512]{3,2,1,0:T(8,128)(2,1)S(1)}, bf16[4,8,16,512]{3,2,1,0:T(8,128)(2,1)S(1)}, u32[]{:S(2)}, u32[]{:S(2)}) collective-permute-start(bf16[4,8,16,512]{3,2,1,0:T(8,128)(2,1)S(1)} %pad_maximum_fusion.5.refs_0_), channel_id=1, source_target_pairs={{0,96},{2,98},{4,100},{6,102},{8,104},{10,106},{12,108},{14,110},{... | collective-permute-start | bytes 1572872 | tf_op jit(solution)/shard_map/ppermute | solution.py:44
  187.7 7.0 %collective-permute-start.18 = (bf16[8,16,512]{2,1,0:T(8,128)(2,1)S(1)}, bf16[8,16,512]{2,1,0:T(8,128)(2,1)S(1)}, u32[]{:S(2)}, u32[]{:S(2)}) collective-permute-start(bf16[8,16,512]{2,1,0:T(8,128)(2,1)S(1)} %get-tuple-element.138), channel_id=1, source_target_pairs={{0,64},{2,66},{4,68},{6,70},{8,72},{10,74},{12,76},{14,78},{16,80}... | collective-permute-start | bytes 393224 | tf_op jit(solution)/shard_map/ppermute | solution.py:44
  189.0 8.4 %collective-permute-start.19 = (bf16[8,16,512]{2,1,0:T(8,128)(2,1)S(1)}, bf16[8,16,512]{2,1,0:T(8,128)(2,1)S(1)}, u32[]{:S(2)}, u32[]{:S(2)}) collective-permute-start(bf16[8,16,512]{2,1,0:T(8,128)(2,1)S(1)} %get-tuple-element.139), channel_id=1, source_target_pairs={{0,32},{2,34},{4,36},{6,38},{8,40},{10,42},{12,44},{14,46},{16,48}... | collective-permute-start | bytes 393224 | tf_op jit(solution)/shard_map/ppermute | solution.py:44
  189.7 16.5 %collective-permute-start.20 = (bf16[8,16,512]{2,1,0:T(8,128)(2,1)S(1)}, bf16[8,16,512]{2,1,0:T(8,128)(2,1)S(1)}, u32[]{:S(2)}, u32[]{:S(2)}) collective-permute-start(bf16[8,16,512]{2,1,0:T(8,128)(2,1)S(1)} %get-tuple-element.140), channel_id=1, source_target_pairs={{0,96},{2,98},{4,100},{6,102},{8,104},{10,106},{12,108},{14,110},{... | collective-permute-start | bytes 393224 | tf_op jit(solution)/shard_map/ppermute | solution.py:44
  194.7 32.0 %collective-permute-start.43 = (bf16[4,8,16,512]{3,2,1,0:T(8,128)(2,1)S(1)}, bf16[4,8,16,512]{3,2,1,0:T(8,128)(2,1)S(1)}, u32[]{:S(2)}, u32[]{:S(2)}) collective-permute-start(bf16[4,8,16,512]{3,2,1,0:T(8,128)(2,1)S(1)} %pad_maximum_fusion.4.refs_0_), channel_id=1, source_target_pairs={{0,8},{2,10},{4,12},{6,14},{8,16},{10,18},{12,20},{14,22},{16,24},... | collective-permute-start | bytes 1572872 | tf_op jit(solution)/shard_map/ppermute | solution.py:44
  197.5 29.3 %collective-permute-start.44 = (bf16[4,8,16,512]{3,2,1,0:T(8,128)(2,1)S(1)}, bf16[4,8,16,512]{3,2,1,0:T(8,128)(2,1)S(1)}, u32[]{:S(2)}, u32[]{:S(2)}) collective-permute-start(bf16[4,8,16,512]{3,2,1,0:T(8,128)(2,1)S(1)} %pad_maximum_fusion.4.refs_0_), channel_id=1, source_target_pairs={{0,16},{2,18},{4,20},{6,22},{8,24},{10,26},{12,28},{14,30},{16,0},... | collective-permute-start | bytes 1572872 | tf_op jit(solution)/shard_map/ppermute | solution.py:44
  206.2 25.8 %collective-permute-start.45 = (bf16[4,8,16,512]{3,2,1,0:T(8,128)(2,1)S(1)}, bf16[4,8,16,512]{3,2,1,0:T(8,128)(2,1)S(1)}, u32[]{:S(2)}, u32[]{:S(2)}) collective-permute-start(bf16[4,8,16,512]{3,2,1,0:T(8,128)(2,1)S(1)} %pad_maximum_fusion.4.refs_0_), channel_id=1, source_target_pairs={{0,24},{2,26},{4,28},{6,30},{8,0},{10,2},{12,4},{14,6},{16,8},{18,... | collective-permute-start | bytes 1572872 | tf_op jit(solution)/shard_map/ppermute | solution.py:44
  213.2 43.7 %slice-start = ((s8[6291456]{0:T(1024)(128)(4,1)}), s8[4194304]{0:T(1024)(128)(4,1)S(1)}, s32[]{:S(2)}) async-start(s8[6291456]{0:T(1024)(128)(4,1)} %bitcast.67), calls=%async_computation | async-start | bytes 8388608
  213.5 6.3 %collective-permute-start.30 = (bf16[8,16,512]{2,1,0:T(8,128)(2,1)S(1)}, bf16[8,16,512]{2,1,0:T(8,128)(2,1)S(1)}, u32[]{:S(2)}, u32[]{:S(2)}) collective-permute-start(bf16[8,16,512]{2,1,0:T(8,128)(2,1)S(1)} %get-tuple-element.161), channel_id=1, source_target_pairs={{0,32},{2,34},{4,36},{6,38},{8,40},{10,42},{12,44},{14,46},{16,48}... | collective-permute-start | bytes 393224 | tf_op jit(solution)/shard_map/ppermute | solution.py:44
  215.7 7.4 %collective-permute-start.31 = (bf16[8,16,512]{2,1,0:T(8,128)(2,1)S(1)}, bf16[8,16,512]{2,1,0:T(8,128)(2,1)S(1)}, u32[]{:S(2)}, u32[]{:S(2)}) collective-permute-start(bf16[8,16,512]{2,1,0:T(8,128)(2,1)S(1)} %get-tuple-element.161), channel_id=1, source_target_pairs={{0,64},{2,66},{4,68},{6,70},{8,72},{10,74},{12,76},{14,78},{16,80}... | collective-permute-start | bytes 393224 | tf_op jit(solution)/shard_map/ppermute | solution.py:44
  219.8 4.1 %collective-permute-start.32 = (bf16[8,16,512]{2,1,0:T(8,128)(2,1)S(1)}, bf16[8,16,512]{2,1,0:T(8,128)(2,1)S(1)}, u32[]{:S(2)}, u32[]{:S(2)}) collective-permute-start(bf16[8,16,512]{2,1,0:T(8,128)(2,1)S(1)} %get-tuple-element.161), channel_id=1, source_target_pairs={{0,96},{2,98},{4,100},{6,102},{8,104},{10,106},{12,108},{14,110},{... | collective-permute-start | bytes 393224 | tf_op jit(solution)/shard_map/ppermute | solution.py:44
  224.0 11.1 %collective-permute-start.33 = (bf16[4,8,16,512]{3,2,1,0:T(8,128)(2,1)S(1)}, bf16[4,8,16,512]{3,2,1,0:T(8,128)(2,1)S(1)}, u32[]{:S(2)}, u32[]{:S(2)}) collective-permute-start(bf16[4,8,16,512]{3,2,1,0:T(8,128)(2,1)S(1)} %pad_maximum_fusion.3.refs_0_), channel_id=1, source_target_pairs={{0,2},{2,4},{4,6},{6,0},{8,10},{10,12},{12,14},{14,8},{16,18},{18,... | collective-permute-start | bytes 1572872 | tf_op jit(solution)/shard_map/ppermute | solution.py:44
  224.0 22.2 %collective-permute-start.34 = (bf16[4,8,16,512]{3,2,1,0:T(8,128)(2,1)S(1)}, bf16[4,8,16,512]{3,2,1,0:T(8,128)(2,1)S(1)}, u32[]{:S(2)}, u32[]{:S(2)}) collective-permute-start(bf16[4,8,16,512]{3,2,1,0:T(8,128)(2,1)S(1)} %pad_maximum_fusion.3.refs_0_), channel_id=1, source_target_pairs={{0,4},{2,6},{4,0},{6,2},{8,12},{10,14},{12,8},{14,10},{16,20},{18,... | collective-permute-start | bytes 1572872 | tf_op jit(solution)/shard_map/ppermute | solution.py:44
  226.7 22.6 %collective-permute-start.35 = (bf16[4,8,16,512]{3,2,1,0:T(8,128)(2,1)S(1)}, bf16[4,8,16,512]{3,2,1,0:T(8,128)(2,1)S(1)}, u32[]{:S(2)}, u32[]{:S(2)}) collective-permute-start(bf16[4,8,16,512]{3,2,1,0:T(8,128)(2,1)S(1)} %pad_maximum_fusion.3.refs_0_), channel_id=1, source_target_pairs={{0,6},{2,0},{4,2},{6,4},{8,14},{10,8},{12,10},{14,12},{16,22},{18,... | collective-permute-start | bytes 1572872 | tf_op jit(solution)/shard_map/ppermute | solution.py:44
  226.7 25.6 %collective-permute-start.56 = (bf16[4,4,4,16,512]{4,3,2,1,0:T(8,128)(2,1)S(1)}, bf16[4,4,4,16,512]{4,3,2,1,0:T(8,128)(2,1)S(1)}, u32[]{:S(2)}, u32[]{:S(2)}) collective-permute-start(bf16[4,4,4,16,512]{4,3,2,1,0:T(8,128)(2,1)S(1)} %get-tuple-element.186), channel_id=1, source_target_pairs={{0,1},{1,0},{2,3},{3,2},{4,5},{5,4},{6,7},{7,6},{8,9},{9,8},{10,11... | collective-permute-start | bytes 3145736 | tf_op jit(solution)/shard_map/ppermute | solution.py:239
  232.8 23.0 %collective-permute-start.46 = (bf16[4,4,4,16,512]{4,3,2,1,0:T(8,128)(2,1)S(1)}, bf16[4,4,4,16,512]{4,3,2,1,0:T(8,128)(2,1)S(1)}, u32[]{:S(2)}, u32[]{:S(2)}) collective-permute-start(bf16[4,4,4,16,512]{4,3,2,1,0:T(8,128)(2,1)S(1)} %get-tuple-element.176), channel_id=1, source_target_pairs={{0,1},{1,0},{2,3},{3,2},{4,5},{5,4},{6,7},{7,6},{8,9},{9,8},{10,11... | collective-permute-start | bytes 3145736 | tf_op jit(solution)/shard_map/ppermute | solution.py:239
  250.1 7.8 %collective-permute-start.36 = (bf16[4,4,4,16,512]{4,3,2,1,0:T(8,128)(2,1)S(1)}, bf16[4,4,4,16,512]{4,3,2,1,0:T(8,128)(2,1)S(1)}, u32[]{:S(2)}, u32[]{:S(2)}) collective-permute-start(bf16[4,4,4,16,512]{4,3,2,1,0:T(8,128)(2,1)S(1)} %get-tuple-element.166), channel_id=1, source_target_pairs={{0,1},{1,0},{2,3},{3,2},{4,5},{5,4},{6,7},{7,6},{8,9},{9,8},{10,11... | collective-permute-start | bytes 3145736 | tf_op jit(solution)/shard_map/ppermute | solution.py:239
  252.5 14.7 %collective-permute-start.57 = (bf16[2,4,4,16,512]{4,3,2,1,0:T(8,128)(2,1)S(1)}, bf16[2,4,4,16,512]{4,3,2,1,0:T(8,128)(2,1)S(1)}, u32[]{:S(2)}, u32[]{:S(2)}) collective-permute-start(bf16[2,4,4,16,512]{4,3,2,1,0:T(8,128)(2,1)S(1)} %get-tuple-element.188), channel_id=1, source_target_pairs={{0,2},{2,4},{4,6},{6,0},{8,10},{10,12},{12,14},{14,8},{16,18},{18,... | collective-permute-start | bytes 1572872 | tf_op jit(solution)/shard_map/ppermute | solution.py:44
  252.5 26.5 %collective-permute-start.58 = (bf16[2,4,4,16,512]{4,3,2,1,0:T(8,128)(2,1)S(1)}, bf16[2,4,4,16,512]{4,3,2,1,0:T(8,128)(2,1)S(1)}, u32[]{:S(2)}, u32[]{:S(2)}) collective-permute-start(bf16[2,4,4,16,512]{4,3,2,1,0:T(8,128)(2,1)S(1)} %get-tuple-element.189), channel_id=1, source_target_pairs={{0,4},{2,6},{4,0},{6,2},{8,12},{10,14},{12,8},{14,10},{16,20},{18,... | collective-permute-start | bytes 1572872 | tf_op jit(solution)/shard_map/ppermute | solution.py:44
  255.8 23.2 %collective-permute-start.59 = (bf16[2,4,4,16,512]{4,3,2,1,0:T(8,128)(2,1)S(1)}, bf16[2,4,4,16,512]{4,3,2,1,0:T(8,128)(2,1)S(1)}, u32[]{:S(2)}, u32[]{:S(2)}) collective-permute-start(bf16[2,4,4,16,512]{4,3,2,1,0:T(8,128)(2,1)S(1)} %get-tuple-element.190), channel_id=1, source_target_pairs={{0,6},{2,0},{4,2},{6,4},{8,14},{10,8},{12,10},{14,12},{16,22},{18,... | collective-permute-start | bytes 1572872 | tf_op jit(solution)/shard_map/ppermute | solution.py:44
  255.9 25.2 %collective-permute-start.47 = (bf16[2,4,4,16,512]{4,3,2,1,0:T(8,128)(2,1)S(1)}, bf16[2,4,4,16,512]{4,3,2,1,0:T(8,128)(2,1)S(1)}, u32[]{:S(2)}, u32[]{:S(2)}) collective-permute-start(bf16[2,4,4,16,512]{4,3,2,1,0:T(8,128)(2,1)S(1)} %get-tuple-element.178), channel_id=1, source_target_pairs={{0,32},{2,34},{4,36},{6,38},{8,40},{10,42},{12,44},{14,46},{16,48}... | collective-permute-start | bytes 1572872 | tf_op jit(solution)/shard_map/ppermute | solution.py:44
  257.9 31.3 %collective-permute-start.48 = (bf16[2,4,4,16,512]{4,3,2,1,0:T(8,128)(2,1)S(1)}, bf16[2,4,4,16,512]{4,3,2,1,0:T(8,128)(2,1)S(1)}, u32[]{:S(2)}, u32[]{:S(2)}) collective-permute-start(bf16[2,4,4,16,512]{4,3,2,1,0:T(8,128)(2,1)S(1)} %get-tuple-element.179), channel_id=1, source_target_pairs={{0,64},{2,66},{4,68},{6,70},{8,72},{10,74},{12,76},{14,78},{16,80}... | collective-permute-start | bytes 1572872 | tf_op jit(solution)/shard_map/ppermute | solution.py:44
  267.2 22.0 %collective-permute-start.49 = (bf16[2,4,4,16,512]{4,3,2,1,0:T(8,128)(2,1)S(1)}, bf16[2,4,4,16,512]{4,3,2,1,0:T(8,128)(2,1)S(1)}, u32[]{:S(2)}, u32[]{:S(2)}) collective-permute-start(bf16[2,4,4,16,512]{4,3,2,1,0:T(8,128)(2,1)S(1)} %get-tuple-element.180), channel_id=1, source_target_pairs={{0,96},{2,98},{4,100},{6,102},{8,104},{10,106},{12,108},{14,110},{... | collective-permute-start | bytes 1572872 | tf_op jit(solution)/shard_map/ppermute | solution.py:44
  279.0 14.4 %collective-permute-start.37 = (bf16[2,4,4,16,512]{4,3,2,1,0:T(8,128)(2,1)S(1)}, bf16[2,4,4,16,512]{4,3,2,1,0:T(8,128)(2,1)S(1)}, u32[]{:S(2)}, u32[]{:S(2)}) collective-permute-start(bf16[2,4,4,16,512]{4,3,2,1,0:T(8,128)(2,1)S(1)} %get-tuple-element.168), channel_id=1, source_target_pairs={{0,8},{2,10},{4,12},{6,14},{8,16},{10,18},{12,20},{14,22},{16,24},... | collective-permute-start | bytes 1572872 | tf_op jit(solution)/shard_map/ppermute | solution.py:44
  279.0 24.5 %collective-permute-start.38 = (bf16[2,4,4,16,512]{4,3,2,1,0:T(8,128)(2,1)S(1)}, bf16[2,4,4,16,512]{4,3,2,1,0:T(8,128)(2,1)S(1)}, u32[]{:S(2)}, u32[]{:S(2)}) collective-permute-start(bf16[2,4,4,16,512]{4,3,2,1,0:T(8,128)(2,1)S(1)} %get-tuple-element.169), channel_id=1, source_target_pairs={{0,16},{2,18},{4,20},{6,22},{8,24},{10,26},{12,28},{14,30},{16,0},... | collective-permute-start | bytes 1572872 | tf_op jit(solution)/shard_map/ppermute | solution.py:44
  281.1 23.7 %collective-permute-start.39 = (bf16[2,4,4,16,512]{4,3,2,1,0:T(8,128)(2,1)S(1)}, bf16[2,4,4,16,512]{4,3,2,1,0:T(8,128)(2,1)S(1)}, u32[]{:S(2)}, u32[]{:S(2)}) collective-permute-start(bf16[2,4,4,16,512]{4,3,2,1,0:T(8,128)(2,1)S(1)} %get-tuple-element.170), channel_id=1, source_target_pairs={{0,24},{2,26},{4,28},{6,30},{8,0},{10,2},{12,4},{14,6},{16,8},{18,... | collective-permute-start | bytes 1572872 | tf_op jit(solution)/shard_map/ppermute | solution.py:44
  (6 other events, 111.0 us)
where the time goes:
time: 307 us
  waiting for transfers between devices  161 us (52%)
  starting transfers between devices  97.3 us (32%)
  Pallas kernels  38.3 us (12%)
  local copies, waits for them, and re-layouts  5.68 us (2%)
  matrix products  3.16 us (1%)
    ppermute x54, waiting for transfers between devices, shift(): lax.ppermute(array, 'wide', [(chip, moved(chip, axis, steps)) for chip in...  161 us
    ppermute x54, starting transfers between devices, shift(): lax.ppermute(array, 'wide', [(chip, moved(chip, axis, steps)) for chip in...  87.2 us
    pallas_call x24, Pallas kernels, call(): pl.pallas_call(body, out_shape=outs, in_specs=in_specs, out_specs=specs,...  38.3 us
    ppermute x3, starting transfers between devices, send_weights(): other = lax.ppermute(sent, 'narrow', [(0, 1), (1, 0)])  7.58 us
  transfers between devices with their start and end apart: 60, of which 33 were waited for; matrix products, arithmetic and copies ran while one was open for 2% of the time, Pallas kernels for 8%

commit v1 on v0

--- a/solution.py
+++ b/solution.py
@@ -94,12 +94,8 @@
     for back_b in range(RING):
         for k in range(RING * CORES):
             expert = expert_of[slot_of(pos, order, k // CORES, back_b, k % CORES)]
-
-            def add(block, carry, expert=expert, piece=ins[back_b].at[k]):
-                total[block, expert] += piece[block].astype(F32)
-                return carry
-
-            lax.fori_loop(0, RING, add, 0)
+            for block in range(RING):
+                total[block, expert] += ins[back_b][k, block].astype(F32)
     for steps in range(RING):
         target = (pos[d] + steps) & (RING - 1)
         outs[steps][...] = total[target].astype(outs[steps].dtype)
@@ -207,7 +203,8 @@
         (pos, slot_expert, parts[0], parts[2], parts[1], parts[3]),
         scratch_shapes=[pltpu.VMEM((RING, *tile), F32)],
     )
-    return around(parts, d)
+    parts = around(parts, d)
+    return parts[0], parts[2], parts[1], parts[3]
 
 
 def update(grads, part, master, moment_m, moment_v):
@@ -371,20 +368,19 @@
     up_sum[...] = mul(chosen, d_up[...], (1, 0)).astype(BF16)
 
 
-def pool_grads(pos, pool, gate_sum, up_sum, gate_own, gate_other, up_own, up_other, grad):
-    width, hidden_units = pool.shape[1], gate_sum.shape[1]
+def pool_grad(pos, pool, total, own, other, grad):
+    width, hidden_units = pool.shape[1], total.shape[1]
     scale_in = width ** (-0.5)
     blocks = hidden_units // (BLOCK * CORES)
-    for total, own, other in ((gate_sum, gate_own, gate_other), (up_sum, up_own, up_other)):
-
-        def outer(step, carry, total=total):
-            r = pl.ds(pl.multiple_of(step * hidden_units, hidden_units), hidden_units)
-            values = (mul(pool[:, r], total[...], (0, 0)) * scale_in).astype(BF16)
-            grad[pl.ds(step * blocks, blocks)] = values.reshape(blocks, CORES, BLOCK, hidden_units)
-            return carry
-
-        lax.fori_loop(0, width // hidden_units, outer, 0)
-        halve(pos, grad, own, other)
+
+    def outer(step, carry):
+        r = pl.ds(pl.multiple_of(step * hidden_units, hidden_units), hidden_units)
+        values = (mul(pool[:, r], total[...], (0, 0)) * scale_in).astype(BF16)
+        grad[pl.ds(step * blocks, blocks)] = values.reshape(blocks, CORES, BLOCK, hidden_units)
+        return carry
+
+    lax.fori_loop(0, width // hidden_units, outer, 0)
+    halve(pos, grad, own, other)
 
 
 def run_forward(pos, index, route, pool, weights, cot):
@@ -428,17 +424,17 @@
     )
 
 
-def run_pool_grads(pos, pool, gate_sum, up_sum):
-    width, hid = pool.shape[1], gate_sum.shape[1]
+def run_pool_grad(pos, pool, total):
+    width, hid = pool.shape[1], total.shape[1]
     half = (width // (BLOCK * CORES), BLOCK, hid)
     return call(
-        pool_grads,
-        [shaped(half)] * 4,
-        [SMEM, VMEM, VMEM, VMEM],
-        (pos, pool, gate_sum, up_sum),
+        pool_grad,
+        [shaped(half)] * 2,
+        [SMEM, VMEM, VMEM],
+        (pos, pool, total),
         scratch_shapes=[pltpu.VMEM((half[0], CORES, BLOCK, hid), BF16)],
-        limit=20 * 2**20,
-        work=2 * 10**9,
+        limit=16 * 2**20,
+        work=10**9,
     )
 
 
@@ -468,9 +464,9 @@
     cut = {2: start_grads(own, other, ORDERS[2], pos)}
     gate_sum, up_sum = run_backward(row_index, gate, upper, scaled, wd, tokens)
     cut[2], (gate_sum, up_sum) = lax.optimization_barrier((cut[2], (gate_sum, up_sum)))
-    own_0, other_0, own_1, other_1 = run_pool_grads(pos, pool_tokens, gate_sum, up_sum)
-    cut[0] = start_grads(own_0, other_0, ORDERS[0], pos)
-    cut[1] = start_grads(own_1, other_1, ORDERS[1], pos)
+    for part, total in ((0, gate_sum), (1, up_sum)):
+        own, other = run_pool_grad(pos, pool_tokens, total)
+        cut[part] = start_grads(own, other, ORDERS[part], pos)
     token_grads = (
         mul(gate_sum, weights_in[0, 0], (1, 1)) + mul(up_sum, weights_in[0, 1], (1, 1))
     ) * scale_in

time: 307 us -> 300 us (0.977)
  starting transfers between devices: 97.3 us -> 88.2 us
    ppermute x54, starting transfers between devices: 87.2 us -> 79 us  [shift(): lax.ppermute(array, 'wide', [(chip, moved(chip, axis, steps)) for chip in...]
    pallas_call x24 -> x25, Pallas kernels: 38.3 us -> 36.5 us  [call(): pl.pallas_call(body, out_shape=outs, in_specs=in_specs, out_specs=specs,...]
  transfers between devices with their start and end apart: 60 -> 60, of which waited for: 33 -> 30; matrix products, arithmetic and copies ran while one was open for 2% -> 2% of each run, Pallas kernels for 8% -> 8%
where the time goes in v1:
time: 300 us; the launch traced here: 299 us
  waiting for transfers between devices  164 us (55%)
  starting transfers between devices  88.2 us (29%)
  Pallas kernels  36.5 us (12%)
  local copies, waits for them, and re-layouts  5.69 us (2%)
  matrix products  3.16 us (1%)
    ppermute x54, waiting for transfers between devices, shift(): lax.ppermute(array, 'wide', [(chip, moved(chip, axis, steps)) for chip in...  164 us
    ppermute x54, starting transfers between devices, shift(): lax.ppermute(array, 'wide', [(chip, moved(chip, axis, steps)) for chip in...  79 us
    pallas_call x25, Pallas kernels, call(): pl.pallas_call(body, out_shape=outs, in_specs=in_specs, out_specs=specs,...  36.5 us
    ppermute x3, starting transfers between devices, send_weights(): other = lax.ppermute(sent, 'narrow', [(0, 1), (1, 0)])  6.63 us
  transfers between devices with their start and end apart: 60, of which 30 were waited for; matrix products, arithmetic and copies ran while one was open for 2% of the time, Pallas kernels for 8%

profile of v1, /device:TPU:1, one launch (start us, length us, event | category | flops | bytes accessed | tf_op | source)
XLA Modules:
  0.0 298.7 jit_solution(17319061820979823906)
XLA Ops:
  3.5 10.9 %shard_map.137 = (bf16[64,16,512]{2,1,0:T(8,128)(2,1)S(1)}, bf16[64,16,512]{2,1,0:T(8,128)(2,1)S(1)}, f32[768,512]{1,0:T(8,128)S(1)}, f32[768,512]{1,0:T(8,128)S...) custom-call(s32[4]{0:T(128)S(1)} %pad_add_fusion.pos, s32[1,768]{1,0:T(1,128)S(1)} %copy-done.7, ...), custom_call_target="tpu_custom_call" | custom-call | flops 5000000000 | tf_op jit(solution)/shard_map/pallas_call | solution.py:157
  14.5 1.4 collective-permute-start
  15.9 3.4 %shard_map.139 = (bf16[384,512]{1,0:T(8,128)(2,1)S(1)}, bf16[384,512]{1,0:T(8,128)(2,1)S(1)}) custom-call(s32[1,768]{1,0:T(1,128)S(1)} %copy-done.7, f32[768,512]{1,0:T(8,128)S(1)} %get-tuple-element.104.gate, f32[768,512]{1,0:T(8,128)S(1)} %get-tuple-element.105.upper, bf16[768,2048]{1,0:T(8,128)(2,1)S(1)} %get-tuple-element.106.scaled, ...), custom_call_target="tpu_custom_call" | custom-call | flops 3000000000 | tf_op jit(solution)/shard_map/pallas_call | solution.py:157
  20.1 1.8 collective-permute-start.21
  21.9 3.3 %collective-permute-start.22 = (bf16[2,4,4,16,512]{4,3,2,1,0:T(8,128)(2,1)S(1)}, bf16[2,4,4,16,512]{4,3,2,1,0:T(8,128)(2,1)S(1)}, u32[]{:S(2)}, u32[]{:S(2)}) collective-permute-start(bf16[2,4,4,16,512]{4,3,2,1,0:T(8,128)(2,1)S(1)} %get-tuple-element.144), channel_id=1, source_target_pairs={{0,4},{2,6},{4,0},{6,2},{8,12},{10,14},{12,8},{14,10},{16,20},{18,... | collective-permute-start | bytes 1572872 | tf_op jit(solution)/shard_map/ppermute | solution.py:44
  25.2 2.7 shard_map.140
  29.2 2.7 shard_map.145
  32.3 3.9 %collective-permute-done.21.refs_1_ = bf16[2,4,4,16,512]{4,3,2,1,0:T(8,128)(2,1)S(1)} collective-permute-done((bf16[2,4,4,16,512]{4,3,2,1,0:T(8,128)(2,1)S(1)}, bf16[2,4,4,16,512]{4,3,2,1,0:T(8,128)(2,1)S(1)}, u32[]{:S(2)}, u32[]{:S(2)}) %collective-permute-start.21) | collective-permute-done | bytes 524320 | tf_op jit(solution)/shard_map/ppermute | solution.py:44
  36.3 12.1 %collective-permute-done.22.refs_2_ = bf16[2,4,4,16,512]{4,3,2,1,0:T(8,128)(2,1)S(1)} collective-permute-done((bf16[2,4,4,16,512]{4,3,2,1,0:T(8,128)(2,1)S(1)}, bf16[2,4,4,16,512]{4,3,2,1,0:T(8,128)(2,1)S(1)}, u32[]{:S(2)}, u32[]{:S(2)}) %collective-permute-start.22) | collective-permute-done | bytes 524320 | tf_op jit(solution)/shard_map/ppermute | solution.py:44
  50.5 2.6 collective-permute-start.25
  55.4 7.8 %collective-permute-done.24.refs_1_ = bf16[8,4,16,512]{3,2,1,0:T(8,128)(2,1)S(1)} collective-permute-done((bf16[8,4,16,512]{3,2,1,0:T(8,128)(2,1)S(1)}, bf16[8,4,16,512]{3,2,1,0:T(8,128)(2,1)S(1)}, u32[]{:S(2)}, u32[]{:S(2)}) %collective-permute-start.24) | collective-permute-done | bytes 524320 | tf_op jit(solution)/shard_map/ppermute | solution.py:44
  63.2 12.4 %collective-permute-done.25.refs_2_ = bf16[8,4,16,512]{3,2,1,0:T(8,128)(2,1)S(1)} collective-permute-done((bf16[8,4,16,512]{3,2,1,0:T(8,128)(2,1)S(1)}, bf16[8,4,16,512]{3,2,1,0:T(8,128)(2,1)S(1)}, u32[]{:S(2)}, u32[]{:S(2)}) %collective-permute-start.25) | collective-permute-done | bytes 524320 | tf_op jit(solution)/shard_map/ppermute | solution.py:44
  77.9 2.0 collective-permute-start.3
  79.9 1.8 collective-permute-start.4
  81.7 2.5 collective-permute-start.28
  85.0 2.6 collective-permute-done.28.two
  88.5 3.2 %collective-permute-done.29.three = bf16[8,16,512]{2,1,0:T(8,128)(2,1)S(1)} collective-permute-done((bf16[8,16,512]{2,1,0:T(8,128)(2,1)S(1)}, bf16[8,16,512]{2,1,0:T(8,128)(2,1)S(1)}, u32[]{:S(2)}, u32[]{:S(2)}) %collective-permute-start.29) | collective-permute-done | bytes 131104 | tf_op jit(solution)/shard_map/ppermute | solution.py:44
  92.8 9.6 %collective-permute-done.50 = bf16[8,16,512]{2,1,0:T(8,128)(2,1)S(1)} collective-permute-done((bf16[8,16,512]{2,1,0:T(8,128)(2,1)S(1)}, bf16[8,16,512]{2,1,0:T(8,128)(2,1)S(1)}, u32[]{:S(2)}, u32[]{:S(2)}) %collective-permute-start.50) | collective-permute-done | bytes 131104 | tf_op jit(solution)/shard_map/ppermute | solution.py:44
  103.8 1.7 collective-permute-start.13
  105.5 2.1 collective-permute-start.14
  109.6 1.6 collective-permute-start.7
  111.2 7.0 %collective-permute-done.13.refs_2_ = bf16[2,4,4,16,512]{4,3,2,1,0:T(8,128)(2,1)S(1)} collective-permute-done((bf16[2,4,4,16,512]{4,3,2,1,0:T(8,128)(2,1)S(1)}, bf16[2,4,4,16,512]{4,3,2,1,0:T(8,128)(2,1)S(1)}, u32[]{:S(2)}, u32[]{:S(2)}) %collective-permute-start.13) | collective-permute-done | bytes 524320 | tf_op jit(solution)/shard_map/ppermute | solution.py:44
  118.2 13.1 %collective-permute-done.14.refs_3_ = bf16[2,4,4,16,512]{4,3,2,1,0:T(8,128)(2,1)S(1)} collective-permute-done((bf16[2,4,4,16,512]{4,3,2,1,0:T(8,128)(2,1)S(1)}, bf16[2,4,4,16,512]{4,3,2,1,0:T(8,128)(2,1)S(1)}, u32[]{:S(2)}, u32[]{:S(2)}) %collective-permute-start.14) | collective-permute-done | bytes 524320 | tf_op jit(solution)/shard_map/ppermute | solution.py:44
  132.0 1.8 collective-permute-start.15
  134.2 1.7 collective-permute-start.16
  135.8 4.9 %collective-permute-done.6.refs_2_ = bf16[8,4,16,512]{3,2,1,0:T(8,128)(2,1)S(1)} collective-permute-done((bf16[8,4,16,512]{3,2,1,0:T(8,128)(2,1)S(1)}, bf16[8,4,16,512]{3,2,1,0:T(8,128)(2,1)S(1)}, u32[]{:S(2)}, u32[]{:S(2)}) %collective-permute-start.6) | collective-permute-done | bytes 524320 | tf_op jit(solution)/shard_map/ppermute | solution.py:44
  140.7 13.1 %collective-permute-done.7.refs_3_ = bf16[8,4,16,512]{3,2,1,0:T(8,128)(2,1)S(1)} collective-permute-done((bf16[8,4,16,512]{3,2,1,0:T(8,128)(2,1)S(1)}, bf16[8,4,16,512]{3,2,1,0:T(8,128)(2,1)S(1)}, u32[]{:S(2)}, u32[]{:S(2)}) %collective-permute-start.7) | collective-permute-done | bytes 524320 | tf_op jit(solution)/shard_map/ppermute | solution.py:44
  154.9 2.4 collective-permute-start.10
  157.4 2.0 collective-permute-done.10.three
  160.5 4.2 %collective-permute-done.8.one = bf16[8,16,512]{2,1,0:T(8,128)(2,1)S(1)} collective-permute-done((bf16[8,16,512]{2,1,0:T(8,128)(2,1)S(1)}, bf16[8,16,512]{2,1,0:T(8,128)(2,1)S(1)}, u32[]{:S(2)}, u32[]{:S(2)}) %collective-permute-start.8) | collective-permute-done | bytes 131104 | tf_op jit(solution)/shard_map/ppermute | solution.py:44
  165.4 5.0 %collective-permute-done.9.two = bf16[8,16,512]{2,1,0:T(8,128)(2,1)S(1)} collective-permute-done((bf16[8,16,512]{2,1,0:T(8,128)(2,1)S(1)}, bf16[8,16,512]{2,1,0:T(8,128)(2,1)S(1)}, u32[]{:S(2)}, u32[]{:S(2)}) %collective-permute-start.9) | collective-permute-done | bytes 131104 | tf_op jit(solution)/shard_map/ppermute | solution.py:44
  170.4 2.3 collective-permute-start.54
  173.0 3.2 %collective-permute-start.40 = (bf16[8,16,512]{2,1,0:T(8,128)(2,1)S(1)}, bf16[8,16,512]{2,1,0:T(8,128)(2,1)S(1)}, u32[]{:S(2)}, u32[]{:S(2)}) collective-permute-start(bf16[8,16,512]{2,1,0:T(8,128)(2,1)S(1)} %get-tuple-element.171), channel_id=1, source_target_pairs={{0,2},{2,4},{4,6},{6,0},{8,10},{10,12},{12,14},{14,8},{16,18},{18,... | collective-permute-start | bytes 393224 | tf_op jit(solution)/shard_map/ppermute | solution.py:44
  176.2 3.4 %collective-permute-start.41 = (bf16[8,16,512]{2,1,0:T(8,128)(2,1)S(1)}, bf16[8,16,512]{2,1,0:T(8,128)(2,1)S(1)}, u32[]{:S(2)}, u32[]{:S(2)}) collective-permute-start(bf16[8,16,512]{2,1,0:T(8,128)(2,1)S(1)} %get-tuple-element.171), channel_id=1, source_target_pairs={{0,4},{2,6},{4,0},{6,2},{8,12},{10,14},{12,8},{14,10},{16,20},{18,... | collective-permute-start | bytes 393224 | tf_op jit(solution)/shard_map/ppermute | solution.py:44
  180.7 1.5 collective-permute-start.18
  184.8 6.8 %collective-permute-done.18.one = bf16[8,16,512]{2,1,0:T(8,128)(2,1)S(1)} collective-permute-done((bf16[8,16,512]{2,1,0:T(8,128)(2,1)S(1)}, bf16[8,16,512]{2,1,0:T(8,128)(2,1)S(1)}, u32[]{:S(2)}, u32[]{:S(2)}) %collective-permute-start.18) | collective-permute-done | bytes 131104 | tf_op jit(solution)/shard_map/ppermute | solution.py:44
  192.5 2.3 collective-permute-start.44
  194.9 4.3 %collective-permute-done.20.three = bf16[8,16,512]{2,1,0:T(8,128)(2,1)S(1)} collective-permute-done((bf16[8,16,512]{2,1,0:T(8,128)(2,1)S(1)}, bf16[8,16,512]{2,1,0:T(8,128)(2,1)S(1)}, u32[]{:S(2)}, u32[]{:S(2)}) %collective-permute-start.20) | collective-permute-done | bytes 131104 | tf_op jit(solution)/shard_map/ppermute | solution.py:44
  199.2 2.2 collective-permute-start.45
  201.6 2.6 collective-permute-start.30
  204.1 1.6 collective-permute-start.31
  205.8 1.5 collective-permute-done.30
  209.5 1.8 collective-permute-done.32
  211.4 4.1 %collective-permute-start.33 = (bf16[4,8,16,512]{3,2,1,0:T(8,128)(2,1)S(1)}, bf16[4,8,16,512]{3,2,1,0:T(8,128)(2,1)S(1)}, u32[]{:S(2)}, u32[]{:S(2)}) collective-permute-start(bf16[4,8,16,512]{3,2,1,0:T(8,128)(2,1)S(1)} %pad_maximum_fusion.3.refs_0_), channel_id=1, source_target_pairs={{0,2},{2,4},{4,6},{6,0},{8,10},{10,12},{12,14},{14,8},{16,18},{18,... | collective-permute-start | bytes 1572872 | tf_op jit(solution)/shard_map/ppermute | solution.py:44
  215.6 4.2 %collective-permute-start.34 = (bf16[4,8,16,512]{3,2,1,0:T(8,128)(2,1)S(1)}, bf16[4,8,16,512]{3,2,1,0:T(8,128)(2,1)S(1)}, u32[]{:S(2)}, u32[]{:S(2)}) collective-permute-start(bf16[4,8,16,512]{3,2,1,0:T(8,128)(2,1)S(1)} %pad_maximum_fusion.3.refs_0_), channel_id=1, source_target_pairs={{0,4},{2,6},{4,0},{6,2},{8,12},{10,14},{12,8},{14,10},{16,20},{18,... | collective-permute-start | bytes 1572872 | tf_op jit(solution)/shard_map/ppermute | solution.py:44
  219.8 4.4 %collective-permute-start.56 = (bf16[4,4,4,16,512]{4,3,2,1,0:T(8,128)(2,1)S(1)}, bf16[4,4,4,16,512]{4,3,2,1,0:T(8,128)(2,1)S(1)}, u32[]{:S(2)}, u32[]{:S(2)}) collective-permute-start(bf16[4,4,4,16,512]{4,3,2,1,0:T(8,128)(2,1)S(1)} %get-tuple-element.186), channel_id=1, source_target_pairs={{0,1},{1,0},{2,3},{3,2},{4,5},{5,4},{6,7},{7,6},{8,9},{9,8},{10,11... | collective-permute-start | bytes 3145736 | tf_op jit(solution)/shard_map/ppermute | solution.py:236
  225.1 2.2 collective-permute-done.33.refs_1_
  227.3 12.1 %collective-permute-done.34.refs_2_ = bf16[4,8,16,512]{3,2,1,0:T(8,128)(2,1)S(1)} collective-permute-done((bf16[4,8,16,512]{3,2,1,0:T(8,128)(2,1)S(1)}, bf16[4,8,16,512]{3,2,1,0:T(8,128)(2,1)S(1)}, u32[]{:S(2)}, u32[]{:S(2)}) %collective-permute-start.34) | collective-permute-done | bytes 524320 | tf_op jit(solution)/shard_map/ppermute | solution.py:44
  239.4 2.4 collective-permute-done.35.refs_3_
  242.6 2.1 collective-permute-start.36
  245.0 3.0 %collective-permute-start.58 = (bf16[2,4,4,16,512]{4,3,2,1,0:T(8,128)(2,1)S(1)}, bf16[2,4,4,16,512]{4,3,2,1,0:T(8,128)(2,1)S(1)}, u32[]{:S(2)}, u32[]{:S(2)}) collective-permute-start(bf16[2,4,4,16,512]{4,3,2,1,0:T(8,128)(2,1)S(1)} %get-tuple-element.189), channel_id=1, source_target_pairs={{0,4},{2,6},{4,0},{6,2},{8,12},{10,14},{12,8},{14,10},{16,20},{18,... | collective-permute-start | bytes 1572872 | tf_op jit(solution)/shard_map/ppermute | solution.py:44
  248.1 1.9 collective-permute-start.47
  251.0 1.8 collective-permute-start.48
  253.0 6.6 %collective-permute-done.57.refs_1_ = bf16[2,4,4,16,512]{4,3,2,1,0:T(8,128)(2,1)S(1)} collective-permute-done((bf16[2,4,4,16,512]{4,3,2,1,0:T(8,128)(2,1)S(1)}, bf16[2,4,4,16,512]{4,3,2,1,0:T(8,128)(2,1)S(1)}, u32[]{:S(2)}, u32[]{:S(2)}) %collective-permute-start.57) | collective-permute-done | bytes 524320 | tf_op jit(solution)/shard_map/ppermute | solution.py:44
  259.6 2.4 collective-permute-start.49
  262.0 9.2 %collective-permute-done.58.refs_2_ = bf16[2,4,4,16,512]{4,3,2,1,0:T(8,128)(2,1)S(1)} collective-permute-done((bf16[2,4,4,16,512]{4,3,2,1,0:T(8,128)(2,1)S(1)}, bf16[2,4,4,16,512]{4,3,2,1,0:T(8,128)(2,1)S(1)}, u32[]{:S(2)}, u32[]{:S(2)}) %collective-permute-start.58) | collective-permute-done | bytes 524320 | tf_op jit(solution)/shard_map/ppermute | solution.py:44
  272.5 1.5 collective-permute-start.39
  274.0 2.2 multiply_convert_fusion
  279.2 2.0 shard_map.159.refs_4_
  281.2 2.0 shard_map.160.refs_4_
  283.2 3.1 %collective-permute-done.37.refs_1_ = bf16[2,4,4,16,512]{4,3,2,1,0:T(8,128)(2,1)S(1)} collective-permute-done((bf16[2,4,4,16,512]{4,3,2,1,0:T(8,128)(2,1)S(1)}, bf16[2,4,4,16,512]{4,3,2,1,0:T(8,128)(2,1)S(1)}, u32[]{:S(2)}, u32[]{:S(2)}) %collective-permute-start.37) | collective-permute-done | bytes 524320 | tf_op jit(solution)/shard_map/ppermute | solution.py:44
  286.4 8.5 %collective-permute-done.38.refs_2_ = bf16[2,4,4,16,512]{4,3,2,1,0:T(8,128)(2,1)S(1)} collective-permute-done((bf16[2,4,4,16,512]{4,3,2,1,0:T(8,128)(2,1)S(1)}, bf16[2,4,4,16,512]{4,3,2,1,0:T(8,128)(2,1)S(1)}, u32[]{:S(2)}, u32[]{:S(2)}) %collective-permute-start.38) | collective-permute-done | bytes 524320 | tf_op jit(solution)/shard_map/ppermute | solution.py:44
  294.9 1.8 collective-permute-done.39.refs_3_
  296.7 2.0 shard_map.161
  (114 shorter events, 37.3 us)
Async XLA Ops:
  14.5 4.9 %collective-permute-start = (bf16[64,16,512]{2,1,0:T(8,128)(2,1)S(1)}, bf16[64,16,512]{2,1,0:T(8,128)(2,1)S(1)}, u32[]{:S(2)}, u32[]{:S(2)}) collective-permute-start(bf16[64,16,512]{2,1,0:T(8,128)(2,1)S(1)} %get-tuple-element.99), channel_id=1, source_target_pairs={{0,1},{1,0},{2,3},{3,2},{4,5},{5,4},{6,7},{7,6},{8,9},{9,8},{10,11... | collective-permute-start | bytes 3145736 | tf_op jit(solution)/shard_map/ppermute | solution.py:178
  20.1 16.2 %collective-permute-start.21 = (bf16[2,4,4,16,512]{4,3,2,1,0:T(8,128)(2,1)S(1)}, bf16[2,4,4,16,512]{4,3,2,1,0:T(8,128)(2,1)S(1)}, u32[]{:S(2)}, u32[]{:S(2)}) collective-permute-start(bf16[2,4,4,16,512]{4,3,2,1,0:T(8,128)(2,1)S(1)} %get-tuple-element.143), channel_id=1, source_target_pairs={{0,2},{2,4},{4,6},{6,0},{8,10},{10,12},{12,14},{14,8},{16,18},{18,... | collective-permute-start | bytes 1572872 | tf_op jit(solution)/shard_map/ppermute | solution.py:44
  21.9 26.5 %collective-permute-start.22 = (bf16[2,4,4,16,512]{4,3,2,1,0:T(8,128)(2,1)S(1)}, bf16[2,4,4,16,512]{4,3,2,1,0:T(8,128)(2,1)S(1)}, u32[]{:S(2)}, u32[]{:S(2)}) collective-permute-start(bf16[2,4,4,16,512]{4,3,2,1,0:T(8,128)(2,1)S(1)} %get-tuple-element.144), channel_id=1, source_target_pairs={{0,4},{2,6},{4,0},{6,2},{8,12},{10,14},{12,8},{14,10},{16,20},{18,... | collective-permute-start | bytes 1572872 | tf_op jit(solution)/shard_map/ppermute | solution.py:44
  27.9 47.7 %copy-start.3 = (s32[128,1]{0,1:T(1,128)S(1)}, s32[128,1]{0,1:T(1,128)}, u32[]{:S(2)}) copy-start(s32[128,1]{0,1:T(1,128)} %param.15) | copy-start | bytes 1540
  27.9 26.3 %collective-permute-start.1 = (bf16[64,16,512]{2,1,0:T(8,128)(2,1)S(1)}, bf16[64,16,512]{2,1,0:T(8,128)(2,1)S(1)}, u32[]{:S(2)}, u32[]{:S(2)}) collective-permute-start(bf16[64,16,512]{2,1,0:T(8,128)(2,1)S(1)} %get-tuple-element.113), channel_id=1, source_target_pairs={{0,1},{1,0},{2,3},{3,2},{4,5},{5,4},{6,7},{7,6},{8,9},{9,8},{10,11... | collective-permute-start | bytes 3145736 | tf_op jit(solution)/shard_map/ppermute | solution.py:178
  28.5 19.9 %collective-permute-start.23 = (bf16[2,4,4,16,512]{4,3,2,1,0:T(8,128)(2,1)S(1)}, bf16[2,4,4,16,512]{4,3,2,1,0:T(8,128)(2,1)S(1)}, u32[]{:S(2)}, u32[]{:S(2)}) collective-permute-start(bf16[2,4,4,16,512]{4,3,2,1,0:T(8,128)(2,1)S(1)} %get-tuple-element.145), channel_id=1, source_target_pairs={{0,6},{2,0},{4,2},{6,4},{8,14},{10,8},{12,10},{14,12},{16,22},{18,... | collective-permute-start | bytes 1572872 | tf_op jit(solution)/shard_map/ppermute | solution.py:44
  31.9 49.8 %collective-permute-start.11 = (bf16[64,16,512]{2,1,0:T(8,128)(2,1)S(1)}, bf16[64,16,512]{2,1,0:T(8,128)(2,1)S(1)}, u32[]{:S(2)}, u32[]{:S(2)}) collective-permute-start(bf16[64,16,512]{2,1,0:T(8,128)(2,1)S(1)} %get-tuple-element.128), channel_id=1, source_target_pairs={{0,1},{1,0},{2,3},{3,2},{4,5},{5,4},{6,7},{7,6},{8,9},{9,8},{10,11... | collective-permute-start | bytes 3145736 | tf_op jit(solution)/shard_map/ppermute | solution.py:178
  49.1 14.1 %collective-permute-start.24 = (bf16[8,4,16,512]{3,2,1,0:T(8,128)(2,1)S(1)}, bf16[8,4,16,512]{3,2,1,0:T(8,128)(2,1)S(1)}, u32[]{:S(2)}, u32[]{:S(2)}) collective-permute-start(bf16[8,4,16,512]{3,2,1,0:T(8,128)(2,1)S(1)} %get-tuple-element.147), channel_id=1, source_target_pairs={{0,32},{2,34},{4,36},{6,38},{8,40},{10,42},{12,44},{14,46},{16,48}... | collective-permute-start | bytes 1572872 | tf_op jit(solution)/shard_map/ppermute | solution.py:44
  50.5 25.0 %collective-permute-start.25 = (bf16[8,4,16,512]{3,2,1,0:T(8,128)(2,1)S(1)}, bf16[8,4,16,512]{3,2,1,0:T(8,128)(2,1)S(1)}, u32[]{:S(2)}, u32[]{:S(2)}) collective-permute-start(bf16[8,4,16,512]{3,2,1,0:T(8,128)(2,1)S(1)} %get-tuple-element.148), channel_id=1, source_target_pairs={{0,64},{2,66},{4,68},{6,70},{8,72},{10,74},{12,76},{14,78},{16,80}... | collective-permute-start | bytes 1572872 | tf_op jit(solution)/shard_map/ppermute | solution.py:44
  53.1 22.4 %collective-permute-start.26 = (bf16[8,4,16,512]{3,2,1,0:T(8,128)(2,1)S(1)}, bf16[8,4,16,512]{3,2,1,0:T(8,128)(2,1)S(1)}, u32[]{:S(2)}, u32[]{:S(2)}) collective-permute-start(bf16[8,4,16,512]{3,2,1,0:T(8,128)(2,1)S(1)} %get-tuple-element.149), channel_id=1, source_target_pairs={{0,96},{2,98},{4,100},{6,102},{8,104},{10,106},{12,108},{14,110},{... | collective-permute-start | bytes 1572872 | tf_op jit(solution)/shard_map/ppermute | solution.py:44
  54.2 37.6 %copy-start.1 = (f32[8,3,16,512]{3,2,1,0:T(8,128)S(1)}, f32[8,3,16,512]{3,2,1,0:T(8,128)}, u32[]{:S(2)}) copy-start(f32[8,3,16,512]{3,2,1,0:T(8,128)} %moment_m.5) | copy-start | bytes 2359300
  54.2 37.6 %copy-start.2 = (f32[8,3,16,512]{3,2,1,0:T(8,128)S(1)}, f32[8,3,16,512]{3,2,1,0:T(8,128)}, u32[]{:S(2)}) copy-start(f32[8,3,16,512]{3,2,1,0:T(8,128)} %moment_v.5) | copy-start | bytes 2359300
  54.9 48.8 %collective-permute-start.2 = (bf16[2,4,4,16,512]{4,3,2,1,0:T(8,128)(2,1)S(1)}, bf16[2,4,4,16,512]{4,3,2,1,0:T(8,128)(2,1)S(1)}, u32[]{:S(2)}, u32[]{:S(2)}) collective-permute-start(bf16[2,4,4,16,512]{4,3,2,1,0:T(8,128)(2,1)S(1)} %get-tuple-element.115), channel_id=1, source_target_pairs={{0,32},{2,34},{4,36},{6,38},{8,40},{10,42},{12,44},{14,46},{16,48}... | collective-permute-start | bytes 1572872 | tf_op jit(solution)/shard_map/ppermute | solution.py:44
  76.6 8.3 %collective-permute-start.27 = (bf16[8,16,512]{2,1,0:T(8,128)(2,1)S(1)}, bf16[8,16,512]{2,1,0:T(8,128)(2,1)S(1)}, u32[]{:S(2)}, u32[]{:S(2)}) collective-permute-start(bf16[8,16,512]{2,1,0:T(8,128)(2,1)S(1)} %get-tuple-element.151), channel_id=1, source_target_pairs={{0,8},{2,10},{4,12},{6,14},{8,16},{10,18},{12,20},{14,22},{16,24},... | collective-permute-start | bytes 393224 | tf_op jit(solution)/shard_map/ppermute | solution.py:44
  77.9 25.9 %collective-permute-start.3 = (bf16[2,4,4,16,512]{4,3,2,1,0:T(8,128)(2,1)S(1)}, bf16[2,4,4,16,512]{4,3,2,1,0:T(8,128)(2,1)S(1)}, u32[]{:S(2)}, u32[]{:S(2)}) collective-permute-start(bf16[2,4,4,16,512]{4,3,2,1,0:T(8,128)(2,1)S(1)} %get-tuple-element.116), channel_id=1, source_target_pairs={{0,64},{2,66},{4,68},{6,70},{8,72},{10,74},{12,76},{14,78},{16,80}... | collective-permute-start | bytes 1572872 | tf_op jit(solution)/shard_map/ppermute | solution.py:44
  79.9 25.6 %collective-permute-start.4 = (bf16[2,4,4,16,512]{4,3,2,1,0:T(8,128)(2,1)S(1)}, bf16[2,4,4,16,512]{4,3,2,1,0:T(8,128)(2,1)S(1)}, u32[]{:S(2)}, u32[]{:S(2)}) collective-permute-start(bf16[2,4,4,16,512]{4,3,2,1,0:T(8,128)(2,1)S(1)} %get-tuple-element.117), channel_id=1, source_target_pairs={{0,96},{2,98},{4,100},{6,102},{8,104},{10,106},{12,108},{14,110},{... | collective-permute-start | bytes 1572872 | tf_op jit(solution)/shard_map/ppermute | solution.py:44
  81.7 5.9 %collective-permute-start.28 = (bf16[8,16,512]{2,1,0:T(8,128)(2,1)S(1)}, bf16[8,16,512]{2,1,0:T(8,128)(2,1)S(1)}, u32[]{:S(2)}, u32[]{:S(2)}) collective-permute-start(bf16[8,16,512]{2,1,0:T(8,128)(2,1)S(1)} %get-tuple-element.152), channel_id=1, source_target_pairs={{0,16},{2,18},{4,20},{6,22},{8,24},{10,26},{12,28},{14,30},{16,0},... | collective-permute-start | bytes 393224 | tf_op jit(solution)/shard_map/ppermute | solution.py:44
  84.9 24.6 %collective-permute-start.12 = (bf16[2,4,4,16,512]{4,3,2,1,0:T(8,128)(2,1)S(1)}, bf16[2,4,4,16,512]{4,3,2,1,0:T(8,128)(2,1)S(1)}, u32[]{:S(2)}, u32[]{:S(2)}) collective-permute-start(bf16[2,4,4,16,512]{4,3,2,1,0:T(8,128)(2,1)S(1)} %get-tuple-element.130), channel_id=1, source_target_pairs={{0,8},{2,10},{4,12},{6,14},{8,16},{10,18},{12,20},{14,22},{16,24},... | collective-permute-start | bytes 1572872 | tf_op jit(solution)/shard_map/ppermute | solution.py:44
  87.6 4.1 %collective-permute-start.29 = (bf16[8,16,512]{2,1,0:T(8,128)(2,1)S(1)}, bf16[8,16,512]{2,1,0:T(8,128)(2,1)S(1)}, u32[]{:S(2)}, u32[]{:S(2)}) collective-permute-start(bf16[8,16,512]{2,1,0:T(8,128)(2,1)S(1)} %get-tuple-element.153), channel_id=1, source_target_pairs={{0,24},{2,26},{4,28},{6,30},{8,0},{10,2},{12,4},{14,6},{16,8},{18,... | collective-permute-start | bytes 393224 | tf_op jit(solution)/shard_map/ppermute | solution.py:44
  92.0 10.4 %collective-permute-start.50 = (bf16[8,16,512]{2,1,0:T(8,128)(2,1)S(1)}, bf16[8,16,512]{2,1,0:T(8,128)(2,1)S(1)}, u32[]{:S(2)}, u32[]{:S(2)}) collective-permute-start(bf16[8,16,512]{2,1,0:T(8,128)(2,1)S(1)} %get-tuple-element.181), channel_id=1, source_target_pairs={{0,8},{2,10},{4,12},{6,14},{8,16},{10,18},{12,20},{14,22},{16,24},... | collective-permute-start | bytes 393224 | tf_op jit(solution)/shard_map/ppermute | solution.py:44
  102.4 5.9 %collective-permute-start.51 = (bf16[8,16,512]{2,1,0:T(8,128)(2,1)S(1)}, bf16[8,16,512]{2,1,0:T(8,128)(2,1)S(1)}, u32[]{:S(2)}, u32[]{:S(2)}) collective-permute-start(bf16[8,16,512]{2,1,0:T(8,128)(2,1)S(1)} %get-tuple-element.181), channel_id=1, source_target_pairs={{0,16},{2,18},{4,20},{6,22},{8,24},{10,26},{12,28},{14,30},{16,0},... | collective-permute-start | bytes 393224 | tf_op jit(solution)/shard_map/ppermute | solution.py:44
  103.7 4.8 %collective-permute-start.52 = (bf16[8,16,512]{2,1,0:T(8,128)(2,1)S(1)}, bf16[8,16,512]{2,1,0:T(8,128)(2,1)S(1)}, u32[]{:S(2)}, u32[]{:S(2)}) collective-permute-start(bf16[8,16,512]{2,1,0:T(8,128)(2,1)S(1)} %get-tuple-element.181), channel_id=1, source_target_pairs={{0,24},{2,26},{4,28},{6,30},{8,0},{10,2},{12,4},{14,6},{16,8},{18,... | collective-permute-start | bytes 393224 | tf_op jit(solution)/shard_map/ppermute | solution.py:44
  103.8 14.5 %collective-permute-start.13 = (bf16[2,4,4,16,512]{4,3,2,1,0:T(8,128)(2,1)S(1)}, bf16[2,4,4,16,512]{4,3,2,1,0:T(8,128)(2,1)S(1)}, u32[]{:S(2)}, u32[]{:S(2)}) collective-permute-start(bf16[2,4,4,16,512]{4,3,2,1,0:T(8,128)(2,1)S(1)} %get-tuple-element.131), channel_id=1, source_target_pairs={{0,16},{2,18},{4,20},{6,22},{8,24},{10,26},{12,28},{14,30},{16,0},... | collective-permute-start | bytes 1572872 | tf_op jit(solution)/shard_map/ppermute | solution.py:44
  105.5 25.9 %collective-permute-start.14 = (bf16[2,4,4,16,512]{4,3,2,1,0:T(8,128)(2,1)S(1)}, bf16[2,4,4,16,512]{4,3,2,1,0:T(8,128)(2,1)S(1)}, u32[]{:S(2)}, u32[]{:S(2)}) collective-permute-start(bf16[2,4,4,16,512]{4,3,2,1,0:T(8,128)(2,1)S(1)} %get-tuple-element.132), channel_id=1, source_target_pairs={{0,24},{2,26},{4,28},{6,30},{8,0},{10,2},{12,4},{14,6},{16,8},{18,... | collective-permute-start | bytes 1572872 | tf_op jit(solution)/shard_map/ppermute | solution.py:44
  108.3 25.9 %collective-permute-start.5 = (bf16[8,4,16,512]{3,2,1,0:T(8,128)(2,1)S(1)}, bf16[8,4,16,512]{3,2,1,0:T(8,128)(2,1)S(1)}, u32[]{:S(2)}, u32[]{:S(2)}) collective-permute-start(bf16[8,4,16,512]{3,2,1,0:T(8,128)(2,1)S(1)} %get-tuple-element.119), channel_id=1, source_target_pairs={{0,8},{2,10},{4,12},{6,14},{8,16},{10,18},{12,20},{14,22},{16,24},... | collective-permute-start | bytes 1572872 | tf_op jit(solution)/shard_map/ppermute | solution.py:44
  108.6 32.1 %collective-permute-start.6 = (bf16[8,4,16,512]{3,2,1,0:T(8,128)(2,1)S(1)}, bf16[8,4,16,512]{3,2,1,0:T(8,128)(2,1)S(1)}, u32[]{:S(2)}, u32[]{:S(2)}) collective-permute-start(bf16[8,4,16,512]{3,2,1,0:T(8,128)(2,1)S(1)} %get-tuple-element.120), channel_id=1, source_target_pairs={{0,16},{2,18},{4,20},{6,22},{8,24},{10,26},{12,28},{14,30},{16,0},... | collective-permute-start | bytes 1572872 | tf_op jit(solution)/shard_map/ppermute | solution.py:44
  109.6 44.3 %collective-permute-start.7 = (bf16[8,4,16,512]{3,2,1,0:T(8,128)(2,1)S(1)}, bf16[8,4,16,512]{3,2,1,0:T(8,128)(2,1)S(1)}, u32[]{:S(2)}, u32[]{:S(2)}) collective-permute-start(bf16[8,4,16,512]{3,2,1,0:T(8,128)(2,1)S(1)} %get-tuple-element.121), channel_id=1, source_target_pairs={{0,24},{2,26},{4,28},{6,30},{8,0},{10,2},{12,4},{14,6},{16,8},{18,... | collective-permute-start | bytes 1572872 | tf_op jit(solution)/shard_map/ppermute | solution.py:44
  118.2 54.8 %collective-permute-start.53 = (bf16[4,8,16,512]{3,2,1,0:T(8,128)(2,1)S(1)}, bf16[4,8,16,512]{3,2,1,0:T(8,128)(2,1)S(1)}, u32[]{:S(2)}, u32[]{:S(2)}) collective-permute-start(bf16[4,8,16,512]{3,2,1,0:T(8,128)(2,1)S(1)} %pad_maximum_fusion.5.refs_0_), channel_id=1, source_target_pairs={{0,32},{2,34},{4,36},{6,38},{8,40},{10,42},{12,44},{14,46},{16,48}... | collective-permute-start | bytes 1572872 | tf_op jit(solution)/shard_map/ppermute | solution.py:44
  132.0 44.2 %collective-permute-start.15 = (bf16[8,4,16,512]{3,2,1,0:T(8,128)(2,1)S(1)}, bf16[8,4,16,512]{3,2,1,0:T(8,128)(2,1)S(1)}, u32[]{:S(2)}, u32[]{:S(2)}) collective-permute-start(bf16[8,4,16,512]{3,2,1,0:T(8,128)(2,1)S(1)} %get-tuple-element.134), channel_id=1, source_target_pairs={{0,2},{2,4},{4,6},{6,0},{8,10},{10,12},{12,14},{14,8},{16,18},{18,... | collective-permute-start | bytes 1572872 | tf_op jit(solution)/shard_map/ppermute | solution.py:44
  134.2 45.4 %collective-permute-start.16 = (bf16[8,4,16,512]{3,2,1,0:T(8,128)(2,1)S(1)}, bf16[8,4,16,512]{3,2,1,0:T(8,128)(2,1)S(1)}, u32[]{:S(2)}, u32[]{:S(2)}) collective-permute-start(bf16[8,4,16,512]{3,2,1,0:T(8,128)(2,1)S(1)} %get-tuple-element.135), channel_id=1, source_target_pairs={{0,4},{2,6},{4,0},{6,2},{8,12},{10,14},{12,8},{14,10},{16,20},{18,... | collective-permute-start | bytes 1572872 | tf_op jit(solution)/shard_map/ppermute | solution.py:44
  154.9 4.4 %collective-permute-start.10 = (bf16[8,16,512]{2,1,0:T(8,128)(2,1)S(1)}, bf16[8,16,512]{2,1,0:T(8,128)(2,1)S(1)}, u32[]{:S(2)}, u32[]{:S(2)}) collective-permute-start(bf16[8,16,512]{2,1,0:T(8,128)(2,1)S(1)} %get-tuple-element.125), channel_id=1, source_target_pairs={{0,6},{2,0},{4,2},{6,4},{8,14},{10,8},{12,10},{14,12},{16,22},{18,... | collective-permute-start | bytes 393224 | tf_op jit(solution)/shard_map/ppermute | solution.py:44
  157.3 22.2 %collective-permute-start.17 = (bf16[8,4,16,512]{3,2,1,0:T(8,128)(2,1)S(1)}, bf16[8,4,16,512]{3,2,1,0:T(8,128)(2,1)S(1)}, u32[]{:S(2)}, u32[]{:S(2)}) collective-permute-start(bf16[8,4,16,512]{3,2,1,0:T(8,128)(2,1)S(1)} %get-tuple-element.136), channel_id=1, source_target_pairs={{0,6},{2,0},{4,2},{6,4},{8,14},{10,8},{12,10},{14,12},{16,22},{18,... | collective-permute-start | bytes 1572872 | tf_op jit(solution)/shard_map/ppermute | solution.py:44
  159.3 5.3 %collective-permute-start.8 = (bf16[8,16,512]{2,1,0:T(8,128)(2,1)S(1)}, bf16[8,16,512]{2,1,0:T(8,128)(2,1)S(1)}, u32[]{:S(2)}, u32[]{:S(2)}) collective-permute-start(bf16[8,16,512]{2,1,0:T(8,128)(2,1)S(1)} %get-tuple-element.123), channel_id=1, source_target_pairs={{0,2},{2,4},{4,6},{6,0},{8,10},{10,12},{12,14},{14,8},{16,18},{18,... | collective-permute-start | bytes 393224 | tf_op jit(solution)/shard_map/ppermute | solution.py:44
  164.7 5.7 %collective-permute-start.9 = (bf16[8,16,512]{2,1,0:T(8,128)(2,1)S(1)}, bf16[8,16,512]{2,1,0:T(8,128)(2,1)S(1)}, u32[]{:S(2)}, u32[]{:S(2)}) collective-permute-start(bf16[8,16,512]{2,1,0:T(8,128)(2,1)S(1)} %get-tuple-element.124), channel_id=1, source_target_pairs={{0,4},{2,6},{4,0},{6,2},{8,12},{10,14},{12,8},{14,10},{16,20},{18,... | collective-permute-start | bytes 393224 | tf_op jit(solution)/shard_map/ppermute | solution.py:44
  170.4 31.2 %collective-permute-start.54 = (bf16[4,8,16,512]{3,2,1,0:T(8,128)(2,1)S(1)}, bf16[4,8,16,512]{3,2,1,0:T(8,128)(2,1)S(1)}, u32[]{:S(2)}, u32[]{:S(2)}) collective-permute-start(bf16[4,8,16,512]{3,2,1,0:T(8,128)(2,1)S(1)} %pad_maximum_fusion.5.refs_0_), channel_id=1, source_target_pairs={{0,64},{2,66},{4,68},{6,70},{8,72},{10,74},{12,76},{14,78},{16,80}... | collective-permute-start | bytes 1572872 | tf_op jit(solution)/shard_map/ppermute | solution.py:44
  173.0 7.7 %collective-permute-start.40 = (bf16[8,16,512]{2,1,0:T(8,128)(2,1)S(1)}, bf16[8,16,512]{2,1,0:T(8,128)(2,1)S(1)}, u32[]{:S(2)}, u32[]{:S(2)}) collective-permute-start(bf16[8,16,512]{2,1,0:T(8,128)(2,1)S(1)} %get-tuple-element.171), channel_id=1, source_target_pairs={{0,2},{2,4},{4,6},{6,0},{8,10},{10,12},{12,14},{14,8},{16,18},{18,... | collective-permute-start | bytes 393224 | tf_op jit(solution)/shard_map/ppermute | solution.py:44
  176.2 7.4 %collective-permute-start.41 = (bf16[8,16,512]{2,1,0:T(8,128)(2,1)S(1)}, bf16[8,16,512]{2,1,0:T(8,128)(2,1)S(1)}, u32[]{:S(2)}, u32[]{:S(2)}) collective-permute-start(bf16[8,16,512]{2,1,0:T(8,128)(2,1)S(1)} %get-tuple-element.171), channel_id=1, source_target_pairs={{0,4},{2,6},{4,0},{6,2},{8,12},{10,14},{12,8},{14,10},{16,20},{18,... | collective-permute-start | bytes 393224 | tf_op jit(solution)/shard_map/ppermute | solution.py:44
  179.5 4.5 %collective-permute-start.42 = (bf16[8,16,512]{2,1,0:T(8,128)(2,1)S(1)}, bf16[8,16,512]{2,1,0:T(8,128)(2,1)S(1)}, u32[]{:S(2)}, u32[]{:S(2)}) collective-permute-start(bf16[8,16,512]{2,1,0:T(8,128)(2,1)S(1)} %get-tuple-element.171), channel_id=1, source_target_pairs={{0,6},{2,0},{4,2},{6,4},{8,14},{10,8},{12,10},{14,12},{16,22},{18,... | collective-permute-start | bytes 393224 | tf_op jit(solution)/shard_map/ppermute | solution.py:44
  179.5 24.6 %collective-permute-start.55 = (bf16[4,8,16,512]{3,2,1,0:T(8,128)(2,1)S(1)}, bf16[4,8,16,512]{3,2,1,0:T(8,128)(2,1)S(1)}, u32[]{:S(2)}, u32[]{:S(2)}) collective-permute-start(bf16[4,8,16,512]{3,2,1,0:T(8,128)(2,1)S(1)} %pad_maximum_fusion.5.refs_0_), channel_id=1, source_target_pairs={{0,96},{2,98},{4,100},{6,102},{8,104},{10,106},{12,108},{14,110},{... | collective-permute-start | bytes 1572872 | tf_op jit(solution)/shard_map/ppermute | solution.py:44
  180.7 10.9 %collective-permute-start.18 = (bf16[8,16,512]{2,1,0:T(8,128)(2,1)S(1)}, bf16[8,16,512]{2,1,0:T(8,128)(2,1)S(1)}, u32[]{:S(2)}, u32[]{:S(2)}) collective-permute-start(bf16[8,16,512]{2,1,0:T(8,128)(2,1)S(1)} %get-tuple-element.138), channel_id=1, source_target_pairs={{0,32},{2,34},{4,36},{6,38},{8,40},{10,42},{12,44},{14,46},{16,48}... | collective-permute-start | bytes 393224 | tf_op jit(solution)/shard_map/ppermute | solution.py:44
  183.6 9.0 %collective-permute-start.19 = (bf16[8,16,512]{2,1,0:T(8,128)(2,1)S(1)}, bf16[8,16,512]{2,1,0:T(8,128)(2,1)S(1)}, u32[]{:S(2)}, u32[]{:S(2)}) collective-permute-start(bf16[8,16,512]{2,1,0:T(8,128)(2,1)S(1)} %get-tuple-element.139), channel_id=1, source_target_pairs={{0,64},{2,66},{4,68},{6,70},{8,72},{10,74},{12,76},{14,78},{16,80}... | collective-permute-start | bytes 393224 | tf_op jit(solution)/shard_map/ppermute | solution.py:44
  184.0 15.1 %collective-permute-start.20 = (bf16[8,16,512]{2,1,0:T(8,128)(2,1)S(1)}, bf16[8,16,512]{2,1,0:T(8,128)(2,1)S(1)}, u32[]{:S(2)}, u32[]{:S(2)}) collective-permute-start(bf16[8,16,512]{2,1,0:T(8,128)(2,1)S(1)} %get-tuple-element.140), channel_id=1, source_target_pairs={{0,96},{2,98},{4,100},{6,102},{8,104},{10,106},{12,108},{14,110},{... | collective-permute-start | bytes 393224 | tf_op jit(solution)/shard_map/ppermute | solution.py:44
  191.6 28.1 %collective-permute-start.43 = (bf16[4,8,16,512]{3,2,1,0:T(8,128)(2,1)S(1)}, bf16[4,8,16,512]{3,2,1,0:T(8,128)(2,1)S(1)}, u32[]{:S(2)}, u32[]{:S(2)}) collective-permute-start(bf16[4,8,16,512]{3,2,1,0:T(8,128)(2,1)S(1)} %pad_maximum_fusion.4.refs_0_), channel_id=1, source_target_pairs={{0,8},{2,10},{4,12},{6,14},{8,16},{10,18},{12,20},{14,22},{16,24},... | collective-permute-start | bytes 1572872 | tf_op jit(solution)/shard_map/ppermute | solution.py:44
  192.5 27.2 %collective-permute-start.44 = (bf16[4,8,16,512]{3,2,1,0:T(8,128)(2,1)S(1)}, bf16[4,8,16,512]{3,2,1,0:T(8,128)(2,1)S(1)}, u32[]{:S(2)}, u32[]{:S(2)}) collective-permute-start(bf16[4,8,16,512]{3,2,1,0:T(8,128)(2,1)S(1)} %pad_maximum_fusion.4.refs_0_), channel_id=1, source_target_pairs={{0,16},{2,18},{4,20},{6,22},{8,24},{10,26},{12,28},{14,30},{16,0},... | collective-permute-start | bytes 1572872 | tf_op jit(solution)/shard_map/ppermute | solution.py:44
  199.2 25.0 %collective-permute-start.45 = (bf16[4,8,16,512]{3,2,1,0:T(8,128)(2,1)S(1)}, bf16[4,8,16,512]{3,2,1,0:T(8,128)(2,1)S(1)}, u32[]{:S(2)}, u32[]{:S(2)}) collective-permute-start(bf16[4,8,16,512]{3,2,1,0:T(8,128)(2,1)S(1)} %pad_maximum_fusion.4.refs_0_), channel_id=1, source_target_pairs={{0,24},{2,26},{4,28},{6,30},{8,0},{10,2},{12,4},{14,6},{16,8},{18,... | collective-permute-start | bytes 1572872 | tf_op jit(solution)/shard_map/ppermute | solution.py:44
  201.3 48.7 %slice-start = ((s8[6291456]{0:T(1024)(128)(4,1)}), s8[4194304]{0:T(1024)(128)(4,1)S(1)}, s32[]{:S(2)}) async-start(s8[6291456]{0:T(1024)(128)(4,1)} %bitcast.67), calls=%async_computation | async-start | bytes 8388608
  201.6 5.7 %collective-permute-start.30 = (bf16[8,16,512]{2,1,0:T(8,128)(2,1)S(1)}, bf16[8,16,512]{2,1,0:T(8,128)(2,1)S(1)}, u32[]{:S(2)}, u32[]{:S(2)}) collective-permute-start(bf16[8,16,512]{2,1,0:T(8,128)(2,1)S(1)} %get-tuple-element.161), channel_id=1, source_target_pairs={{0,32},{2,34},{4,36},{6,38},{8,40},{10,42},{12,44},{14,46},{16,48}... | collective-permute-start | bytes 393224 | tf_op jit(solution)/shard_map/ppermute | solution.py:44
  204.1 5.4 %collective-permute-start.31 = (bf16[8,16,512]{2,1,0:T(8,128)(2,1)S(1)}, bf16[8,16,512]{2,1,0:T(8,128)(2,1)S(1)}, u32[]{:S(2)}, u32[]{:S(2)}) collective-permute-start(bf16[8,16,512]{2,1,0:T(8,128)(2,1)S(1)} %get-tuple-element.161), channel_id=1, source_target_pairs={{0,64},{2,66},{4,68},{6,70},{8,72},{10,74},{12,76},{14,78},{16,80}... | collective-permute-start | bytes 393224 | tf_op jit(solution)/shard_map/ppermute | solution.py:44
  207.3 4.1 %collective-permute-start.32 = (bf16[8,16,512]{2,1,0:T(8,128)(2,1)S(1)}, bf16[8,16,512]{2,1,0:T(8,128)(2,1)S(1)}, u32[]{:S(2)}, u32[]{:S(2)}) collective-permute-start(bf16[8,16,512]{2,1,0:T(8,128)(2,1)S(1)} %get-tuple-element.161), channel_id=1, source_target_pairs={{0,96},{2,98},{4,100},{6,102},{8,104},{10,106},{12,108},{14,110},{... | collective-permute-start | bytes 393224 | tf_op jit(solution)/shard_map/ppermute | solution.py:44
  211.4 15.9 %collective-permute-start.33 = (bf16[4,8,16,512]{3,2,1,0:T(8,128)(2,1)S(1)}, bf16[4,8,16,512]{3,2,1,0:T(8,128)(2,1)S(1)}, u32[]{:S(2)}, u32[]{:S(2)}) collective-permute-start(bf16[4,8,16,512]{3,2,1,0:T(8,128)(2,1)S(1)} %pad_maximum_fusion.3.refs_0_), channel_id=1, source_target_pairs={{0,2},{2,4},{4,6},{6,0},{8,10},{10,12},{12,14},{14,8},{16,18},{18,... | collective-permute-start | bytes 1572872 | tf_op jit(solution)/shard_map/ppermute | solution.py:44
  215.6 23.9 %collective-permute-start.34 = (bf16[4,8,16,512]{3,2,1,0:T(8,128)(2,1)S(1)}, bf16[4,8,16,512]{3,2,1,0:T(8,128)(2,1)S(1)}, u32[]{:S(2)}, u32[]{:S(2)}) collective-permute-start(bf16[4,8,16,512]{3,2,1,0:T(8,128)(2,1)S(1)} %pad_maximum_fusion.3.refs_0_), channel_id=1, source_target_pairs={{0,4},{2,6},{4,0},{6,2},{8,12},{10,14},{12,8},{14,10},{16,20},{18,... | collective-permute-start | bytes 1572872 | tf_op jit(solution)/shard_map/ppermute | solution.py:44
  219.7 22.1 %collective-permute-start.35 = (bf16[4,8,16,512]{3,2,1,0:T(8,128)(2,1)S(1)}, bf16[4,8,16,512]{3,2,1,0:T(8,128)(2,1)S(1)}, u32[]{:S(2)}, u32[]{:S(2)}) collective-permute-start(bf16[4,8,16,512]{3,2,1,0:T(8,128)(2,1)S(1)} %pad_maximum_fusion.3.refs_0_), channel_id=1, source_target_pairs={{0,6},{2,0},{4,2},{6,4},{8,14},{10,8},{12,10},{14,12},{16,22},{18,... | collective-permute-start | bytes 1572872 | tf_op jit(solution)/shard_map/ppermute | solution.py:44
  219.8 25.0 %collective-permute-start.56 = (bf16[4,4,4,16,512]{4,3,2,1,0:T(8,128)(2,1)S(1)}, bf16[4,4,4,16,512]{4,3,2,1,0:T(8,128)(2,1)S(1)}, u32[]{:S(2)}, u32[]{:S(2)}) collective-permute-start(bf16[4,4,4,16,512]{4,3,2,1,0:T(8,128)(2,1)S(1)} %get-tuple-element.186), channel_id=1, source_target_pairs={{0,1},{1,0},{2,3},{3,2},{4,5},{5,4},{6,7},{7,6},{8,9},{9,8},{10,11... | collective-permute-start | bytes 3145736 | tf_op jit(solution)/shard_map/ppermute | solution.py:236
  225.0 23.0 %collective-permute-start.46 = (bf16[4,4,4,16,512]{4,3,2,1,0:T(8,128)(2,1)S(1)}, bf16[4,4,4,16,512]{4,3,2,1,0:T(8,128)(2,1)S(1)}, u32[]{:S(2)}, u32[]{:S(2)}) collective-permute-start(bf16[4,4,4,16,512]{4,3,2,1,0:T(8,128)(2,1)S(1)} %get-tuple-element.176), channel_id=1, source_target_pairs={{0,1},{1,0},{2,3},{3,2},{4,5},{5,4},{6,7},{7,6},{8,9},{9,8},{10,11... | collective-permute-start | bytes 3145736 | tf_op jit(solution)/shard_map/ppermute | solution.py:236
  242.6 8.4 %collective-permute-start.36 = (bf16[4,4,4,16,512]{4,3,2,1,0:T(8,128)(2,1)S(1)}, bf16[4,4,4,16,512]{4,3,2,1,0:T(8,128)(2,1)S(1)}, u32[]{:S(2)}, u32[]{:S(2)}) collective-permute-start(bf16[4,4,4,16,512]{4,3,2,1,0:T(8,128)(2,1)S(1)} %get-tuple-element.166), channel_id=1, source_target_pairs={{0,1},{1,0},{2,3},{3,2},{4,5},{5,4},{6,7},{7,6},{8,9},{9,8},{10,11... | collective-permute-start | bytes 3145736 | tf_op jit(solution)/shard_map/ppermute | solution.py:236
  244.9 14.7 %collective-permute-start.57 = (bf16[2,4,4,16,512]{4,3,2,1,0:T(8,128)(2,1)S(1)}, bf16[2,4,4,16,512]{4,3,2,1,0:T(8,128)(2,1)S(1)}, u32[]{:S(2)}, u32[]{:S(2)}) collective-permute-start(bf16[2,4,4,16,512]{4,3,2,1,0:T(8,128)(2,1)S(1)} %get-tuple-element.188), channel_id=1, source_target_pairs={{0,2},{2,4},{4,6},{6,0},{8,10},{10,12},{12,14},{14,8},{16,18},{18,... | collective-permute-start | bytes 1572872 | tf_op jit(solution)/shard_map/ppermute | solution.py:44
  245.0 26.3 %collective-permute-start.58 = (bf16[2,4,4,16,512]{4,3,2,1,0:T(8,128)(2,1)S(1)}, bf16[2,4,4,16,512]{4,3,2,1,0:T(8,128)(2,1)S(1)}, u32[]{:S(2)}, u32[]{:S(2)}) collective-permute-start(bf16[2,4,4,16,512]{4,3,2,1,0:T(8,128)(2,1)S(1)} %get-tuple-element.189), channel_id=1, source_target_pairs={{0,4},{2,6},{4,0},{6,2},{8,12},{10,14},{12,8},{14,10},{16,20},{18,... | collective-permute-start | bytes 1572872 | tf_op jit(solution)/shard_map/ppermute | solution.py:44
  248.0 23.2 %collective-permute-start.59 = (bf16[2,4,4,16,512]{4,3,2,1,0:T(8,128)(2,1)S(1)}, bf16[2,4,4,16,512]{4,3,2,1,0:T(8,128)(2,1)S(1)}, u32[]{:S(2)}, u32[]{:S(2)}) collective-permute-start(bf16[2,4,4,16,512]{4,3,2,1,0:T(8,128)(2,1)S(1)} %get-tuple-element.190), channel_id=1, source_target_pairs={{0,6},{2,0},{4,2},{6,4},{8,14},{10,8},{12,10},{14,12},{16,22},{18,... | collective-permute-start | bytes 1572872 | tf_op jit(solution)/shard_map/ppermute | solution.py:44
  248.1 24.3 %collective-permute-start.47 = (bf16[2,4,4,16,512]{4,3,2,1,0:T(8,128)(2,1)S(1)}, bf16[2,4,4,16,512]{4,3,2,1,0:T(8,128)(2,1)S(1)}, u32[]{:S(2)}, u32[]{:S(2)}) collective-permute-start(bf16[2,4,4,16,512]{4,3,2,1,0:T(8,128)(2,1)S(1)} %get-tuple-element.178), channel_id=1, source_target_pairs={{0,32},{2,34},{4,36},{6,38},{8,40},{10,42},{12,44},{14,46},{16,48}... | collective-permute-start | bytes 1572872 | tf_op jit(solution)/shard_map/ppermute | solution.py:44
  251.0 30.2 %collective-permute-start.48 = (bf16[2,4,4,16,512]{4,3,2,1,0:T(8,128)(2,1)S(1)}, bf16[2,4,4,16,512]{4,3,2,1,0:T(8,128)(2,1)S(1)}, u32[]{:S(2)}, u32[]{:S(2)}) collective-permute-start(bf16[2,4,4,16,512]{4,3,2,1,0:T(8,128)(2,1)S(1)} %get-tuple-element.179), channel_id=1, source_target_pairs={{0,64},{2,66},{4,68},{6,70},{8,72},{10,74},{12,76},{14,78},{16,80}... | collective-permute-start | bytes 1572872 | tf_op jit(solution)/shard_map/ppermute | solution.py:44
  259.6 21.6 %collective-permute-start.49 = (bf16[2,4,4,16,512]{4,3,2,1,0:T(8,128)(2,1)S(1)}, bf16[2,4,4,16,512]{4,3,2,1,0:T(8,128)(2,1)S(1)}, u32[]{:S(2)}, u32[]{:S(2)}) collective-permute-start(bf16[2,4,4,16,512]{4,3,2,1,0:T(8,128)(2,1)S(1)} %get-tuple-element.180), channel_id=1, source_target_pairs={{0,96},{2,98},{4,100},{6,102},{8,104},{10,106},{12,108},{14,110},{... | collective-permute-start | bytes 1572872 | tf_op jit(solution)/shard_map/ppermute | solution.py:44
  271.2 15.2 %collective-permute-start.37 = (bf16[2,4,4,16,512]{4,3,2,1,0:T(8,128)(2,1)S(1)}, bf16[2,4,4,16,512]{4,3,2,1,0:T(8,128)(2,1)S(1)}, u32[]{:S(2)}, u32[]{:S(2)}) collective-permute-start(bf16[2,4,4,16,512]{4,3,2,1,0:T(8,128)(2,1)S(1)} %get-tuple-element.168), channel_id=1, source_target_pairs={{0,8},{2,10},{4,12},{6,14},{8,16},{10,18},{12,20},{14,22},{16,24},... | collective-permute-start | bytes 1572872 | tf_op jit(solution)/shard_map/ppermute | solution.py:44
  271.2 23.7 %collective-permute-start.38 = (bf16[2,4,4,16,512]{4,3,2,1,0:T(8,128)(2,1)S(1)}, bf16[2,4,4,16,512]{4,3,2,1,0:T(8,128)(2,1)S(1)}, u32[]{:S(2)}, u32[]{:S(2)}) collective-permute-start(bf16[2,4,4,16,512]{4,3,2,1,0:T(8,128)(2,1)S(1)} %get-tuple-element.169), channel_id=1, source_target_pairs={{0,16},{2,18},{4,20},{6,22},{8,24},{10,26},{12,28},{14,30},{16,0},... | collective-permute-start | bytes 1572872 | tf_op jit(solution)/shard_map/ppermute | solution.py:44
  272.5 24.2 %collective-permute-start.39 = (bf16[2,4,4,16,512]{4,3,2,1,0:T(8,128)(2,1)S(1)}, bf16[2,4,4,16,512]{4,3,2,1,0:T(8,128)(2,1)S(1)}, u32[]{:S(2)}, u32[]{:S(2)}) collective-permute-start(bf16[2,4,4,16,512]{4,3,2,1,0:T(8,128)(2,1)S(1)} %get-tuple-element.170), channel_id=1, source_target_pairs={{0,24},{2,26},{4,28},{6,30},{8,0},{10,2},{12,4},{14,6},{16,8},{18,... | collective-permute-start | bytes 1572872 | tf_op jit(solution)/shard_map/ppermute | solution.py:44
  (6 other events, 106.1 us)

commit v2 on v1

--- a/solution.py
+++ b/solution.py
@@ -142,10 +142,18 @@
 def lay_out(order, pos, *refs):
     ins, out = refs[:RING], refs[-1]
     a = order[0]
+    y = pl.program_id(0)
     for back in range(RING):
         source = (pos[a] - back) & (RING - 1)
         for k in range(CORES):
-            out[(0,) + at_axis(3, a, source, pos[3] ^ k)] = ins[back][k]
+            if a == 0:
+
+                @pl.when(source == y)
+                def _(piece=ins[back].at[k], k=k):
+                    out[0, 0, :, :, pos[3] ^ k] = piece[...]
+
+            else:
+                out[(0, 0) + at_axis(2, a - 1, source, pos[3] ^ k)] = ins[back][k, y]
 
 
 def shaped(shape, dtype=BF16):
@@ -253,8 +261,8 @@
         [shaped(dims)],
         specs,
         args,
-        out_specs=[pl.BlockSpec((1, *dims[1:]), lambda i: (part,) + (0,) * 6)],
-        grid=(1,),
+        out_specs=[pl.BlockSpec((1, 1, *dims[2:]), lambda i: (part, i) + (0,) * 5)],
+        grid=(RING,),
         input_output_aliases=alias,
     )[0]
 
@@ -267,7 +275,7 @@
     return jnp.transpose(jnp.broadcast_to(row, (LANES, row.shape[1])))
 
 
-def forward(pos, index, route, pool, weights_in, cot_in, own, other, gate, upper, scaled, wd,
+def forward(pos, columns, pool, weights_in, cot_in, own, other, gate, upper, scaled, wd,
             wg, wu, cot, spot, factor, high, low, hidden, grad, sems):
     pairs = (
         (weights_in.at[0, 0], wg),
@@ -277,14 +285,15 @@
     )
     copies = [pltpu.make_async_copy(a, b, sems.at[k]) for k, (a, b) in enumerate(pairs)]
     copies[0].start()
+    copies[1].start()
     width, hidden_units = wg.shape
-    rows = index.shape[1]
+    rows = columns.shape[1]
     scale_in, scale_out = width ** (-0.5), hidden_units ** (-0.5)
-    spot[...] = down_columns(index[...].astype(F32))
-    factor[...] = down_columns(route[...])
+    spot[...] = down_columns(columns[0:1, :])
+    factor[...] = down_columns(columns[1:2, :])
     for k, w in enumerate((wg, wu)):
         copies[k].wait()
-        copies[k + 1].start()
+        copies[k + 2].start()
         values = mul(pool[...], w[...], (1, 0)) * scale_in
         top = values.astype(BF16)
         high[k] = top
@@ -314,7 +323,6 @@
 
     lax.fori_loop(0, rows // 64, activate, 0)
     copies[2].wait()
-    copies[3].start()
 
     def scale(step, carry):
         r = pl.ds(pl.multiple_of(step * 32, 32), 32)
@@ -349,9 +357,9 @@
     lax.fori_loop(0, 16, step, 0)
 
 
-def backward(index, gate, upper, scaled, wd, gate_sum, up_sum, d_gate, d_up):
-    spots = lax.broadcasted_iota(jnp.int32, (gate_sum.shape[0], index.shape[1]), 0)
-    chosen = jnp.where(index[...] == spots, 1.0, 0.0).astype(BF16)
+def backward(columns, gate, upper, scaled, wd, gate_sum, up_sum, d_gate, d_up):
+    spots = lax.broadcasted_iota(jnp.int32, (gate_sum.shape[0], columns.shape[1]), 0)
+    chosen = jnp.where(columns[0:1, :] == spots.astype(F32), 1.0, 0.0).astype(BF16)
     scale_out = wd.shape[1] ** (-0.5)
 
     def step(k, carry):
@@ -383,7 +391,7 @@
     halve(pos, grad, own, other)
 
 
-def run_forward(pos, index, route, pool, weights, cot):
+def run_forward(pos, columns, pool, weights, cot):
     rows, width = cot.shape
     tokens, hid = pool.shape[0], weights.shape[3]
     half = (width // (BLOCK * CORES), BLOCK, hid)
@@ -392,8 +400,8 @@
         [shaped(half)] * 2
         + [shaped((rows, hid), F32)] * 2
         + [shaped((rows, width)), shaped((width, hid))],
-        [SMEM, VMEM, VMEM, VMEM, HBM, HBM],
-        (pos, index, route, pool, weights, cot),
+        [SMEM, VMEM, VMEM, HBM, HBM],
+        (pos, columns, pool, weights, cot),
         scratch_shapes=[
             pltpu.VMEM((width, hid), BF16),
             pltpu.VMEM((width, hid), BF16),
@@ -411,13 +419,13 @@
     )
 
 
-def run_backward(index, gate, upper, scaled, wd, tokens):
+def run_backward(columns, gate, upper, scaled, wd, tokens):
     rows, hid = gate.shape
     return call(
         backward,
         [shaped((tokens, hid))] * 2,
         [VMEM] * 5,
-        (index, gate, upper, scaled, wd),
+        (columns, gate, upper, scaled, wd),
         scratch_shapes=[pltpu.VMEM((rows, hid), BF16), pltpu.VMEM((rows, hid), BF16)],
         limit=24 * 2**20,
         work=3 * 10**9,
@@ -458,11 +466,13 @@
     weights_in = slot_weights
     scale_in = pool_tokens.shape[1] ** (-0.5)
     tokens = pool_tokens.shape[0]
+    first_row = lax.broadcasted_iota(jnp.int32, (2, row_index.shape[1]), 0) == 0
+    columns = jnp.where(first_row, row_index.astype(F32), route_weight)
     own, other, gate, upper, scaled, wd = run_forward(
-        pos, row_index, route_weight, pool_tokens, weights_in, cotangent
+        pos, columns, pool_tokens, weights_in, cotangent
     )
     cut = {2: start_grads(own, other, ORDERS[2], pos)}
-    gate_sum, up_sum = run_backward(row_index, gate, upper, scaled, wd, tokens)
+    gate_sum, up_sum = run_backward(columns, gate, upper, scaled, wd, tokens)
     cut[2], (gate_sum, up_sum) = lax.optimization_barrier((cut[2], (gate_sum, up_sum)))
     for part, total in ((0, gate_sum), (1, up_sum)):
         own, other = run_pool_grad(pos, pool_tokens, total)

time: 300 us -> 300 us (level)
  no operation moved by 1% of the time
where the time goes in v2:
time: 300 us; the launch traced here: 299 us
  waiting for transfers between devices  163 us (54%)
  starting transfers between devices  88.1 us (29%)
  Pallas kernels  37.2 us (12%)
  local copies, waits for them, and re-layouts  4.32 us (1%)
  matrix products  3.25 us (1%)
    ppermute x54, waiting for transfers between devices, shift(): lax.ppermute(array, 'wide', [(chip, moved(chip, axis, steps)) for chip in...  163 us
    ppermute x54, starting transfers between devices, shift(): lax.ppermute(array, 'wide', [(chip, moved(chip, axis, steps)) for chip in...  78.9 us
    pallas_call x25, Pallas kernels, call(): pl.pallas_call(body, out_shape=outs, in_specs=in_specs, out_specs=specs,...  37.2 us
    ppermute x3, starting transfers between devices, send_weights(): other = lax.ppermute(sent, 'narrow', [(0, 1), (1, 0)])  6.63 us
  transfers between devices with their start and end apart: 60, of which 30 were waited for; matrix products, arithmetic and copies ran while one was open for 2% of the time, Pallas kernels for 8%

profile of v2, /device:TPU:1, one launch (start us, length us, event | category | flops | bytes accessed | tf_op | source)
XLA Modules:
  0.0 298.5 jit_solution(4207873828873701252)
XLA Ops:
  3.7 10.4 %shard_map.137 = (bf16[64,16,512]{2,1,0:T(8,128)(2,1)S(1)}, bf16[64,16,512]{2,1,0:T(8,128)(2,1)S(1)}, f32[768,512]{1,0:T(8,128)S(1)}, f32[768,512]{1,0:T(8,128)S...) custom-call(s32[4]{0:T(128)S(1)} %pad_add_fusion.pos, f32[2,768]{1,0:T(2,128)S(1)} %broadcast_select_fusion.columns, ...), custom_call_target="tpu_custom_call" | custom-call | flops 5000000000 | tf_op jit(solution)/shard_map/pallas_call | solution.py:165
  14.1 1.5 collective-permute-start
  15.5 3.3 %shard_map.139 = (bf16[384,512]{1,0:T(8,128)(2,1)S(1)}, bf16[384,512]{1,0:T(8,128)(2,1)S(1)}) custom-call(f32[2,768]{1,0:T(2,128)S(1)} %broadcast_select_fusion.columns, f32[768,512]{1,0:T(8,128)S(1)} %get-tuple-element.104.gate, f32[768,512]{1,0:T(8,128)S(1)} %get-tuple-element.105.upper, bf16[768,2048]{1,0:T(8,128)(2,1)S(1)} %get-tuple-element.106.scaled, ...), custom_call_target="tpu_custom_call" | custom-call | flops 3000000000 | tf_op jit(solution)/shard_map/pallas_call | solution.py:165
  19.5 1.8 collective-permute-start.21
  21.3 3.3 %collective-permute-start.22 = (bf16[2,4,4,16,512]{4,3,2,1,0:T(8,128)(2,1)S(1)}, bf16[2,4,4,16,512]{4,3,2,1,0:T(8,128)(2,1)S(1)}, u32[]{:S(2)}, u32[]{:S(2)}) collective-permute-start(bf16[2,4,4,16,512]{4,3,2,1,0:T(8,128)(2,1)S(1)} %get-tuple-element.144), channel_id=1, source_target_pairs={{0,4},{2,6},{4,0},{6,2},{8,12},{10,14},{12,8},{14,10},{16,20},{18,... | collective-permute-start | bytes 1572872 | tf_op jit(solution)/shard_map/ppermute | solution.py:44
  24.7 2.7 shard_map.140
  28.8 2.7 shard_map.145
  31.9 3.8 %collective-permute-done.21.refs_1_ = bf16[2,4,4,16,512]{4,3,2,1,0:T(8,128)(2,1)S(1)} collective-permute-done((bf16[2,4,4,16,512]{4,3,2,1,0:T(8,128)(2,1)S(1)}, bf16[2,4,4,16,512]{4,3,2,1,0:T(8,128)(2,1)S(1)}, u32[]{:S(2)}, u32[]{:S(2)}) %collective-permute-start.21) | collective-permute-done | bytes 524320 | tf_op jit(solution)/shard_map/ppermute | solution.py:44
  35.8 12.1 %collective-permute-done.22.refs_2_ = bf16[2,4,4,16,512]{4,3,2,1,0:T(8,128)(2,1)S(1)} collective-permute-done((bf16[2,4,4,16,512]{4,3,2,1,0:T(8,128)(2,1)S(1)}, bf16[2,4,4,16,512]{4,3,2,1,0:T(8,128)(2,1)S(1)}, u32[]{:S(2)}, u32[]{:S(2)}) %collective-permute-start.22) | collective-permute-done | bytes 524320 | tf_op jit(solution)/shard_map/ppermute | solution.py:44
  50.0 2.6 collective-permute-start.25
  54.8 7.8 %collective-permute-done.24.refs_1_ = bf16[8,4,16,512]{3,2,1,0:T(8,128)(2,1)S(1)} collective-permute-done((bf16[8,4,16,512]{3,2,1,0:T(8,128)(2,1)S(1)}, bf16[8,4,16,512]{3,2,1,0:T(8,128)(2,1)S(1)}, u32[]{:S(2)}, u32[]{:S(2)}) %collective-permute-start.24) | collective-permute-done | bytes 524320 | tf_op jit(solution)/shard_map/ppermute | solution.py:44
  62.6 12.4 %collective-permute-done.25.refs_2_ = bf16[8,4,16,512]{3,2,1,0:T(8,128)(2,1)S(1)} collective-permute-done((bf16[8,4,16,512]{3,2,1,0:T(8,128)(2,1)S(1)}, bf16[8,4,16,512]{3,2,1,0:T(8,128)(2,1)S(1)}, u32[]{:S(2)}, u32[]{:S(2)}) %collective-permute-start.25) | collective-permute-done | bytes 524320 | tf_op jit(solution)/shard_map/ppermute | solution.py:44
  77.4 2.0 collective-permute-start.3
  79.4 1.8 collective-permute-start.4
  81.2 2.4 collective-permute-start.28
  84.4 2.6 collective-permute-done.28.two
  88.0 3.2 %collective-permute-done.29.three = bf16[8,16,512]{2,1,0:T(8,128)(2,1)S(1)} collective-permute-done((bf16[8,16,512]{2,1,0:T(8,128)(2,1)S(1)}, bf16[8,16,512]{2,1,0:T(8,128)(2,1)S(1)}, u32[]{:S(2)}, u32[]{:S(2)}) %collective-permute-start.29) | collective-permute-done | bytes 131104 | tf_op jit(solution)/shard_map/ppermute | solution.py:44
  92.3 9.6 %collective-permute-done.50 = bf16[8,16,512]{2,1,0:T(8,128)(2,1)S(1)} collective-permute-done((bf16[8,16,512]{2,1,0:T(8,128)(2,1)S(1)}, bf16[8,16,512]{2,1,0:T(8,128)(2,1)S(1)}, u32[]{:S(2)}, u32[]{:S(2)}) %collective-permute-start.50) | collective-permute-done | bytes 131104 | tf_op jit(solution)/shard_map/ppermute | solution.py:44
  103.2 1.7 collective-permute-start.13
  104.9 2.1 collective-permute-start.14
  109.0 1.6 collective-permute-start.7
  110.7 7.0 %collective-permute-done.13.refs_2_ = bf16[2,4,4,16,512]{4,3,2,1,0:T(8,128)(2,1)S(1)} collective-permute-done((bf16[2,4,4,16,512]{4,3,2,1,0:T(8,128)(2,1)S(1)}, bf16[2,4,4,16,512]{4,3,2,1,0:T(8,128)(2,1)S(1)}, u32[]{:S(2)}, u32[]{:S(2)}) %collective-permute-start.13) | collective-permute-done | bytes 524320 | tf_op jit(solution)/shard_map/ppermute | solution.py:44
  117.7 13.1 %collective-permute-done.14.refs_3_ = bf16[2,4,4,16,512]{4,3,2,1,0:T(8,128)(2,1)S(1)} collective-permute-done((bf16[2,4,4,16,512]{4,3,2,1,0:T(8,128)(2,1)S(1)}, bf16[2,4,4,16,512]{4,3,2,1,0:T(8,128)(2,1)S(1)}, u32[]{:S(2)}, u32[]{:S(2)}) %collective-permute-start.14) | collective-permute-done | bytes 524320 | tf_op jit(solution)/shard_map/ppermute | solution.py:44
  131.5 1.8 collective-permute-start.15
  133.6 1.7 collective-permute-start.16
  135.3 4.9 %collective-permute-done.6.refs_2_ = bf16[8,4,16,512]{3,2,1,0:T(8,128)(2,1)S(1)} collective-permute-done((bf16[8,4,16,512]{3,2,1,0:T(8,128)(2,1)S(1)}, bf16[8,4,16,512]{3,2,1,0:T(8,128)(2,1)S(1)}, u32[]{:S(2)}, u32[]{:S(2)}) %collective-permute-start.6) | collective-permute-done | bytes 524320 | tf_op jit(solution)/shard_map/ppermute | solution.py:44
  140.2 13.1 %collective-permute-done.7.refs_3_ = bf16[8,4,16,512]{3,2,1,0:T(8,128)(2,1)S(1)} collective-permute-done((bf16[8,4,16,512]{3,2,1,0:T(8,128)(2,1)S(1)}, bf16[8,4,16,512]{3,2,1,0:T(8,128)(2,1)S(1)}, u32[]{:S(2)}, u32[]{:S(2)}) %collective-permute-start.7) | collective-permute-done | bytes 524320 | tf_op jit(solution)/shard_map/ppermute | solution.py:44
  154.4 2.4 collective-permute-start.10
  156.8 2.0 collective-permute-done.10.three
  160.0 4.2 %collective-permute-done.8.one = bf16[8,16,512]{2,1,0:T(8,128)(2,1)S(1)} collective-permute-done((bf16[8,16,512]{2,1,0:T(8,128)(2,1)S(1)}, bf16[8,16,512]{2,1,0:T(8,128)(2,1)S(1)}, u32[]{:S(2)}, u32[]{:S(2)}) %collective-permute-start.8) | collective-permute-done | bytes 131104 | tf_op jit(solution)/shard_map/ppermute | solution.py:44
  164.9 5.0 %collective-permute-done.9.two = bf16[8,16,512]{2,1,0:T(8,128)(2,1)S(1)} collective-permute-done((bf16[8,16,512]{2,1,0:T(8,128)(2,1)S(1)}, bf16[8,16,512]{2,1,0:T(8,128)(2,1)S(1)}, u32[]{:S(2)}, u32[]{:S(2)}) %collective-permute-start.9) | collective-permute-done | bytes 131104 | tf_op jit(solution)/shard_map/ppermute | solution.py:44
  169.9 2.3 collective-permute-start.54
  172.4 3.2 %collective-permute-start.40 = (bf16[8,16,512]{2,1,0:T(8,128)(2,1)S(1)}, bf16[8,16,512]{2,1,0:T(8,128)(2,1)S(1)}, u32[]{:S(2)}, u32[]{:S(2)}) collective-permute-start(bf16[8,16,512]{2,1,0:T(8,128)(2,1)S(1)} %get-tuple-element.171), channel_id=1, source_target_pairs={{0,2},{2,4},{4,6},{6,0},{8,10},{10,12},{12,14},{14,8},{16,18},{18,... | collective-permute-start | bytes 393224 | tf_op jit(solution)/shard_map/ppermute | solution.py:44
  175.6 3.4 %collective-permute-start.41 = (bf16[8,16,512]{2,1,0:T(8,128)(2,1)S(1)}, bf16[8,16,512]{2,1,0:T(8,128)(2,1)S(1)}, u32[]{:S(2)}, u32[]{:S(2)}) collective-permute-start(bf16[8,16,512]{2,1,0:T(8,128)(2,1)S(1)} %get-tuple-element.171), channel_id=1, source_target_pairs={{0,4},{2,6},{4,0},{6,2},{8,12},{10,14},{12,8},{14,10},{16,20},{18,... | collective-permute-start | bytes 393224 | tf_op jit(solution)/shard_map/ppermute | solution.py:44
  180.2 1.5 collective-permute-start.18
  184.3 6.8 %collective-permute-done.18.one = bf16[8,16,512]{2,1,0:T(8,128)(2,1)S(1)} collective-permute-done((bf16[8,16,512]{2,1,0:T(8,128)(2,1)S(1)}, bf16[8,16,512]{2,1,0:T(8,128)(2,1)S(1)}, u32[]{:S(2)}, u32[]{:S(2)}) %collective-permute-start.18) | collective-permute-done | bytes 131104 | tf_op jit(solution)/shard_map/ppermute | solution.py:44
  192.0 2.3 collective-permute-start.44
  194.3 4.3 %collective-permute-done.20.three = bf16[8,16,512]{2,1,0:T(8,128)(2,1)S(1)} collective-permute-done((bf16[8,16,512]{2,1,0:T(8,128)(2,1)S(1)}, bf16[8,16,512]{2,1,0:T(8,128)(2,1)S(1)}, u32[]{:S(2)}, u32[]{:S(2)}) %collective-permute-start.20) | collective-permute-done | bytes 131104 | tf_op jit(solution)/shard_map/ppermute | solution.py:44
  198.6 2.4 collective-permute-start.45
  201.3 2.3 collective-permute-start.30
  203.6 1.7 collective-permute-start.31
  205.3 1.5 collective-permute-done.30
  209.1 1.8 collective-permute-done.32
  211.0 3.4 %collective-permute-start.33 = (bf16[4,8,16,512]{3,2,1,0:T(8,128)(2,1)S(1)}, bf16[4,8,16,512]{3,2,1,0:T(8,128)(2,1)S(1)}, u32[]{:S(2)}, u32[]{:S(2)}) collective-permute-start(bf16[4,8,16,512]{3,2,1,0:T(8,128)(2,1)S(1)} %pad_maximum_fusion.3.refs_0_), channel_id=1, source_target_pairs={{0,2},{2,4},{4,6},{6,0},{8,10},{10,12},{12,14},{14,8},{16,18},{18,... | collective-permute-start | bytes 1572872 | tf_op jit(solution)/shard_map/ppermute | solution.py:44
  214.4 4.8 %collective-permute-start.34 = (bf16[4,8,16,512]{3,2,1,0:T(8,128)(2,1)S(1)}, bf16[4,8,16,512]{3,2,1,0:T(8,128)(2,1)S(1)}, u32[]{:S(2)}, u32[]{:S(2)}) collective-permute-start(bf16[4,8,16,512]{3,2,1,0:T(8,128)(2,1)S(1)} %pad_maximum_fusion.3.refs_0_), channel_id=1, source_target_pairs={{0,4},{2,6},{4,0},{6,2},{8,12},{10,14},{12,8},{14,10},{16,20},{18,... | collective-permute-start | bytes 1572872 | tf_op jit(solution)/shard_map/ppermute | solution.py:44
  219.2 4.4 %collective-permute-start.56 = (bf16[4,4,4,16,512]{4,3,2,1,0:T(8,128)(2,1)S(1)}, bf16[4,4,4,16,512]{4,3,2,1,0:T(8,128)(2,1)S(1)}, u32[]{:S(2)}, u32[]{:S(2)}) collective-permute-start(bf16[4,4,4,16,512]{4,3,2,1,0:T(8,128)(2,1)S(1)} %get-tuple-element.186), channel_id=1, source_target_pairs={{0,1},{1,0},{2,3},{3,2},{4,5},{5,4},{6,7},{7,6},{8,9},{9,8},{10,11... | collective-permute-start | bytes 3145736 | tf_op jit(solution)/shard_map/ppermute | solution.py:244
  224.6 2.2 collective-permute-done.33.refs_1_
  226.8 12.1 %collective-permute-done.34.refs_2_ = bf16[4,8,16,512]{3,2,1,0:T(8,128)(2,1)S(1)} collective-permute-done((bf16[4,8,16,512]{3,2,1,0:T(8,128)(2,1)S(1)}, bf16[4,8,16,512]{3,2,1,0:T(8,128)(2,1)S(1)}, u32[]{:S(2)}, u32[]{:S(2)}) %collective-permute-start.34) | collective-permute-done | bytes 524320 | tf_op jit(solution)/shard_map/ppermute | solution.py:44
  238.9 2.4 collective-permute-done.35.refs_3_
  242.1 2.1 collective-permute-start.36
  244.4 3.0 %collective-permute-start.58 = (bf16[2,4,4,16,512]{4,3,2,1,0:T(8,128)(2,1)S(1)}, bf16[2,4,4,16,512]{4,3,2,1,0:T(8,128)(2,1)S(1)}, u32[]{:S(2)}, u32[]{:S(2)}) collective-permute-start(bf16[2,4,4,16,512]{4,3,2,1,0:T(8,128)(2,1)S(1)} %get-tuple-element.189), channel_id=1, source_target_pairs={{0,4},{2,6},{4,0},{6,2},{8,12},{10,14},{12,8},{14,10},{16,20},{18,... | collective-permute-start | bytes 1572872 | tf_op jit(solution)/shard_map/ppermute | solution.py:44
  247.6 1.9 collective-permute-start.47
  250.5 1.9 collective-permute-start.48
  252.5 6.6 %collective-permute-done.57.refs_1_ = bf16[2,4,4,16,512]{4,3,2,1,0:T(8,128)(2,1)S(1)} collective-permute-done((bf16[2,4,4,16,512]{4,3,2,1,0:T(8,128)(2,1)S(1)}, bf16[2,4,4,16,512]{4,3,2,1,0:T(8,128)(2,1)S(1)}, u32[]{:S(2)}, u32[]{:S(2)}) %collective-permute-start.57) | collective-permute-done | bytes 524320 | tf_op jit(solution)/shard_map/ppermute | solution.py:44
  259.1 2.4 collective-permute-start.49
  261.4 9.2 %collective-permute-done.58.refs_2_ = bf16[2,4,4,16,512]{4,3,2,1,0:T(8,128)(2,1)S(1)} collective-permute-done((bf16[2,4,4,16,512]{4,3,2,1,0:T(8,128)(2,1)S(1)}, bf16[2,4,4,16,512]{4,3,2,1,0:T(8,128)(2,1)S(1)}, u32[]{:S(2)}, u32[]{:S(2)}) %collective-permute-start.58) | collective-permute-done | bytes 524320 | tf_op jit(solution)/shard_map/ppermute | solution.py:44
  272.0 1.5 collective-permute-start.39
  273.4 2.2 multiply_convert_fusion
  278.8 2.4 shard_map.159.refs_4_
  281.2 2.5 shard_map.160.refs_4_
  283.6 2.2 collective-permute-done.37.refs_1_
  285.8 8.5 %collective-permute-done.38.refs_2_ = bf16[2,4,4,16,512]{4,3,2,1,0:T(8,128)(2,1)S(1)} collective-permute-done((bf16[2,4,4,16,512]{4,3,2,1,0:T(8,128)(2,1)S(1)}, bf16[2,4,4,16,512]{4,3,2,1,0:T(8,128)(2,1)S(1)}, u32[]{:S(2)}, u32[]{:S(2)}) %collective-permute-start.38) | collective-permute-done | bytes 524320 | tf_op jit(solution)/shard_map/ppermute | solution.py:44
  294.4 1.8 collective-permute-done.39.refs_3_
  296.1 2.4 shard_map.161
  (114 shorter events, 37.5 us)
Async XLA Ops:
  14.1 4.7 %collective-permute-start = (bf16[64,16,512]{2,1,0:T(8,128)(2,1)S(1)}, bf16[64,16,512]{2,1,0:T(8,128)(2,1)S(1)}, u32[]{:S(2)}, u32[]{:S(2)}) collective-permute-start(bf16[64,16,512]{2,1,0:T(8,128)(2,1)S(1)} %get-tuple-element.99), channel_id=1, source_target_pairs={{0,1},{1,0},{2,3},{3,2},{4,5},{5,4},{6,7},{7,6},{8,9},{9,8},{10,11... | collective-permute-start | bytes 3145736 | tf_op jit(solution)/shard_map/ppermute | solution.py:186
  19.5 16.2 %collective-permute-start.21 = (bf16[2,4,4,16,512]{4,3,2,1,0:T(8,128)(2,1)S(1)}, bf16[2,4,4,16,512]{4,3,2,1,0:T(8,128)(2,1)S(1)}, u32[]{:S(2)}, u32[]{:S(2)}) collective-permute-start(bf16[2,4,4,16,512]{4,3,2,1,0:T(8,128)(2,1)S(1)} %get-tuple-element.143), channel_id=1, source_target_pairs={{0,2},{2,4},{4,6},{6,0},{8,10},{10,12},{12,14},{14,8},{16,18},{18,... | collective-permute-start | bytes 1572872 | tf_op jit(solution)/shard_map/ppermute | solution.py:44
  21.3 26.5 %collective-permute-start.22 = (bf16[2,4,4,16,512]{4,3,2,1,0:T(8,128)(2,1)S(1)}, bf16[2,4,4,16,512]{4,3,2,1,0:T(8,128)(2,1)S(1)}, u32[]{:S(2)}, u32[]{:S(2)}) collective-permute-start(bf16[2,4,4,16,512]{4,3,2,1,0:T(8,128)(2,1)S(1)} %get-tuple-element.144), channel_id=1, source_target_pairs={{0,4},{2,6},{4,0},{6,2},{8,12},{10,14},{12,8},{14,10},{16,20},{18,... | collective-permute-start | bytes 1572872 | tf_op jit(solution)/shard_map/ppermute | solution.py:44
  27.4 47.6 %copy-start.3 = (s32[128,1]{0,1:T(1,128)S(1)}, s32[128,1]{0,1:T(1,128)}, u32[]{:S(2)}) copy-start(s32[128,1]{0,1:T(1,128)} %param.15) | copy-start | bytes 1540
  27.4 26.2 %collective-permute-start.1 = (bf16[64,16,512]{2,1,0:T(8,128)(2,1)S(1)}, bf16[64,16,512]{2,1,0:T(8,128)(2,1)S(1)}, u32[]{:S(2)}, u32[]{:S(2)}) collective-permute-start(bf16[64,16,512]{2,1,0:T(8,128)(2,1)S(1)} %get-tuple-element.113), channel_id=1, source_target_pairs={{0,1},{1,0},{2,3},{3,2},{4,5},{5,4},{6,7},{7,6},{8,9},{9,8},{10,11... | collective-permute-start | bytes 3145736 | tf_op jit(solution)/shard_map/ppermute | solution.py:186
  28.0 19.8 %collective-permute-start.23 = (bf16[2,4,4,16,512]{4,3,2,1,0:T(8,128)(2,1)S(1)}, bf16[2,4,4,16,512]{4,3,2,1,0:T(8,128)(2,1)S(1)}, u32[]{:S(2)}, u32[]{:S(2)}) collective-permute-start(bf16[2,4,4,16,512]{4,3,2,1,0:T(8,128)(2,1)S(1)} %get-tuple-element.145), channel_id=1, source_target_pairs={{0,6},{2,0},{4,2},{6,4},{8,14},{10,8},{12,10},{14,12},{16,22},{18,... | collective-permute-start | bytes 1572872 | tf_op jit(solution)/shard_map/ppermute | solution.py:44
  31.5 49.7 %collective-permute-start.11 = (bf16[64,16,512]{2,1,0:T(8,128)(2,1)S(1)}, bf16[64,16,512]{2,1,0:T(8,128)(2,1)S(1)}, u32[]{:S(2)}, u32[]{:S(2)}) collective-permute-start(bf16[64,16,512]{2,1,0:T(8,128)(2,1)S(1)} %get-tuple-element.128), channel_id=1, source_target_pairs={{0,1},{1,0},{2,3},{3,2},{4,5},{5,4},{6,7},{7,6},{8,9},{9,8},{10,11... | collective-permute-start | bytes 3145736 | tf_op jit(solution)/shard_map/ppermute | solution.py:186
  48.6 14.0 %collective-permute-start.24 = (bf16[8,4,16,512]{3,2,1,0:T(8,128)(2,1)S(1)}, bf16[8,4,16,512]{3,2,1,0:T(8,128)(2,1)S(1)}, u32[]{:S(2)}, u32[]{:S(2)}) collective-permute-start(bf16[8,4,16,512]{3,2,1,0:T(8,128)(2,1)S(1)} %get-tuple-element.147), channel_id=1, source_target_pairs={{0,32},{2,34},{4,36},{6,38},{8,40},{10,42},{12,44},{14,46},{16,48}... | collective-permute-start | bytes 1572872 | tf_op jit(solution)/shard_map/ppermute | solution.py:44
  50.0 25.0 %collective-permute-start.25 = (bf16[8,4,16,512]{3,2,1,0:T(8,128)(2,1)S(1)}, bf16[8,4,16,512]{3,2,1,0:T(8,128)(2,1)S(1)}, u32[]{:S(2)}, u32[]{:S(2)}) collective-permute-start(bf16[8,4,16,512]{3,2,1,0:T(8,128)(2,1)S(1)} %get-tuple-element.148), channel_id=1, source_target_pairs={{0,64},{2,66},{4,68},{6,70},{8,72},{10,74},{12,76},{14,78},{16,80}... | collective-permute-start | bytes 1572872 | tf_op jit(solution)/shard_map/ppermute | solution.py:44
  52.6 22.4 %collective-permute-start.26 = (bf16[8,4,16,512]{3,2,1,0:T(8,128)(2,1)S(1)}, bf16[8,4,16,512]{3,2,1,0:T(8,128)(2,1)S(1)}, u32[]{:S(2)}, u32[]{:S(2)}) collective-permute-start(bf16[8,4,16,512]{3,2,1,0:T(8,128)(2,1)S(1)} %get-tuple-element.149), channel_id=1, source_target_pairs={{0,96},{2,98},{4,100},{6,102},{8,104},{10,106},{12,108},{14,110},{... | collective-permute-start | bytes 1572872 | tf_op jit(solution)/shard_map/ppermute | solution.py:44
  53.6 37.5 %copy-start.1 = (f32[8,3,16,512]{3,2,1,0:T(8,128)S(1)}, f32[8,3,16,512]{3,2,1,0:T(8,128)}, u32[]{:S(2)}) copy-start(f32[8,3,16,512]{3,2,1,0:T(8,128)} %moment_m.5) | copy-start | bytes 2359300
  53.6 37.6 %copy-start.2 = (f32[8,3,16,512]{3,2,1,0:T(8,128)S(1)}, f32[8,3,16,512]{3,2,1,0:T(8,128)}, u32[]{:S(2)}) copy-start(f32[8,3,16,512]{3,2,1,0:T(8,128)} %moment_v.5) | copy-start | bytes 2359300
  54.4 48.8 %collective-permute-start.2 = (bf16[2,4,4,16,512]{4,3,2,1,0:T(8,128)(2,1)S(1)}, bf16[2,4,4,16,512]{4,3,2,1,0:T(8,128)(2,1)S(1)}, u32[]{:S(2)}, u32[]{:S(2)}) collective-permute-start(bf16[2,4,4,16,512]{4,3,2,1,0:T(8,128)(2,1)S(1)} %get-tuple-element.115), channel_id=1, source_target_pairs={{0,32},{2,34},{4,36},{6,38},{8,40},{10,42},{12,44},{14,46},{16,48}... | collective-permute-start | bytes 1572872 | tf_op jit(solution)/shard_map/ppermute | solution.py:44
  76.1 8.3 %collective-permute-start.27 = (bf16[8,16,512]{2,1,0:T(8,128)(2,1)S(1)}, bf16[8,16,512]{2,1,0:T(8,128)(2,1)S(1)}, u32[]{:S(2)}, u32[]{:S(2)}) collective-permute-start(bf16[8,16,512]{2,1,0:T(8,128)(2,1)S(1)} %get-tuple-element.151), channel_id=1, source_target_pairs={{0,8},{2,10},{4,12},{6,14},{8,16},{10,18},{12,20},{14,22},{16,24},... | collective-permute-start | bytes 393224 | tf_op jit(solution)/shard_map/ppermute | solution.py:44
  77.4 25.9 %collective-permute-start.3 = (bf16[2,4,4,16,512]{4,3,2,1,0:T(8,128)(2,1)S(1)}, bf16[2,4,4,16,512]{4,3,2,1,0:T(8,128)(2,1)S(1)}, u32[]{:S(2)}, u32[]{:S(2)}) collective-permute-start(bf16[2,4,4,16,512]{4,3,2,1,0:T(8,128)(2,1)S(1)} %get-tuple-element.116), channel_id=1, source_target_pairs={{0,64},{2,66},{4,68},{6,70},{8,72},{10,74},{12,76},{14,78},{16,80}... | collective-permute-start | bytes 1572872 | tf_op jit(solution)/shard_map/ppermute | solution.py:44
  79.4 25.6 %collective-permute-start.4 = (bf16[2,4,4,16,512]{4,3,2,1,0:T(8,128)(2,1)S(1)}, bf16[2,4,4,16,512]{4,3,2,1,0:T(8,128)(2,1)S(1)}, u32[]{:S(2)}, u32[]{:S(2)}) collective-permute-start(bf16[2,4,4,16,512]{4,3,2,1,0:T(8,128)(2,1)S(1)} %get-tuple-element.117), channel_id=1, source_target_pairs={{0,96},{2,98},{4,100},{6,102},{8,104},{10,106},{12,108},{14,110},{... | collective-permute-start | bytes 1572872 | tf_op jit(solution)/shard_map/ppermute | solution.py:44
  81.2 5.9 %collective-permute-start.28 = (bf16[8,16,512]{2,1,0:T(8,128)(2,1)S(1)}, bf16[8,16,512]{2,1,0:T(8,128)(2,1)S(1)}, u32[]{:S(2)}, u32[]{:S(2)}) collective-permute-start(bf16[8,16,512]{2,1,0:T(8,128)(2,1)S(1)} %get-tuple-element.152), channel_id=1, source_target_pairs={{0,16},{2,18},{4,20},{6,22},{8,24},{10,26},{12,28},{14,30},{16,0},... | collective-permute-start | bytes 393224 | tf_op jit(solution)/shard_map/ppermute | solution.py:44
  84.4 24.7 %collective-permute-start.12 = (bf16[2,4,4,16,512]{4,3,2,1,0:T(8,128)(2,1)S(1)}, bf16[2,4,4,16,512]{4,3,2,1,0:T(8,128)(2,1)S(1)}, u32[]{:S(2)}, u32[]{:S(2)}) collective-permute-start(bf16[2,4,4,16,512]{4,3,2,1,0:T(8,128)(2,1)S(1)} %get-tuple-element.130), channel_id=1, source_target_pairs={{0,8},{2,10},{4,12},{6,14},{8,16},{10,18},{12,20},{14,22},{16,24},... | collective-permute-start | bytes 1572872 | tf_op jit(solution)/shard_map/ppermute | solution.py:44
  87.1 4.1 %collective-permute-start.29 = (bf16[8,16,512]{2,1,0:T(8,128)(2,1)S(1)}, bf16[8,16,512]{2,1,0:T(8,128)(2,1)S(1)}, u32[]{:S(2)}, u32[]{:S(2)}) collective-permute-start(bf16[8,16,512]{2,1,0:T(8,128)(2,1)S(1)} %get-tuple-element.153), channel_id=1, source_target_pairs={{0,24},{2,26},{4,28},{6,30},{8,0},{10,2},{12,4},{14,6},{16,8},{18,... | collective-permute-start | bytes 393224 | tf_op jit(solution)/shard_map/ppermute | solution.py:44
  91.4 10.4 %collective-permute-start.50 = (bf16[8,16,512]{2,1,0:T(8,128)(2,1)S(1)}, bf16[8,16,512]{2,1,0:T(8,128)(2,1)S(1)}, u32[]{:S(2)}, u32[]{:S(2)}) collective-permute-start(bf16[8,16,512]{2,1,0:T(8,128)(2,1)S(1)} %get-tuple-element.181), channel_id=1, source_target_pairs={{0,8},{2,10},{4,12},{6,14},{8,16},{10,18},{12,20},{14,22},{16,24},... | collective-permute-start | bytes 393224 | tf_op jit(solution)/shard_map/ppermute | solution.py:44
  101.9 5.9 %collective-permute-start.51 = (bf16[8,16,512]{2,1,0:T(8,128)(2,1)S(1)}, bf16[8,16,512]{2,1,0:T(8,128)(2,1)S(1)}, u32[]{:S(2)}, u32[]{:S(2)}) collective-permute-start(bf16[8,16,512]{2,1,0:T(8,128)(2,1)S(1)} %get-tuple-element.181), channel_id=1, source_target_pairs={{0,16},{2,18},{4,20},{6,22},{8,24},{10,26},{12,28},{14,30},{16,0},... | collective-permute-start | bytes 393224 | tf_op jit(solution)/shard_map/ppermute | solution.py:44
  103.2 4.8 %collective-permute-start.52 = (bf16[8,16,512]{2,1,0:T(8,128)(2,1)S(1)}, bf16[8,16,512]{2,1,0:T(8,128)(2,1)S(1)}, u32[]{:S(2)}, u32[]{:S(2)}) collective-permute-start(bf16[8,16,512]{2,1,0:T(8,128)(2,1)S(1)} %get-tuple-element.181), channel_id=1, source_target_pairs={{0,24},{2,26},{4,28},{6,30},{8,0},{10,2},{12,4},{14,6},{16,8},{18,... | collective-permute-start | bytes 393224 | tf_op jit(solution)/shard_map/ppermute | solution.py:44
  103.2 14.5 %collective-permute-start.13 = (bf16[2,4,4,16,512]{4,3,2,1,0:T(8,128)(2,1)S(1)}, bf16[2,4,4,16,512]{4,3,2,1,0:T(8,128)(2,1)S(1)}, u32[]{:S(2)}, u32[]{:S(2)}) collective-permute-start(bf16[2,4,4,16,512]{4,3,2,1,0:T(8,128)(2,1)S(1)} %get-tuple-element.131), channel_id=1, source_target_pairs={{0,16},{2,18},{4,20},{6,22},{8,24},{10,26},{12,28},{14,30},{16,0},... | collective-permute-start | bytes 1572872 | tf_op jit(solution)/shard_map/ppermute | solution.py:44
  104.9 25.9 %collective-permute-start.14 = (bf16[2,4,4,16,512]{4,3,2,1,0:T(8,128)(2,1)S(1)}, bf16[2,4,4,16,512]{4,3,2,1,0:T(8,128)(2,1)S(1)}, u32[]{:S(2)}, u32[]{:S(2)}) collective-permute-start(bf16[2,4,4,16,512]{4,3,2,1,0:T(8,128)(2,1)S(1)} %get-tuple-element.132), channel_id=1, source_target_pairs={{0,24},{2,26},{4,28},{6,30},{8,0},{10,2},{12,4},{14,6},{16,8},{18,... | collective-permute-start | bytes 1572872 | tf_op jit(solution)/shard_map/ppermute | solution.py:44
  107.8 25.8 %collective-permute-start.5 = (bf16[8,4,16,512]{3,2,1,0:T(8,128)(2,1)S(1)}, bf16[8,4,16,512]{3,2,1,0:T(8,128)(2,1)S(1)}, u32[]{:S(2)}, u32[]{:S(2)}) collective-permute-start(bf16[8,4,16,512]{3,2,1,0:T(8,128)(2,1)S(1)} %get-tuple-element.119), channel_id=1, source_target_pairs={{0,8},{2,10},{4,12},{6,14},{8,16},{10,18},{12,20},{14,22},{16,24},... | collective-permute-start | bytes 1572872 | tf_op jit(solution)/shard_map/ppermute | solution.py:44
  108.0 32.1 %collective-permute-start.6 = (bf16[8,4,16,512]{3,2,1,0:T(8,128)(2,1)S(1)}, bf16[8,4,16,512]{3,2,1,0:T(8,128)(2,1)S(1)}, u32[]{:S(2)}, u32[]{:S(2)}) collective-permute-start(bf16[8,4,16,512]{3,2,1,0:T(8,128)(2,1)S(1)} %get-tuple-element.120), channel_id=1, source_target_pairs={{0,16},{2,18},{4,20},{6,22},{8,24},{10,26},{12,28},{14,30},{16,0},... | collective-permute-start | bytes 1572872 | tf_op jit(solution)/shard_map/ppermute | solution.py:44
  109.0 44.3 %collective-permute-start.7 = (bf16[8,4,16,512]{3,2,1,0:T(8,128)(2,1)S(1)}, bf16[8,4,16,512]{3,2,1,0:T(8,128)(2,1)S(1)}, u32[]{:S(2)}, u32[]{:S(2)}) collective-permute-start(bf16[8,4,16,512]{3,2,1,0:T(8,128)(2,1)S(1)} %get-tuple-element.121), channel_id=1, source_target_pairs={{0,24},{2,26},{4,28},{6,30},{8,0},{10,2},{12,4},{14,6},{16,8},{18,... | collective-permute-start | bytes 1572872 | tf_op jit(solution)/shard_map/ppermute | solution.py:44
  117.7 54.7 %collective-permute-start.53 = (bf16[4,8,16,512]{3,2,1,0:T(8,128)(2,1)S(1)}, bf16[4,8,16,512]{3,2,1,0:T(8,128)(2,1)S(1)}, u32[]{:S(2)}, u32[]{:S(2)}) collective-permute-start(bf16[4,8,16,512]{3,2,1,0:T(8,128)(2,1)S(1)} %pad_maximum_fusion.5.refs_0_), channel_id=1, source_target_pairs={{0,32},{2,34},{4,36},{6,38},{8,40},{10,42},{12,44},{14,46},{16,48}... | collective-permute-start | bytes 1572872 | tf_op jit(solution)/shard_map/ppermute | solution.py:44
  131.5 44.1 %collective-permute-start.15 = (bf16[8,4,16,512]{3,2,1,0:T(8,128)(2,1)S(1)}, bf16[8,4,16,512]{3,2,1,0:T(8,128)(2,1)S(1)}, u32[]{:S(2)}, u32[]{:S(2)}) collective-permute-start(bf16[8,4,16,512]{3,2,1,0:T(8,128)(2,1)S(1)} %get-tuple-element.134), channel_id=1, source_target_pairs={{0,2},{2,4},{4,6},{6,0},{8,10},{10,12},{12,14},{14,8},{16,18},{18,... | collective-permute-start | bytes 1572872 | tf_op jit(solution)/shard_map/ppermute | solution.py:44
  133.6 45.4 %collective-permute-start.16 = (bf16[8,4,16,512]{3,2,1,0:T(8,128)(2,1)S(1)}, bf16[8,4,16,512]{3,2,1,0:T(8,128)(2,1)S(1)}, u32[]{:S(2)}, u32[]{:S(2)}) collective-permute-start(bf16[8,4,16,512]{3,2,1,0:T(8,128)(2,1)S(1)} %get-tuple-element.135), channel_id=1, source_target_pairs={{0,4},{2,6},{4,0},{6,2},{8,12},{10,14},{12,8},{14,10},{16,20},{18,... | collective-permute-start | bytes 1572872 | tf_op jit(solution)/shard_map/ppermute | solution.py:44
  154.4 4.4 %collective-permute-start.10 = (bf16[8,16,512]{2,1,0:T(8,128)(2,1)S(1)}, bf16[8,16,512]{2,1,0:T(8,128)(2,1)S(1)}, u32[]{:S(2)}, u32[]{:S(2)}) collective-permute-start(bf16[8,16,512]{2,1,0:T(8,128)(2,1)S(1)} %get-tuple-element.125), channel_id=1, source_target_pairs={{0,6},{2,0},{4,2},{6,4},{8,14},{10,8},{12,10},{14,12},{16,22},{18,... | collective-permute-start | bytes 393224 | tf_op jit(solution)/shard_map/ppermute | solution.py:44
  156.8 22.2 %collective-permute-start.17 = (bf16[8,4,16,512]{3,2,1,0:T(8,128)(2,1)S(1)}, bf16[8,4,16,512]{3,2,1,0:T(8,128)(2,1)S(1)}, u32[]{:S(2)}, u32[]{:S(2)}) collective-permute-start(bf16[8,4,16,512]{3,2,1,0:T(8,128)(2,1)S(1)} %get-tuple-element.136), channel_id=1, source_target_pairs={{0,6},{2,0},{4,2},{6,4},{8,14},{10,8},{12,10},{14,12},{16,22},{18,... | collective-permute-start | bytes 1572872 | tf_op jit(solution)/shard_map/ppermute | solution.py:44
  158.8 5.3 %collective-permute-start.8 = (bf16[8,16,512]{2,1,0:T(8,128)(2,1)S(1)}, bf16[8,16,512]{2,1,0:T(8,128)(2,1)S(1)}, u32[]{:S(2)}, u32[]{:S(2)}) collective-permute-start(bf16[8,16,512]{2,1,0:T(8,128)(2,1)S(1)} %get-tuple-element.123), channel_id=1, source_target_pairs={{0,2},{2,4},{4,6},{6,0},{8,10},{10,12},{12,14},{14,8},{16,18},{18,... | collective-permute-start | bytes 393224 | tf_op jit(solution)/shard_map/ppermute | solution.py:44
  164.2 5.8 %collective-permute-start.9 = (bf16[8,16,512]{2,1,0:T(8,128)(2,1)S(1)}, bf16[8,16,512]{2,1,0:T(8,128)(2,1)S(1)}, u32[]{:S(2)}, u32[]{:S(2)}) collective-permute-start(bf16[8,16,512]{2,1,0:T(8,128)(2,1)S(1)} %get-tuple-element.124), channel_id=1, source_target_pairs={{0,4},{2,6},{4,0},{6,2},{8,12},{10,14},{12,8},{14,10},{16,20},{18,... | collective-permute-start | bytes 393224 | tf_op jit(solution)/shard_map/ppermute | solution.py:44
  169.9 31.4 %collective-permute-start.54 = (bf16[4,8,16,512]{3,2,1,0:T(8,128)(2,1)S(1)}, bf16[4,8,16,512]{3,2,1,0:T(8,128)(2,1)S(1)}, u32[]{:S(2)}, u32[]{:S(2)}) collective-permute-start(bf16[4,8,16,512]{3,2,1,0:T(8,128)(2,1)S(1)} %pad_maximum_fusion.5.refs_0_), channel_id=1, source_target_pairs={{0,64},{2,66},{4,68},{6,70},{8,72},{10,74},{12,76},{14,78},{16,80}... | collective-permute-start | bytes 1572872 | tf_op jit(solution)/shard_map/ppermute | solution.py:44
  172.4 7.7 %collective-permute-start.40 = (bf16[8,16,512]{2,1,0:T(8,128)(2,1)S(1)}, bf16[8,16,512]{2,1,0:T(8,128)(2,1)S(1)}, u32[]{:S(2)}, u32[]{:S(2)}) collective-permute-start(bf16[8,16,512]{2,1,0:T(8,128)(2,1)S(1)} %get-tuple-element.171), channel_id=1, source_target_pairs={{0,2},{2,4},{4,6},{6,0},{8,10},{10,12},{12,14},{14,8},{16,18},{18,... | collective-permute-start | bytes 393224 | tf_op jit(solution)/shard_map/ppermute | solution.py:44
  175.6 7.4 %collective-permute-start.41 = (bf16[8,16,512]{2,1,0:T(8,128)(2,1)S(1)}, bf16[8,16,512]{2,1,0:T(8,128)(2,1)S(1)}, u32[]{:S(2)}, u32[]{:S(2)}) collective-permute-start(bf16[8,16,512]{2,1,0:T(8,128)(2,1)S(1)} %get-tuple-element.171), channel_id=1, source_target_pairs={{0,4},{2,6},{4,0},{6,2},{8,12},{10,14},{12,8},{14,10},{16,20},{18,... | collective-permute-start | bytes 393224 | tf_op jit(solution)/shard_map/ppermute | solution.py:44
  179.0 4.5 %collective-permute-start.42 = (bf16[8,16,512]{2,1,0:T(8,128)(2,1)S(1)}, bf16[8,16,512]{2,1,0:T(8,128)(2,1)S(1)}, u32[]{:S(2)}, u32[]{:S(2)}) collective-permute-start(bf16[8,16,512]{2,1,0:T(8,128)(2,1)S(1)} %get-tuple-element.171), channel_id=1, source_target_pairs={{0,6},{2,0},{4,2},{6,4},{8,14},{10,8},{12,10},{14,12},{16,22},{18,... | collective-permute-start | bytes 393224 | tf_op jit(solution)/shard_map/ppermute | solution.py:44
  179.0 24.6 %collective-permute-start.55 = (bf16[4,8,16,512]{3,2,1,0:T(8,128)(2,1)S(1)}, bf16[4,8,16,512]{3,2,1,0:T(8,128)(2,1)S(1)}, u32[]{:S(2)}, u32[]{:S(2)}) collective-permute-start(bf16[4,8,16,512]{3,2,1,0:T(8,128)(2,1)S(1)} %pad_maximum_fusion.5.refs_0_), channel_id=1, source_target_pairs={{0,96},{2,98},{4,100},{6,102},{8,104},{10,106},{12,108},{14,110},{... | collective-permute-start | bytes 1572872 | tf_op jit(solution)/shard_map/ppermute | solution.py:44
  180.2 10.9 %collective-permute-start.18 = (bf16[8,16,512]{2,1,0:T(8,128)(2,1)S(1)}, bf16[8,16,512]{2,1,0:T(8,128)(2,1)S(1)}, u32[]{:S(2)}, u32[]{:S(2)}) collective-permute-start(bf16[8,16,512]{2,1,0:T(8,128)(2,1)S(1)} %get-tuple-element.138), channel_id=1, source_target_pairs={{0,32},{2,34},{4,36},{6,38},{8,40},{10,42},{12,44},{14,46},{16,48}... | collective-permute-start | bytes 393224 | tf_op jit(solution)/shard_map/ppermute | solution.py:44
  183.0 9.0 %collective-permute-start.19 = (bf16[8,16,512]{2,1,0:T(8,128)(2,1)S(1)}, bf16[8,16,512]{2,1,0:T(8,128)(2,1)S(1)}, u32[]{:S(2)}, u32[]{:S(2)}) collective-permute-start(bf16[8,16,512]{2,1,0:T(8,128)(2,1)S(1)} %get-tuple-element.139), channel_id=1, source_target_pairs={{0,64},{2,66},{4,68},{6,70},{8,72},{10,74},{12,76},{14,78},{16,80}... | collective-permute-start | bytes 393224 | tf_op jit(solution)/shard_map/ppermute | solution.py:44
  183.5 15.1 %collective-permute-start.20 = (bf16[8,16,512]{2,1,0:T(8,128)(2,1)S(1)}, bf16[8,16,512]{2,1,0:T(8,128)(2,1)S(1)}, u32[]{:S(2)}, u32[]{:S(2)}) collective-permute-start(bf16[8,16,512]{2,1,0:T(8,128)(2,1)S(1)} %get-tuple-element.140), channel_id=1, source_target_pairs={{0,96},{2,98},{4,100},{6,102},{8,104},{10,106},{12,108},{14,110},{... | collective-permute-start | bytes 393224 | tf_op jit(solution)/shard_map/ppermute | solution.py:44
  191.1 28.1 %collective-permute-start.43 = (bf16[4,8,16,512]{3,2,1,0:T(8,128)(2,1)S(1)}, bf16[4,8,16,512]{3,2,1,0:T(8,128)(2,1)S(1)}, u32[]{:S(2)}, u32[]{:S(2)}) collective-permute-start(bf16[4,8,16,512]{3,2,1,0:T(8,128)(2,1)S(1)} %pad_maximum_fusion.4.refs_0_), channel_id=1, source_target_pairs={{0,8},{2,10},{4,12},{6,14},{8,16},{10,18},{12,20},{14,22},{16,24},... | collective-permute-start | bytes 1572872 | tf_op jit(solution)/shard_map/ppermute | solution.py:44
  192.0 27.2 %collective-permute-start.44 = (bf16[4,8,16,512]{3,2,1,0:T(8,128)(2,1)S(1)}, bf16[4,8,16,512]{3,2,1,0:T(8,128)(2,1)S(1)}, u32[]{:S(2)}, u32[]{:S(2)}) collective-permute-start(bf16[4,8,16,512]{3,2,1,0:T(8,128)(2,1)S(1)} %pad_maximum_fusion.4.refs_0_), channel_id=1, source_target_pairs={{0,16},{2,18},{4,20},{6,22},{8,24},{10,26},{12,28},{14,30},{16,0},... | collective-permute-start | bytes 1572872 | tf_op jit(solution)/shard_map/ppermute | solution.py:44
  198.6 25.0 %collective-permute-start.45 = (bf16[4,8,16,512]{3,2,1,0:T(8,128)(2,1)S(1)}, bf16[4,8,16,512]{3,2,1,0:T(8,128)(2,1)S(1)}, u32[]{:S(2)}, u32[]{:S(2)}) collective-permute-start(bf16[4,8,16,512]{3,2,1,0:T(8,128)(2,1)S(1)} %pad_maximum_fusion.4.refs_0_), channel_id=1, source_target_pairs={{0,24},{2,26},{4,28},{6,30},{8,0},{10,2},{12,4},{14,6},{16,8},{18,... | collective-permute-start | bytes 1572872 | tf_op jit(solution)/shard_map/ppermute | solution.py:44
  201.0 48.5 %slice-start = ((s8[6291456]{0:T(1024)(128)(4,1)}), s8[4194304]{0:T(1024)(128)(4,1)S(1)}, s32[]{:S(2)}) async-start(s8[6291456]{0:T(1024)(128)(4,1)} %bitcast.67), calls=%async_computation | async-start | bytes 8388608
  201.3 5.5 %collective-permute-start.30 = (bf16[8,16,512]{2,1,0:T(8,128)(2,1)S(1)}, bf16[8,16,512]{2,1,0:T(8,128)(2,1)S(1)}, u32[]{:S(2)}, u32[]{:S(2)}) collective-permute-start(bf16[8,16,512]{2,1,0:T(8,128)(2,1)S(1)} %get-tuple-element.161), channel_id=1, source_target_pairs={{0,32},{2,34},{4,36},{6,38},{8,40},{10,42},{12,44},{14,46},{16,48}... | collective-permute-start | bytes 393224 | tf_op jit(solution)/shard_map/ppermute | solution.py:44
  203.6 5.5 %collective-permute-start.31 = (bf16[8,16,512]{2,1,0:T(8,128)(2,1)S(1)}, bf16[8,16,512]{2,1,0:T(8,128)(2,1)S(1)}, u32[]{:S(2)}, u32[]{:S(2)}) collective-permute-start(bf16[8,16,512]{2,1,0:T(8,128)(2,1)S(1)} %get-tuple-element.161), channel_id=1, source_target_pairs={{0,64},{2,66},{4,68},{6,70},{8,72},{10,74},{12,76},{14,78},{16,80}... | collective-permute-start | bytes 393224 | tf_op jit(solution)/shard_map/ppermute | solution.py:44
  206.8 4.1 %collective-permute-start.32 = (bf16[8,16,512]{2,1,0:T(8,128)(2,1)S(1)}, bf16[8,16,512]{2,1,0:T(8,128)(2,1)S(1)}, u32[]{:S(2)}, u32[]{:S(2)}) collective-permute-start(bf16[8,16,512]{2,1,0:T(8,128)(2,1)S(1)} %get-tuple-element.161), channel_id=1, source_target_pairs={{0,96},{2,98},{4,100},{6,102},{8,104},{10,106},{12,108},{14,110},{... | collective-permute-start | bytes 393224 | tf_op jit(solution)/shard_map/ppermute | solution.py:44
  211.0 15.8 %collective-permute-start.33 = (bf16[4,8,16,512]{3,2,1,0:T(8,128)(2,1)S(1)}, bf16[4,8,16,512]{3,2,1,0:T(8,128)(2,1)S(1)}, u32[]{:S(2)}, u32[]{:S(2)}) collective-permute-start(bf16[4,8,16,512]{3,2,1,0:T(8,128)(2,1)S(1)} %pad_maximum_fusion.3.refs_0_), channel_id=1, source_target_pairs={{0,2},{2,4},{4,6},{6,0},{8,10},{10,12},{12,14},{14,8},{16,18},{18,... | collective-permute-start | bytes 1572872 | tf_op jit(solution)/shard_map/ppermute | solution.py:44
  214.4 24.5 %collective-permute-start.34 = (bf16[4,8,16,512]{3,2,1,0:T(8,128)(2,1)S(1)}, bf16[4,8,16,512]{3,2,1,0:T(8,128)(2,1)S(1)}, u32[]{:S(2)}, u32[]{:S(2)}) collective-permute-start(bf16[4,8,16,512]{3,2,1,0:T(8,128)(2,1)S(1)} %pad_maximum_fusion.3.refs_0_), channel_id=1, source_target_pairs={{0,4},{2,6},{4,0},{6,2},{8,12},{10,14},{12,8},{14,10},{16,20},{18,... | collective-permute-start | bytes 1572872 | tf_op jit(solution)/shard_map/ppermute | solution.py:44
  219.2 22.1 %collective-permute-start.35 = (bf16[4,8,16,512]{3,2,1,0:T(8,128)(2,1)S(1)}, bf16[4,8,16,512]{3,2,1,0:T(8,128)(2,1)S(1)}, u32[]{:S(2)}, u32[]{:S(2)}) collective-permute-start(bf16[4,8,16,512]{3,2,1,0:T(8,128)(2,1)S(1)} %pad_maximum_fusion.3.refs_0_), channel_id=1, source_target_pairs={{0,6},{2,0},{4,2},{6,4},{8,14},{10,8},{12,10},{14,12},{16,22},{18,... | collective-permute-start | bytes 1572872 | tf_op jit(solution)/shard_map/ppermute | solution.py:44
  219.2 25.0 %collective-permute-start.56 = (bf16[4,4,4,16,512]{4,3,2,1,0:T(8,128)(2,1)S(1)}, bf16[4,4,4,16,512]{4,3,2,1,0:T(8,128)(2,1)S(1)}, u32[]{:S(2)}, u32[]{:S(2)}) collective-permute-start(bf16[4,4,4,16,512]{4,3,2,1,0:T(8,128)(2,1)S(1)} %get-tuple-element.186), channel_id=1, source_target_pairs={{0,1},{1,0},{2,3},{3,2},{4,5},{5,4},{6,7},{7,6},{8,9},{9,8},{10,11... | collective-permute-start | bytes 3145736 | tf_op jit(solution)/shard_map/ppermute | solution.py:244
  224.4 23.0 %collective-permute-start.46 = (bf16[4,4,4,16,512]{4,3,2,1,0:T(8,128)(2,1)S(1)}, bf16[4,4,4,16,512]{4,3,2,1,0:T(8,128)(2,1)S(1)}, u32[]{:S(2)}, u32[]{:S(2)}) collective-permute-start(bf16[4,4,4,16,512]{4,3,2,1,0:T(8,128)(2,1)S(1)} %get-tuple-element.176), channel_id=1, source_target_pairs={{0,1},{1,0},{2,3},{3,2},{4,5},{5,4},{6,7},{7,6},{8,9},{9,8},{10,11... | collective-permute-start | bytes 3145736 | tf_op jit(solution)/shard_map/ppermute | solution.py:244
  242.1 8.4 %collective-permute-start.36 = (bf16[4,4,4,16,512]{4,3,2,1,0:T(8,128)(2,1)S(1)}, bf16[4,4,4,16,512]{4,3,2,1,0:T(8,128)(2,1)S(1)}, u32[]{:S(2)}, u32[]{:S(2)}) collective-permute-start(bf16[4,4,4,16,512]{4,3,2,1,0:T(8,128)(2,1)S(1)} %get-tuple-element.166), channel_id=1, source_target_pairs={{0,1},{1,0},{2,3},{3,2},{4,5},{5,4},{6,7},{7,6},{8,9},{9,8},{10,11... | collective-permute-start | bytes 3145736 | tf_op jit(solution)/shard_map/ppermute | solution.py:244
  244.3 14.7 %collective-permute-start.57 = (bf16[2,4,4,16,512]{4,3,2,1,0:T(8,128)(2,1)S(1)}, bf16[2,4,4,16,512]{4,3,2,1,0:T(8,128)(2,1)S(1)}, u32[]{:S(2)}, u32[]{:S(2)}) collective-permute-start(bf16[2,4,4,16,512]{4,3,2,1,0:T(8,128)(2,1)S(1)} %get-tuple-element.188), channel_id=1, source_target_pairs={{0,2},{2,4},{4,6},{6,0},{8,10},{10,12},{12,14},{14,8},{16,18},{18,... | collective-permute-start | bytes 1572872 | tf_op jit(solution)/shard_map/ppermute | solution.py:44
  244.4 26.3 %collective-permute-start.58 = (bf16[2,4,4,16,512]{4,3,2,1,0:T(8,128)(2,1)S(1)}, bf16[2,4,4,16,512]{4,3,2,1,0:T(8,128)(2,1)S(1)}, u32[]{:S(2)}, u32[]{:S(2)}) collective-permute-start(bf16[2,4,4,16,512]{4,3,2,1,0:T(8,128)(2,1)S(1)} %get-tuple-element.189), channel_id=1, source_target_pairs={{0,4},{2,6},{4,0},{6,2},{8,12},{10,14},{12,8},{14,10},{16,20},{18,... | collective-permute-start | bytes 1572872 | tf_op jit(solution)/shard_map/ppermute | solution.py:44
  247.5 23.2 %collective-permute-start.59 = (bf16[2,4,4,16,512]{4,3,2,1,0:T(8,128)(2,1)S(1)}, bf16[2,4,4,16,512]{4,3,2,1,0:T(8,128)(2,1)S(1)}, u32[]{:S(2)}, u32[]{:S(2)}) collective-permute-start(bf16[2,4,4,16,512]{4,3,2,1,0:T(8,128)(2,1)S(1)} %get-tuple-element.190), channel_id=1, source_target_pairs={{0,6},{2,0},{4,2},{6,4},{8,14},{10,8},{12,10},{14,12},{16,22},{18,... | collective-permute-start | bytes 1572872 | tf_op jit(solution)/shard_map/ppermute | solution.py:44
  247.6 24.4 %collective-permute-start.47 = (bf16[2,4,4,16,512]{4,3,2,1,0:T(8,128)(2,1)S(1)}, bf16[2,4,4,16,512]{4,3,2,1,0:T(8,128)(2,1)S(1)}, u32[]{:S(2)}, u32[]{:S(2)}) collective-permute-start(bf16[2,4,4,16,512]{4,3,2,1,0:T(8,128)(2,1)S(1)} %get-tuple-element.178), channel_id=1, source_target_pairs={{0,32},{2,34},{4,36},{6,38},{8,40},{10,42},{12,44},{14,46},{16,48}... | collective-permute-start | bytes 1572872 | tf_op jit(solution)/shard_map/ppermute | solution.py:44
  250.5 30.6 %collective-permute-start.48 = (bf16[2,4,4,16,512]{4,3,2,1,0:T(8,128)(2,1)S(1)}, bf16[2,4,4,16,512]{4,3,2,1,0:T(8,128)(2,1)S(1)}, u32[]{:S(2)}, u32[]{:S(2)}) collective-permute-start(bf16[2,4,4,16,512]{4,3,2,1,0:T(8,128)(2,1)S(1)} %get-tuple-element.179), channel_id=1, source_target_pairs={{0,64},{2,66},{4,68},{6,70},{8,72},{10,74},{12,76},{14,78},{16,80}... | collective-permute-start | bytes 1572872 | tf_op jit(solution)/shard_map/ppermute | solution.py:44
  259.1 22.1 %collective-permute-start.49 = (bf16[2,4,4,16,512]{4,3,2,1,0:T(8,128)(2,1)S(1)}, bf16[2,4,4,16,512]{4,3,2,1,0:T(8,128)(2,1)S(1)}, u32[]{:S(2)}, u32[]{:S(2)}) collective-permute-start(bf16[2,4,4,16,512]{4,3,2,1,0:T(8,128)(2,1)S(1)} %get-tuple-element.180), channel_id=1, source_target_pairs={{0,96},{2,98},{4,100},{6,102},{8,104},{10,106},{12,108},{14,110},{... | collective-permute-start | bytes 1572872 | tf_op jit(solution)/shard_map/ppermute | solution.py:44
  270.7 15.2 %collective-permute-start.37 = (bf16[2,4,4,16,512]{4,3,2,1,0:T(8,128)(2,1)S(1)}, bf16[2,4,4,16,512]{4,3,2,1,0:T(8,128)(2,1)S(1)}, u32[]{:S(2)}, u32[]{:S(2)}) collective-permute-start(bf16[2,4,4,16,512]{4,3,2,1,0:T(8,128)(2,1)S(1)} %get-tuple-element.168), channel_id=1, source_target_pairs={{0,8},{2,10},{4,12},{6,14},{8,16},{10,18},{12,20},{14,22},{16,24},... | collective-permute-start | bytes 1572872 | tf_op jit(solution)/shard_map/ppermute | solution.py:44
  270.7 23.7 %collective-permute-start.38 = (bf16[2,4,4,16,512]{4,3,2,1,0:T(8,128)(2,1)S(1)}, bf16[2,4,4,16,512]{4,3,2,1,0:T(8,128)(2,1)S(1)}, u32[]{:S(2)}, u32[]{:S(2)}) collective-permute-start(bf16[2,4,4,16,512]{4,3,2,1,0:T(8,128)(2,1)S(1)} %get-tuple-element.169), channel_id=1, source_target_pairs={{0,16},{2,18},{4,20},{6,22},{8,24},{10,26},{12,28},{14,30},{16,0},... | collective-permute-start | bytes 1572872 | tf_op jit(solution)/shard_map/ppermute | solution.py:44
  272.0 24.2 %collective-permute-start.39 = (bf16[2,4,4,16,512]{4,3,2,1,0:T(8,128)(2,1)S(1)}, bf16[2,4,4,16,512]{4,3,2,1,0:T(8,128)(2,1)S(1)}, u32[]{:S(2)}, u32[]{:S(2)}) collective-permute-start(bf16[2,4,4,16,512]{4,3,2,1,0:T(8,128)(2,1)S(1)} %get-tuple-element.170), channel_id=1, source_target_pairs={{0,24},{2,26},{4,28},{6,30},{8,0},{10,2},{12,4},{14,6},{16,8},{18,... | collective-permute-start | bytes 1572872 | tf_op jit(solution)/shard_map/ppermute | solution.py:44
  (4 other events, 104.8 us)
